TPU v7x, 32 devices: a whole 2x2x4 slice. The times are simulated.
32 devices in a mesh: gx: 8 (over y, x, core), gy: 4 (over z).
Axes of the slice: x: 2, y: 2, z: 4, core: 2. Of those that a mesh axis runs over, the one named last changes fastest.
Arguments:
- image: bfloat16 [32, 32, 16, 1024], P(None, 'gx', None, 'gy'), may hold values from -6 to 6
- w_first: bfloat16 [32, 32, 3, 3, 3], replicated, may hold values from -0.21875 to 0.21875
- b_first: float32 [32], replicated, may hold values from -3 to 3
- w_second: bfloat16 [64, 32, 3, 3, 3], replicated, may hold values from -0.21875 to 0.21875
- b_second: float32 [64], replicated, may hold values from -3 to 3
- w_third: bfloat16 [64, 64, 3, 3, 3], replicated, may hold values from -0.15625 to 0.15625
- b_third: float32 [64], replicated, may hold values from -3 to 3
Outputs:
- coarse_out: bfloat16 [64, 16, 8, 512], P(None, 'gx', None, 'gy')
All inputs are finite; a program needn't handle non-finite values.
Results may differ from a plain program's by a relative error of at most 0.0056.
Values may be sent and summed in bfloat16 or wider, within the bound.
No kernel may reach another device: no remote copies, remote signals or barrier semaphores. Data moves between devices by JAX's collectives and lax.ppermute only.
A program may use at most 64 MiB of HBM per device.

v0:
```python
import jax
import jax.numpy as jnp
from jax import lax
from jax.sharding import PartitionSpec as P


def extended(cells, sides, width):
    for axis, dim in sides:
        count = lax.axis_size(axis)
        ends = count - 1
        head = lax.slice_in_dim(cells, 0, width, axis=dim)
        tail = lax.slice_in_dim(cells, cells.shape[dim] - width, cells.shape[dim], axis=dim)
        cells = jnp.concatenate(
            [
                lax.ppermute(tail, axis, [(i, (i + 1) % count) for i in range(ends)]),
                cells,
                lax.ppermute(head, axis, [((i + 1) % count, i) for i in range(ends)]),
            ],
            axis=dim,
        )
    return cells


def convolve(padded, kernel, offset):
    summed = lax.conv_general_dilated(
        padded[None],
        kernel,
        (1, 1, 1),
        "VALID",
        dimension_numbers=("NCDHW", "OIDHW", "NCDHW"),
        preferred_element_type=jnp.float32,
    )[0]
    return jnp.maximum(summed + offset[:, None, None, None], 0.0)


def max_pool(values):
    chans, inline, depth, cross = values.shape
    blocks = values.reshape(chans, inline // 2, 2, depth // 2, 2, cross // 2, 2)
    return jnp.max(blocks, axis=(2, 4, 6))


def per_device(image, w_first, b_first, w_second, b_second, w_third, b_third):
    fine_pad = extended(image, (("gx", 1), ("gy", 3)), 1)
    fine_pad = jnp.pad(fine_pad, ((0, 0), (0, 0), (1, 1), (0, 0)))
    layer_one = convolve(fine_pad, w_first, b_first).astype(jnp.bfloat16)
    pooled = max_pool(layer_one)
    padded = extended(pooled, (("gx", 1), ("gy", 3)), 1)
    padded = jnp.pad(padded, ((0, 0), (0, 0), (1, 1), (0, 0)))
    second = convolve(padded, w_second, b_second).astype(jnp.bfloat16)
    padded = extended(second, (("gx", 1), ("gy", 3)), 1)
    padded = jnp.pad(padded, ((0, 0), (0, 0), (1, 1), (0, 0)))
    return convolve(padded, w_third, b_third).astype(jnp.bfloat16)


def solution(mesh):
    placed = (P(None, "gx", None, "gy"), P(), P(), P(), P(), P(), P())
    return jax.shard_map(
        per_device, mesh=mesh, in_specs=placed, out_specs=P(None, "gx", None, "gy"), check_vma=False
    )
```

profile of v0, /device:TPU:3, one launch (start us, length us, event | category | flops | bytes accessed | tf_op | source)
XLA Modules:
  0.0 175.7 jit_solution(1049440083789488596)
XLA Ops:
  1.2 3.7 %collective-permute-start = (bf16[32,1,16,256]{3,2,1,0:T(8,128)(2,1)S(1)}, bf16[32,1,16,256]{3,2,1,0:T(8,128)(2,1)S(1)}, u32[]{:S(2)}, u32[]{:S(2)}) collective-permute-start(bf16[32,1,16,256]{3,2,1,0:T(8,128)(2,1)S(1)} %get-tuple-element.10), channel_id=1, source_target_pairs={{0,4},{4,8},{8,12},{12,16},{16,20},{20,24},{24,28},{1,5},{5,9},{9,... | collective-permute-start | bytes 786440 | tf_op jit(solution)/shard_map/ppermute | solution.py:15
  8.3 5.2 %collective-permute-done.1 = bf16[32,1,16,256]{3,2,1,0:T(8,128)(2,1)S(1)} collective-permute-done((bf16[32,1,16,256]{3,2,1,0:T(8,128)(2,1)S(1)}, bf16[32,1,16,256]{3,2,1,0:T(8,128)(2,1)S(1)}, u32[]{:S(2)}, u32[]{:S(2)}) %collective-permute-start.1) | collective-permute-done | bytes 262176 | tf_op jit(solution)/shard_map/ppermute | solution.py:17
  16.7 3.2 %collective-permute-start.2 = (bf16[32,6,16,1]{0,2,3,1:T(8,128)(2,1)S(1)}, bf16[32,6,16,1]{0,2,3,1:T(8,128)(2,1)S(1)}, u32[]{:S(2)}, u32[]{:S(2)}) collective-permute-start(bf16[32,6,16,1]{0,2,3,1:T(8,128)(2,1)S(1)} %copy.78), channel_id=1, source_target_pairs={{0,1},{1,2},{2,3},{4,5},{5,6},{6,7},{8,9},{9,10},{10,11},{12,13},{... | collective-permute-start | bytes 18440 | tf_op jit(solution)/shard_map/ppermute | solution.py:15
  27.6 5.1 %fusion.17 = bf16[32,6,18,1,258]{4,2,1,0,3:T(8,128)(2,1)S(1)} fusion(bf16[32,6,16,1]{3,2,1,0:T(8,128)(2,1)} %copy.56, bf16[32,6,16,256]{3,2,1,0:T(8,128)(2,1)S(1)} %constant_dynamic-update-slice_fusion, bf16[32,6,16,1]{3,2,1,0:T(8,128)(2,1)S(1)} %copy.55), kind=kLoop, calls=%fused_computation.23 | loop fusion | flops 10699776 | bytes 3368448 | tf_op jit(solution)/shard_map/broadcast_in_dim | solution.py:26
  32.7 2.3 %pad.15 = bf16[32,6,18,1,264]{4,2,1,0,3:T(8,128)(2,1)} pad(bf16[32,6,18,1,258]{4,2,1,0,3:T(8,128)(2,1)S(1)} %fusion.17, bf16[]{:T(256)} %constant.3.clone.1), padding=0_0x0_0x0_0x0_0x0_6 | pad | bytes 3608066 | tf_op jit(solution)/shard_map/broadcast_in_dim | solution.py:26
  35.0 10.8 %reshape.41 = bf16[32,6,18,1,8,33]{5,4,2,1,0,3:T(8,128)(2,1)} reshape(bf16[32,6,18,1,264]{4,2,1,0,3:T(8,128)(2,1)} %pad.15) | data formatting | bytes 3649536 | tf_op jit(solution)/shard_map/conv_general_dilated | solution.py:25
  45.9 13.1 %copy.59 = bf16[32,6,18,1,8,33]{0,4,5,2,1,3:T(8,128)(2,1)} copy(bf16[32,6,18,1,8,33]{5,4,2,1,0,3:T(8,128)(2,1)} %reshape.41) | data formatting | bytes 3649536 | tf_op jit(solution)/shard_map/conv_general_dilated | solution.py:25
  60.1 19.3 %broadcast_select_fusion = f32[4,16,8,33,32]{4,2,3,1,0:T(8,128)} fusion(pred[8,33]{0,1:T(8,128)(4,1)S(1)} %copy-done.7, bf16[32,32,3,3,3]{1,0,4,3,2:T(8,128)(2,1)S(1)} %copy-done.5, bf16[32,6,18,1,7,2]{0,4,5,2,1,3:T(8,128)(2,1)S(1)} %slice.56, bf16[32,6,18,1,8,33]{0,4,5,2,1,3:T(8,128)(2,1)} %copy.59), kind=kOutput, calls=%fused_computation.14 | convolution fusion | flops 940627968 | bytes 4139784 | tf_op jit(solution)/shard_map/conv_general_dilated | solution.py:25
  79.4 10.7 %copy.60 = f32[4,16,8,33,32]{3,2,4,1,0:T(8,128)} copy(f32[4,16,8,33,32]{4,2,3,1,0:T(8,128)} %broadcast_select_fusion) | data formatting | bytes 4325376 | tf_op jit(solution)/shard_map/conv_general_dilated | solution.py:25
  90.2 7.4 %reshape.11 = f32[4,16,1,264,32]{3,4,1,0,2:T(8,128)} reshape(f32[4,16,8,33,32]{3,2,4,1,0:T(8,128)} %copy.60) | data formatting | bytes 4325376 | tf_op jit(solution)/shard_map/conv_general_dilated | solution.py:25
  99.3 4.7 %copy.61 = f32[1,32,4,16,256]{1,4,3,2,0:T(8,128)} copy(f32[1,32,4,16,256]{4,1,3,2,0:T(8,128)S(1)} %slice_bitcast_fusion) | data formatting | bytes 4194304 | tf_op jit(solution)/shard_map/conv_general_dilated | solution.py:25
  104.0 10.5 %fusion.10 = bf16[32,2,8,128]{0,3,2,1:T(8,128)(2,1)S(1)} fusion(f32[32,2,2,8,2,128,2]{0,6,5,4,3,2,1:T(2,128)} %bitcast.57, f32[32]{0:T(128)S(1)} %copy-done.2), kind=kLoop, calls=%fused_computation.16 | loop fusion | flops 2031616 | bytes 2228352 | tf_op jit(solution)/shard_map/reduce_max | solution.py:39
  114.6 3.2 %collective-permute-start.4 = (bf16[32,1,8,128]{0,3,2,1:T(8,128)(2,1)S(1)}, bf16[32,1,8,128]{0,3,2,1:T(8,128)(2,1)S(1)}, u32[]{:S(2)}, u32[]{:S(2)}) collective-permute-start(bf16[32,1,8,128]{0,3,2,1:T(8,128)(2,1)S(1)} %get-tuple-element.13), channel_id=1, source_target_pairs={{0,4},{4,8},{8,12},{12,16},{16,20},{20,24},{24,28},{1,5},{5,9},{9,... | collective-permute-start | bytes 196616 | tf_op jit(solution)/shard_map/ppermute | solution.py:15
  122.1 4.3 %collective-permute-done.5 = bf16[32,1,8,128]{0,3,2,1:T(8,128)(2,1)S(1)} collective-permute-done((bf16[32,1,8,128]{0,3,2,1:T(8,128)(2,1)S(1)}, bf16[32,1,8,128]{0,3,2,1:T(8,128)(2,1)S(1)}, u32[]{:S(2)}, u32[]{:S(2)}) %collective-permute-start.5) | collective-permute-done | bytes 65568 | tf_op jit(solution)/shard_map/ppermute | solution.py:17
  126.7 3.2 %collective-permute-start.6 = (bf16[32,4,8,1]{3,2,1,0:T(8,128)(2,1)S(1)}, bf16[32,4,8,1]{3,2,1,0:T(8,128)(2,1)S(1)}, u32[]{:S(2)}, u32[]{:S(2)}) collective-permute-start(bf16[32,4,8,1]{3,2,1,0:T(8,128)(2,1)S(1)} %get-tuple-element.15), channel_id=1, source_target_pairs={{0,1},{1,2},{2,3},{4,5},{5,6},{6,7},{8,9},{9,10},{10,11},{12,13},{... | collective-permute-start | bytes 6152 | tf_op jit(solution)/shard_map/ppermute | solution.py:15
  131.2 3.2 %collective-permute-done.6 = bf16[32,4,8,1]{3,2,1,0:T(8,128)(2,1)S(1)} collective-permute-done((bf16[32,4,8,1]{3,2,1,0:T(8,128)(2,1)S(1)}, bf16[32,4,8,1]{3,2,1,0:T(8,128)(2,1)S(1)}, u32[]{:S(2)}, u32[]{:S(2)}) %collective-permute-start.6) | collective-permute-done | bytes 2080 | tf_op jit(solution)/shard_map/ppermute | solution.py:15
  134.4 4.1 %collective-permute-done.7 = bf16[32,4,8,1]{3,2,1,0:T(8,128)(2,1)S(1)} collective-permute-done((bf16[32,4,8,1]{3,2,1,0:T(8,128)(2,1)S(1)}, bf16[32,4,8,1]{3,2,1,0:T(8,128)(2,1)S(1)}, u32[]{:S(2)}, u32[]{:S(2)}) %collective-permute-start.7) | collective-permute-done | bytes 2080 | tf_op jit(solution)/shard_map/ppermute | solution.py:17
  139.6 3.4 %copy.80 = bf16[32,4,10,1,130]{0,1,4,2,3:T(4,128)(2,1)S(1)} copy(bf16[32,4,10,1,130]{4,2,1,0,3:T(8,128)(2,1)S(1)} %fusion.55) | data formatting | bytes 665600
  147.2 3.3 %collective-permute-start.8 = (bf16[64,1,8,128]{0,2,3,1:T(8,128)(2,1)S(1)}, bf16[64,1,8,128]{0,2,3,1:T(8,128)(2,1)S(1)}, u32[]{:S(2)}, u32[]{:S(2)}) collective-permute-start(bf16[64,1,8,128]{0,2,3,1:T(8,128)(2,1)S(1)} %get-tuple-element.11), channel_id=1, source_target_pairs={{0,4},{4,8},{8,12},{12,16},{16,20},{20,24},{24,28},{1,5},{5,9},{9,... | collective-permute-start | bytes 393224 | tf_op jit(solution)/shard_map/ppermute | solution.py:15
  152.4 2.3 %collective-permute-done.8 = bf16[64,1,8,128]{0,2,3,1:T(8,128)(2,1)S(1)} collective-permute-done((bf16[64,1,8,128]{0,2,3,1:T(8,128)(2,1)S(1)}, bf16[64,1,8,128]{0,2,3,1:T(8,128)(2,1)S(1)}, u32[]{:S(2)}, u32[]{:S(2)}) %collective-permute-start.8) | collective-permute-done | bytes 131104 | tf_op jit(solution)/shard_map/ppermute | solution.py:15
  154.7 4.3 %collective-permute-done.9 = bf16[64,1,8,128]{0,2,3,1:T(8,128)(2,1)S(1)} collective-permute-done((bf16[64,1,8,128]{0,2,3,1:T(8,128)(2,1)S(1)}, bf16[64,1,8,128]{0,2,3,1:T(8,128)(2,1)S(1)}, u32[]{:S(2)}, u32[]{:S(2)}) %collective-permute-start.9) | collective-permute-done | bytes 131104 | tf_op jit(solution)/shard_map/ppermute | solution.py:17
  159.0 3.2 %collective-permute-start.10 = (bf16[64,4,8,1]{0,2,3,1:T(8,128)(2,1)S(1)}, bf16[64,4,8,1]{0,2,3,1:T(8,128)(2,1)S(1)}, u32[]{:S(2)}, u32[]{:S(2)}) collective-permute-start(bf16[64,4,8,1]{0,2,3,1:T(8,128)(2,1)S(1)} %get-tuple-element.7), channel_id=1, source_target_pairs={{0,1},{1,2},{2,3},{4,5},{5,6},{6,7},{8,9},{9,10},{10,11},{12,13},{... | collective-permute-start | bytes 12296 | tf_op jit(solution)/shard_map/ppermute | solution.py:15
  163.5 3.1 %collective-permute-done.11 = bf16[64,4,8,1]{0,2,3,1:T(8,128)(2,1)S(1)} collective-permute-done((bf16[64,4,8,1]{0,2,3,1:T(8,128)(2,1)S(1)}, bf16[64,4,8,1]{0,2,3,1:T(8,128)(2,1)S(1)}, u32[]{:S(2)}, u32[]{:S(2)}) %collective-permute-start.11) | collective-permute-done | bytes 4128 | tf_op jit(solution)/shard_map/ppermute | solution.py:17
  169.4 4.3 %fusion.46 = f32[2,8,8,17,64]{4,2,3,1,0:T(8,128)S(1)} fusion(bf16[64,64,3,3,3]{1,0,4,3,2:T(8,128)(2,1)S(1)} %copy-done, bf16[64,4,10,1,7,2]{0,4,5,2,1,3:T(8,128)(2,1)S(1)} %slice.66, bf16[64,4,10,1,8,17]{0,4,5,2,1,3:T(8,128)(2,1)S(1)} %copy.71, pred[8,17]{0,1:T(8,128)(4,1)S(1)} %copy-done.8), kind=kOutput, calls=%fused_computation.53 | convolution fusion | flops 483770368 | bytes 1546376 | tf_op jit(solution)/shard_map/conv_general_dilated | solution.py:25
  (62 shorter events, 37.4 us)
Async XLA Ops:
  0.0 169.4 %copy-start = (bf16[64,64,3,3,3]{1,0,4,3,2:T(8,128)(2,1)S(1)}, bf16[64,64,3,3,3]{1,0,4,3,2:T(8,128)(2,1)}, u32[]{:S(2)}) copy-start(bf16[64,64,3,3,3]{1,0,4,3,2:T(8,128)(2,1)} %param.12) | copy-start | bytes 663556
  0.0 8.2 %copy-start.1 = (bf16[32,4,16,256]{3,2,1,0:T(8,128)(2,1)S(1)}, bf16[32,4,16,256]{3,2,1,0:T(8,128)(2,1)}, u32[]{:S(2)}) copy-start(bf16[32,4,16,256]{3,2,1,0:T(8,128)(2,1)} %param.7) | copy-start | bytes 3145732
  1.2 7.0 %collective-permute-start = (bf16[32,1,16,256]{3,2,1,0:T(8,128)(2,1)S(1)}, bf16[32,1,16,256]{3,2,1,0:T(8,128)(2,1)S(1)}, u32[]{:S(2)}, u32[]{:S(2)}) collective-permute-start(bf16[32,1,16,256]{3,2,1,0:T(8,128)(2,1)S(1)} %get-tuple-element.10), channel_id=1, source_target_pairs={{0,4},{4,8},{8,12},{12,16},{16,20},{20,24},{24,28},{1,5},{5,9},{9,... | collective-permute-start | bytes 786440 | tf_op jit(solution)/shard_map/ppermute | solution.py:15
  4.9 8.6 %collective-permute-start.1 = (bf16[32,1,16,256]{3,2,1,0:T(8,128)(2,1)S(1)}, bf16[32,1,16,256]{3,2,1,0:T(8,128)(2,1)S(1)}, u32[]{:S(2)}, u32[]{:S(2)}) collective-permute-start(bf16[32,1,16,256]{3,2,1,0:T(8,128)(2,1)S(1)} %get-tuple-element.9), channel_id=1, source_target_pairs={{4,0},{8,4},{12,8},{16,12},{20,16},{24,20},{28,24},{5,1},{9,5},{13... | collective-permute-start | bytes 786440 | tf_op jit(solution)/shard_map/ppermute | solution.py:17
  16.7 5.4 %collective-permute-start.2 = (bf16[32,6,16,1]{0,2,3,1:T(8,128)(2,1)S(1)}, bf16[32,6,16,1]{0,2,3,1:T(8,128)(2,1)S(1)}, u32[]{:S(2)}, u32[]{:S(2)}) collective-permute-start(bf16[32,6,16,1]{0,2,3,1:T(8,128)(2,1)S(1)} %copy.78), channel_id=1, source_target_pairs={{0,1},{1,2},{2,3},{4,5},{5,6},{6,7},{8,9},{9,10},{10,11},{12,13},{... | collective-permute-start | bytes 18440 | tf_op jit(solution)/shard_map/ppermute | solution.py:15
  20.9 4.6 %collective-permute-start.3 = (bf16[32,6,16,1]{0,2,3,1:T(8,128)(2,1)S(1)}, bf16[32,6,16,1]{0,2,3,1:T(8,128)(2,1)S(1)}, u32[]{:S(2)}, u32[]{:S(2)}) collective-permute-start(bf16[32,6,16,1]{0,2,3,1:T(8,128)(2,1)S(1)} %copy.79), channel_id=1, source_target_pairs={{1,0},{2,1},{3,2},{5,4},{6,5},{7,6},{9,8},{10,9},{11,10},{13,12},{... | collective-permute-start | bytes 18440 | tf_op jit(solution)/shard_map/ppermute | solution.py:17
  45.9 14.2 %copy-start.5 = (bf16[32,32,3,3,3]{1,0,4,3,2:T(8,128)(2,1)S(1)}, bf16[32,32,3,3,3]{1,0,4,3,2:T(8,128)(2,1)}, u32[]{:S(2)}) copy-start(bf16[32,32,3,3,3]{1,0,4,3,2:T(8,128)(2,1)} %param.8) | copy-start | bytes 165892
  45.9 14.2 %copy-start.7 = (pred[8,33]{0,1:T(8,128)(4,1)S(1)}, pred[8,33]{0,1:T(8,128)(4,1)}, u32[]{:S(2)}) copy-start(pred[8,33]{0,1:T(8,128)(4,1)} %constant.29) | copy-start | bytes 796
  99.3 4.7 %copy-start.2 = (f32[32]{0:T(128)S(1)}, f32[32]{0:T(128)}, u32[]{:S(2)}) copy-start(f32[32]{0:T(128)} %param.9) | copy-start | bytes 388
  114.6 7.4 %collective-permute-start.4 = (bf16[32,1,8,128]{0,3,2,1:T(8,128)(2,1)S(1)}, bf16[32,1,8,128]{0,3,2,1:T(8,128)(2,1)S(1)}, u32[]{:S(2)}, u32[]{:S(2)}) collective-permute-start(bf16[32,1,8,128]{0,3,2,1:T(8,128)(2,1)S(1)} %get-tuple-element.13), channel_id=1, source_target_pairs={{0,4},{4,8},{8,12},{12,16},{16,20},{20,24},{24,28},{1,5},{5,9},{9,... | collective-permute-start | bytes 196616 | tf_op jit(solution)/shard_map/ppermute | solution.py:15
  117.8 8.6 %collective-permute-start.5 = (bf16[32,1,8,128]{0,3,2,1:T(8,128)(2,1)S(1)}, bf16[32,1,8,128]{0,3,2,1:T(8,128)(2,1)S(1)}, u32[]{:S(2)}, u32[]{:S(2)}) collective-permute-start(bf16[32,1,8,128]{0,3,2,1:T(8,128)(2,1)S(1)} %get-tuple-element.14), channel_id=1, source_target_pairs={{4,0},{8,4},{12,8},{16,12},{20,16},{24,20},{28,24},{5,1},{9,5},{13... | collective-permute-start | bytes 196616 | tf_op jit(solution)/shard_map/ppermute | solution.py:17
  126.7 7.7 %collective-permute-start.6 = (bf16[32,4,8,1]{3,2,1,0:T(8,128)(2,1)S(1)}, bf16[32,4,8,1]{3,2,1,0:T(8,128)(2,1)S(1)}, u32[]{:S(2)}, u32[]{:S(2)}) collective-permute-start(bf16[32,4,8,1]{3,2,1,0:T(8,128)(2,1)S(1)} %get-tuple-element.15), channel_id=1, source_target_pairs={{0,1},{1,2},{2,3},{4,5},{5,6},{6,7},{8,9},{9,10},{10,11},{12,13},{... | collective-permute-start | bytes 6152 | tf_op jit(solution)/shard_map/ppermute | solution.py:15
  129.9 8.6 %collective-permute-start.7 = (bf16[32,4,8,1]{3,2,1,0:T(8,128)(2,1)S(1)}, bf16[32,4,8,1]{3,2,1,0:T(8,128)(2,1)S(1)}, u32[]{:S(2)}, u32[]{:S(2)}) collective-permute-start(bf16[32,4,8,1]{3,2,1,0:T(8,128)(2,1)S(1)} %get-tuple-element.16), channel_id=1, source_target_pairs={{1,0},{2,1},{3,2},{5,4},{6,5},{7,6},{9,8},{10,9},{11,10},{13,12},{... | collective-permute-start | bytes 6152 | tf_op jit(solution)/shard_map/ppermute | solution.py:17
  143.7 0.9 copy-start.6
  143.7 0.9 copy-start.8
  146.4 0.7 copy-start.3
  147.2 7.5 %collective-permute-start.8 = (bf16[64,1,8,128]{0,2,3,1:T(8,128)(2,1)S(1)}, bf16[64,1,8,128]{0,2,3,1:T(8,128)(2,1)S(1)}, u32[]{:S(2)}, u32[]{:S(2)}) collective-permute-start(bf16[64,1,8,128]{0,2,3,1:T(8,128)(2,1)S(1)} %get-tuple-element.11), channel_id=1, source_target_pairs={{0,4},{4,8},{8,12},{12,16},{16,20},{20,24},{24,28},{1,5},{5,9},{9,... | collective-permute-start | bytes 393224 | tf_op jit(solution)/shard_map/ppermute | solution.py:15
  150.4 8.6 %collective-permute-start.9 = (bf16[64,1,8,128]{0,2,3,1:T(8,128)(2,1)S(1)}, bf16[64,1,8,128]{0,2,3,1:T(8,128)(2,1)S(1)}, u32[]{:S(2)}, u32[]{:S(2)}) collective-permute-start(bf16[64,1,8,128]{0,2,3,1:T(8,128)(2,1)S(1)} %get-tuple-element.12), channel_id=1, source_target_pairs={{4,0},{8,4},{12,8},{16,12},{20,16},{24,20},{28,24},{5,1},{9,5},{13... | collective-permute-start | bytes 393224 | tf_op jit(solution)/shard_map/ppermute | solution.py:17
  159.0 4.5 %collective-permute-start.10 = (bf16[64,4,8,1]{0,2,3,1:T(8,128)(2,1)S(1)}, bf16[64,4,8,1]{0,2,3,1:T(8,128)(2,1)S(1)}, u32[]{:S(2)}, u32[]{:S(2)}) collective-permute-start(bf16[64,4,8,1]{0,2,3,1:T(8,128)(2,1)S(1)} %get-tuple-element.7), channel_id=1, source_target_pairs={{0,1},{1,2},{2,3},{4,5},{5,6},{6,7},{8,9},{9,10},{10,11},{12,13},{... | collective-permute-start | bytes 12296 | tf_op jit(solution)/shard_map/ppermute | solution.py:15
  162.2 4.4 %collective-permute-start.11 = (bf16[64,4,8,1]{0,2,3,1:T(8,128)(2,1)S(1)}, bf16[64,4,8,1]{0,2,3,1:T(8,128)(2,1)S(1)}, u32[]{:S(2)}, u32[]{:S(2)}) collective-permute-start(bf16[64,4,8,1]{0,2,3,1:T(8,128)(2,1)S(1)} %get-tuple-element.8), channel_id=1, source_target_pairs={{1,0},{2,1},{3,2},{5,4},{6,5},{7,6},{9,8},{10,9},{11,10},{13,12},{... | collective-permute-start | bytes 12296 | tf_op jit(solution)/shard_map/ppermute | solution.py:17
  173.8 0.7 copy-start.4
where the time goes:
time: 177 us; the launch traced here: 176 us
  local copies, waits for them, and re-layouts  70 us (40%)
  waiting for transfers between devices  31.7 us (18%)
  starting transfers between devices  29.3 us (17%)
  matrix products  25.4 us (14%)
  other arithmetic  18.8 us (11%)
    conv_general_dilated x13, local copies, waits for them, and re-layouts, convolve(): lax.conv_general_dilated(padded[None], kernel, (1, 1, 1), 'VALID', dimens...  50.7 us
    conv_general_dilated x3, matrix products, convolve(): lax.conv_general_dilated(padded[None], kernel, (1, 1, 1), 'VALID', dimens...  25.4 us
    ppermute x6, waiting for transfers between devices, extended(): lax.ppermute(head, axis, [((i + 1) % count, i) for i in range(ends)])  22.8 us
    ppermute x6, starting transfers between devices, extended(): lax.ppermute(tail, axis, [(i, (i + 1) % count) for i in range(ends)])  19.7 us
    reduce_max x1, other arithmetic, max_pool(): return jnp.max(blocks, axis=(2, 4, 6))  10.5 us
    ppermute x6, starting transfers between devices, extended(): lax.ppermute(head, axis, [((i + 1) % count, i) for i in range(ends)])  9.63 us
    ppermute x6, waiting for transfers between devices, extended(): lax.ppermute(tail, axis, [(i, (i + 1) % count) for i in range(ends)])  8.9 us
    broadcast_in_dim x3, other arithmetic, convolve(): padded[None]  8.01 us
  transfers between devices with their start and end apart: 12, of which 10 were waited for; matrix products, arithmetic and copies ran while one was open for 2% of the time, Pallas kernels for 0%

commit v1 on v0

v1 whole, which is shorter than its diff:
```python
import functools

import jax
import jax.numpy as jnp
from jax import lax
from jax.experimental import pallas as pl
from jax.experimental.pallas import tpu as pltpu
from jax.sharding import PartitionSpec as P

BF = jnp.bfloat16
F32 = jnp.float32
VM = pl.BlockSpec(memory_space=pltpu.VMEM)
G = 8


def call(body, outs, scratch=(), flops=0, name=None):
    return pl.pallas_call(
        body,
        out_shape=[jax.ShapeDtypeStruct(s, d) for s, d in outs],
        out_specs=[VM] * len(outs),
        scratch_shapes=list(scratch),
        compiler_params=pltpu.CompilerParams(vmem_limit_bytes=48 << 20),
        cost_estimate=pl.CostEstimate(flops=flops, bytes_accessed=1 << 20, transcendentals=0),
        name=name,
    )


def dot(a, b):
    return jnp.dot(a, b, preferred_element_type=F32)


def lanes(shape):
    return lax.broadcasted_iota(jnp.int32, shape, len(shape) - 1)


def roll(v, by):
    size = v.shape[-1]
    return pltpu.roll(v, by % size, v.ndim - 1)


def weights_kernel(w1, w2, w3, a1, a1s, a2, a3):
    def band(pieces, first):
        zero = jnp.zeros_like(pieces[0])
        return jnp.concatenate([zero] + pieces if first else pieces + [zero], axis=1)

    c1, c2 = w1.shape[3], w3.shape[3]
    for e in range(3):
        for f in range(3):
            p1 = [w1[a, e, f].astype(F32) for a in range(3)]
            p2 = [w2[a, e, f].astype(F32).T for a in range(3)]
            p3 = [w3[a, e, f].astype(F32) for a in range(3)]
            for xo in range(2):
                b1 = band(p1, xo).astype(BF)
                k1 = b1.shape[1]
                a1[pl.ds((xo * 3 + f) * c1, c1), pl.ds(e * k1, k1)] = b1
                a1s[pl.ds(((xo * 3 + e) * 3 + f) * c1, c1), :] = b1
                a2[pl.ds((xo * 3 + f) * c2, c2), pl.ds(e * k1, k1)] = band(p2, xo).astype(BF)
                a3[pl.ds((xo * 3 + f) * c2, c2), pl.ds(e * 2 * k1, 2 * k1)] = band(p3, xo).astype(BF)


def pack_kernel(image, own, row_a, row_b, send_a, send_b, strip_l, strip_r, lo, hi):
    chans, inline, depth, cross = image.shape
    odd = lax.axis_index("gx") % 2
    odd_y = lax.axis_index("gy") % 2
    lane = lanes((chans, 128))
    for x in range(inline):
        cells = image[:, x].astype(F32).reshape(chans * depth, cross)
        lo[...] = cells[:, :128]
        hi[...] = cells[:, cross - 128 :]
        left = jnp.zeros((chans, 128), F32)
        right = jnp.zeros((chans, 128), F32)
        for z in range(depth):
            a = lo[pl.ds(z, chans, stride=depth), :]
            b = hi[pl.ds(z, chans, stride=depth), :]
            own[z, x, :, :128] = a.astype(BF)
            own[z, x, :, 128:] = b.astype(BF)
            here = (lane >= z * G) & (lane < z * G + G)
            left = jnp.where(here, roll(a, z * G), left)
            right = jnp.where(here, roll(b, z * G + G), right)
        part = lane % G
        msg_l = jnp.where(part >= 3, roll(left, 3), 0.0).astype(BF)
        own_l = jnp.where(part >= 5, roll(left, 5), 0.0).astype(BF)
        msg_r = jnp.where(part < 5, roll(right, -3), 0.0).astype(BF)
        own_r = jnp.where(part < 3, roll(right, -5), 0.0).astype(BF)
        strip_l[x] = own_l
        strip_r[x] = own_r
        send_a[x] = jnp.where(odd_y == 0, msg_r, msg_l)
        send_b[x] = jnp.where(odd_y == 0, msg_l, msg_r)
    row_a[...] = own[:, (inline - 1) * (1 - odd)]
    row_b[...] = own[:, (inline - 1) * odd]


def strip_kernel(strip_l, strip_r, got_a, got_b, strips, corner_a, corner_b):
    inline = strip_l.shape[0]
    odd = lax.axis_index("gx") % 2
    odd_y = lax.axis_index("gy") % 2
    part = lanes(strip_l.shape) % G
    ga, gb = got_a[...], got_b[...]
    from_l = jnp.where(odd_y == 0, gb, ga)
    from_r = jnp.where(odd_y == 0, ga, gb)
    strips[:, :, :128] = jnp.where(part < 5, from_l, strip_l[...])
    strips[:, :, 128:] = jnp.where(part < 3, strip_r[...], from_r)
    corner_a[...] = strips[(inline - 1) * (1 - odd)]
    corner_b[...] = strips[(inline - 1) * odd]


def fine_pair(own, halo, halo_first, a1, bias, pooled, pad, acc):
    depth, inline, chans, cross = own.shape
    width = inline * chans
    zero = jnp.zeros((width, cross), BF)
    pad[pl.ds(0, width), :] = zero
    pad[pl.ds((depth + 1) * width, width), :] = zero
    first = 1 - halo_first

    def fill(z, carry):
        base = (z + 1) * width
        pad[pl.ds(pl.multiple_of(base + (1 - halo_first) * (inline - 1) * chans, chans), chans), :] = halo[z]
        for r in range(inline - 1):
            pad[pl.ds(pl.multiple_of(base + (r + halo_first) * chans, chans), chans), :] = own[z, first + r]
        return carry

    lax.fori_loop(0, depth, fill, 0)

    def layer(z):
        g = dot(a1[...], pad[pl.ds(pl.multiple_of(z * width, width), 3 * width), :])
        rows = []
        for xo in range(2):
            t = g[xo * 3 * chans : (xo + 1) * 3 * chans]
            rows.append(roll(t[:chans], 1) + t[chans : 2 * chans] + roll(t[2 * chans :], -1))
        return jnp.maximum(rows[0], rows[1])

    def step(z, carry):
        m = jnp.maximum(layer(2 * z), layer(2 * z + 1))
        m = jnp.maximum(jnp.maximum(m, roll(m, -1)) + bias[...], 0.0)
        acc[pl.ds(pl.multiple_of(z * chans, chans), chans), :] = m.astype(BF)
        return carry

    lax.fori_loop(0, depth // 2, step, 0)
    half = cross // 2
    src = lax.broadcasted_iota(jnp.int32, (cross, half), 0)
    dst = lax.broadcasted_iota(jnp.int32, (cross, half), 1)
    pick = jnp.where(src == 2 * dst, 1.0, 0.0).astype(BF)
    pooled[...] = dot(acc[...], pick).astype(BF).reshape(depth // 2, chans, half)


def early_kernel(own, halo, a1, bias, pooled, pad, acc):
    fine_pair(own, halo, lax.axis_index("gx") % 2, a1, bias, pooled, pad, acc)


def late_kernel(own, halo, a1, bias, pooled, pad, acc):
    fine_pair(own, halo, 1 - lax.axis_index("gx") % 2, a1, bias, pooled, pad, acc)


def edge_kernel(strips, corner_a, corner_b, early, late, a1s, bias, message, rows):
    inline, chans, _ = strips.shape
    half_depth = early.shape[0]
    odd = lax.axis_index("gx") % 2
    at = lax.axis_index("gy")
    end = lax.axis_size("gy") - 1
    ca, cb = corner_a[...], corner_b[...]
    rows[pl.ds(0, chans), :] = jnp.where(odd == 1, ca, cb)
    rows[pl.ds(chans, inline * chans), :] = strips[...].reshape(inline * chans, 256)
    rows[pl.ds((inline + 1) * chans, chans), :] = jnp.where(odd == 1, cb, ca)
    lane = lanes((chans, 128))
    for pair in range(2):
        g = dot(a1s[...], rows[pl.ds(pair * 2 * chans, 4 * chans), :])
        sides = []
        for side in range(2):
            best = None
            for xo in range(2):
                total = jnp.zeros((chans, 128), F32)
                for e in range(3):
                    part = None
                    for f in range(3):
                        k = (xo * 3 + e) * 3 + f
                        t = g[k * chans : (k + 1) * chans, side * 128 : side * 128 + 128]
                        t = roll(t, -(G * (e - 1) + f - 1))
                        part = t if part is None else part + t
                    if e == 0:
                        part = jnp.where(lane >= G, part, 0.0)
                    if e == 2:
                        part = jnp.where(lane < 128 - G, part, 0.0)
                    total = total + part
                best = total if best is None else jnp.maximum(best, total)
            best = jnp.maximum(best, roll(best, -G))
            best = jnp.maximum(best, roll(best, -1))
            best = jnp.maximum(best + bias[...], 0.0)
            cell = lane % G
            outside = (cell < 5) & (at == 0) if side == 0 else (cell > 1) & (at == end)
            sides.append(jnp.where(outside, 0.0, best))
        edges = jnp.where((lane // G) % 2 == 0, sides[0], roll(sides[1], G))
        message[pair, half_depth] = edges.astype(BF)
    message[odd, pl.ds(0, half_depth)] = late[...]
    message[1 - odd, pl.ds(0, half_depth)] = early[...]


def coarse_kernel(own, got_a, got_b, a2, b2, a3, b3, out, edge, pad2, pad3, wide):
    coarse, tall, chans, half = own.shape
    depth = tall - 1
    c2 = b2.shape[0]
    odd = lax.axis_index("gx") % 2
    at_x, end_x = lax.axis_index("gx"), lax.axis_size("gx") - 1
    at_y, end_y = lax.axis_index("gy"), lax.axis_size("gy") - 1
    width = 4 * chans
    parts = [(0, got_a, got_b), (2, None, None), (4, got_b, got_a)]

    def row_of(i, z):
        if 2 <= i < 4:
            return own[i - 2, z]
        r = i % 2
        if i < 2:
            return jnp.where(odd == 1, got_a[r, z], got_b[r, z])
        return jnp.where(odd == 1, got_b[r, z], got_a[r, z])

    src = lax.broadcasted_iota(jnp.int32, (half, 256), 0)
    dst = lax.broadcasted_iota(jnp.int32, (half, 256), 1)
    for i in range(6):
        edge[pl.ds(i * chans, chans), :] = row_of(i, depth)
    zero = jnp.zeros((width, 256), BF)
    for pair in range(2):
        pad2[pair, pl.ds(0, width), :] = zero
        pad2[pair, pl.ds((depth + 1) * width, width), :] = zero
    lane = lanes((chans, half))
    inner = (lane > 0) & (lane < half - 1)
    for z in range(depth):
        l, r = 2 * z * G, (2 * z + 1) * G
        pick = (
            ((dst == 0) & (src == l + 5))
            | ((dst == half - 1) & (src == r + 1))
            | ((dst == half) & (src == r + 3))
            | ((dst == half + 1) & (src == r + 5))
            | ((dst == 254) & (src == l + 1))
            | ((dst == 255) & (src == l + 3))
        )
        ends = dot(edge[...], jnp.where(pick, 1.0, 0.0).astype(BF)).astype(BF)
        for i in range(6):
            e = ends[i * chans : (i + 1) * chans]
            main = jnp.where(inner, row_of(i, z), e[:, :half])
            for pair in range(2):
                j = i - 2 * pair
                if 0 <= j < 4:
                    base = (z + 1) * width + j * chans
                    pad2[pair, pl.ds(base, chans), :half] = main
                    pad2[pair, pl.ds(base, chans), half:] = e[:, half:]

    wide3 = 4 * c2
    zero = jnp.zeros((wide3, 256), BF)
    pad3[pl.ds(0, wide3), :] = zero
    pad3[pl.ds((depth + 1) * wide3, wide3), :] = zero
    col = lanes((c2, 256))
    outside_y = ((col == 255) & (at_y == 0)) | ((col == half) & (at_y == end_y))

    def shifted(g):
        return roll(g[:c2], 1) + g[c2 : 2 * c2] + roll(g[2 * c2 :], -1)

    def second(z, carry):
        for pair in range(2):
            g = dot(a2[...], pad2[pair, pl.ds(pl.multiple_of(z * width, width), 3 * width), :])
            for xo in range(2):
                v = jnp.maximum(shifted(g[xo * 3 * c2 : (xo + 1) * 3 * c2]) + b2[...], 0.0)
                r = 2 * pair + xo
                outside = outside_y
                if r == 0:
                    outside = outside | (at_x == 0)
                if r == 3:
                    outside = outside | (at_x == end_x)
                v = jnp.where(outside, 0.0, v).astype(BF)
                pad3[pl.ds(pl.multiple_of((z + 1) * wide3 + r * c2, c2), c2), :] = v
        return carry

    lax.fori_loop(0, depth, second, 0)

    def third(z, carry):
        g = dot(a3[...], pad3[pl.ds(pl.multiple_of(z * wide3, wide3), 3 * wide3), :])
        for xo in range(2):
            v = jnp.maximum(shifted(g[xo * 3 * c2 : (xo + 1) * 3 * c2]) + b3[...], 0.0)
            wide[xo, pl.ds(z, c2, stride=depth), :] = v[:, :half]
        return carry

    lax.fori_loop(0, depth, third, 0)
    for xo in range(2):
        out[:, xo] = wide[xo].reshape(c2, depth, half).astype(BF)


def swap(value, axis, parity):
    pairs = []
    for i in range(parity, lax.axis_size(axis) - 1, 2):
        pairs += [(i, i + 1), (i + 1, i)]
    return lax.ppermute(value, axis, pairs)


def per_device(image, w_first, b_first, w_second, b_second, w_third, b_third):
    c1, inline, depth, cross = image.shape
    c2 = w_third.shape[0]
    half, hz = cross // 2, depth // 2
    w1 = jnp.transpose(w_first, (2, 3, 4, 0, 1))
    w2 = jnp.transpose(w_second, (2, 3, 4, 1, 0))
    w3 = jnp.transpose(w_third, (2, 3, 4, 0, 1))
    k1 = 4 * c1
    own, row_a, row_b, send_a, send_b, strip_l, strip_r = call(
        pack_kernel,
        [
            ((depth, inline, c1, cross), BF),
            ((depth, c1, cross), BF),
            ((depth, c1, cross), BF),
        ]
        + [((inline, c1, 128), BF)] * 4,
        [pltpu.VMEM((c1 * depth, 128), F32)] * 2,
        flops=1 << 20,
        name="pack",
    )(image)
    got_ya = swap(send_a, "gy", 0)
    got_yb = swap(send_b, "gy", 1)
    got_a = swap(row_a, "gx", 0)
    got_b = swap(row_b, "gx", 1)
    a1, a1s, a2, a3 = call(
        weights_kernel,
        [
            ((6 * c1, 3 * k1), BF),
            ((18 * c1, k1), BF),
            ((6 * c2, 3 * k1), BF),
            ((6 * c2, 12 * c2), BF),
        ],
        flops=1 << 28,
        name="weights",
    )(w1, w2, w3)
    b1 = b_first.reshape(c1, 1)
    b2 = b_second.reshape(c2, 1)
    b3 = b_third.reshape(c2, 1)
    strips, corner_a, corner_b = call(
        strip_kernel,
        [((inline, c1, 256), BF), ((c1, 256), BF), ((c1, 256), BF)],
        flops=1 << 20,
        name="strip",
    )(strip_l, strip_r, got_ya, got_yb)
    got_ca = swap(corner_a, "gx", 0)
    got_cb = swap(corner_b, "gx", 1)
    fine = [pltpu.VMEM(((depth + 2) * k1, cross), BF), pltpu.VMEM((hz * c1, cross), BF)]
    (early,) = call(early_kernel, [((hz, c1, half), BF)], fine, flops=1 << 30, name="early")(own, got_a, a1, b1)
    (late,) = call(late_kernel, [((hz, c1, half), BF)], fine, flops=1 << 30, name="late")(own, got_b, a1, b1)
    (message,) = call(
        edge_kernel,
        [((inline // 2, hz + 1, c1, half), BF)],
        [pltpu.VMEM(((inline + 2) * c1, 256), BF)],
        flops=1 << 28,
        name="edge",
    )(strips, got_ca, got_cb, early, late, a1s, b1)
    got_pa = swap(message, "gx", 0)
    got_pb = swap(message, "gx", 1)
    (out,) = call(
        coarse_kernel,
        [((c2, inline // 2, hz, half), BF)],
        [
            pltpu.VMEM((6 * c1, half), BF),
            pltpu.VMEM((2, (hz + 2) * k1, 256), BF),
            pltpu.VMEM(((hz + 2) * 4 * c2, 256), BF),
            pltpu.VMEM((2, c2 * hz, half), F32),
        ],
        flops=1 << 31,
        name="coarse",
    )(message, got_pa, got_pb, a2, b2, a3, b3)
    return out


def solution(mesh):
    placed = (P(None, "gx", None, "gy"), P(), P(), P(), P(), P(), P())
    return jax.shard_map(
        per_device, mesh=mesh, in_specs=placed, out_specs=P(None, "gx", None, "gy"), check_vma=False
    )
```

time: 177 us -> 42.2 us (0.24)
  the two profiles are of different devices: /device:TPU:3 before, /device:TPU:20 now
where the time goes in v1:
time: 42.2 us; the launch traced here: 42 us
  Pallas kernels  18.3 us (43%)
  starting transfers between devices  13.8 us (33%)
  waiting for transfers between devices  6.64 us (16%)
  local copies, waits for them, and re-layouts  3 us (7%)
    ppermute x8, starting transfers between devices, swap(): return lax.ppermute(value, axis, pairs)  13.8 us
    pallas_call x1, Pallas kernels, per_device(): call(coarse_kernel, [((c2, inline // 2, hz, half), BF)], [pltpu.VMEM((6 *...  8.14 us
    ppermute x8, waiting for transfers between devices, swap(): return lax.ppermute(value, axis, pairs)  6.64 us
    pallas_call x1, Pallas kernels, per_device(): call(early_kernel, [((hz, c1, half), BF)], fine, flops=1 << 30, name='ear...  3.85 us
    pallas_call x1, Pallas kernels, per_device(): call(late_kernel, [((hz, c1, half), BF)], fine, flops=1 << 30, name='late')  3.85 us
    unnamed x18, local copies, waits for them, and re-layouts  2.72 us
    pallas_call x1, Pallas kernels, per_device(): call(pack_kernel, [((depth, inline, c1, cross), BF), ((depth, c1, cross),...  1.13 us
  transfers between devices with their start and end apart: 8, of which 2 were waited for; matrix products, arithmetic and copies ran while one was open for 1% of the time, Pallas kernels for 20%

profile of v1, /device:TPU:20, one launch (start us, length us, event | category | flops | bytes accessed | tf_op | source)
XLA Modules:
  0.0 42.0 jit_solution(3587355551248415428)
XLA Ops:
  0.0 1.2 %copy-done = bf16[32,4,16,256]{3,2,1,0:T(8,128)(2,1)S(1)} copy-done((bf16[32,4,16,256]{3,2,1,0:T(8,128)(2,1)S(1)}, bf16[32,4,16,256]{3,2,1,0:T(8,128)(2,1)}, u32[]{:S(2)}) %copy-start) | copy-done | bytes 1048600
  1.2 1.1 %pack.1 = (bf16[16,4,32,256]{3,2,1,0:T(8,128)(2,1)S(1)}, bf16[16,32,256]{2,1,0:T(8,128)(2,1)S(1)}, bf16[16,32,256]{2,1,0:T(8,128)(2,1)S(1)}, bf16[4,32,128]{2,1,...) custom-call(bf16[32,4,16,256]{3,2,1,0:T(8,128)(2,1)S(1)} %copy-done), custom_call_target="tpu_custom_call" | custom-call | flops 1048576 | bytes 1048576 | tf_op jit(solution)/shard_map/pack/pallas_call | solution.py:300
  2.4 2.8 %collective-permute-start.5 = (bf16[16,32,256]{2,1,0:T(8,128)(2,1)S(1)}, bf16[16,32,256]{2,1,0:T(8,128)(2,1)S(1)}, u32[]{:S(2)}, u32[]{:S(2)}) collective-permute-start(bf16[16,32,256]{2,1,0:T(8,128)(2,1)S(1)} %get-tuple-element.29), channel_id=1, source_target_pairs={{4,8},{8,4},{12,16},{16,12},{20,24},{24,20},{5,9},{9,5},{13,17},{1... | collective-permute-start | bytes 786440 | tf_op jit(solution)/shard_map/ppermute | solution.py:289
  5.2 0.8 %collective-permute-start.4 = (bf16[16,32,256]{2,1,0:T(8,128)(2,1)S(1)}, bf16[16,32,256]{2,1,0:T(8,128)(2,1)S(1)}, u32[]{:S(2)}, u32[]{:S(2)}) collective-permute-start(bf16[16,32,256]{2,1,0:T(8,128)(2,1)S(1)} %get-tuple-element.27), channel_id=1, source_target_pairs={{0,4},{4,0},{8,12},{12,8},{16,20},{20,16},{24,28},{28,24},{1,5},{5... | collective-permute-start | bytes 786440 | tf_op jit(solution)/shard_map/ppermute | solution.py:289
  6.0 1.6 %collective-permute-start = (bf16[4,32,128]{2,1,0:T(8,128)(2,1)S(1)}, bf16[4,32,128]{2,1,0:T(8,128)(2,1)S(1)}, u32[]{:S(2)}, u32[]{:S(2)}) collective-permute-start(bf16[4,32,128]{2,1,0:T(8,128)(2,1)S(1)} %get-tuple-element.21), channel_id=1, source_target_pairs={{0,1},{1,0},{2,3},{3,2},{4,5},{5,4},{6,7},{7,6},{8,9},{9,8},{10,11... | collective-permute-start | bytes 98312 | tf_op jit(solution)/shard_map/ppermute | solution.py:289
  7.5 2.0 %collective-permute-start.1 = (bf16[4,32,128]{2,1,0:T(8,128)(2,1)S(1)}, bf16[4,32,128]{2,1,0:T(8,128)(2,1)S(1)}, u32[]{:S(2)}, u32[]{:S(2)}) collective-permute-start(bf16[4,32,128]{2,1,0:T(8,128)(2,1)S(1)} %get-tuple-element.22), channel_id=1, source_target_pairs={{1,2},{2,1},{5,6},{6,5},{9,10},{10,9},{13,14},{14,13},{17,18},{18,... | collective-permute-start | bytes 98312 | tf_op jit(solution)/shard_map/ppermute | solution.py:289
  9.6 0.1 copy.8.bias
  9.7 0.7 %weights.1 = (bf16[192,384]{1,0:T(8,128)(2,1)S(1)}, bf16[576,128]{1,0:T(8,128)(2,1)S(1)}, bf16[384,384]{1,0:T(8,128)(2,1)S(1)}, bf16[384,768]{1,0:T(8,128)(2,1)S(1)}) custom-call(bf16[3,3,3,32,32]{4,3,2,1,0:T(8,128)(2,1)S(1)} %bitcast.7, bf16[3,3,3,32,64]{4,3,2,1,0:T(8,128)(2,1)S(1)} %bitcast.8, bf16[3,3,3,64,64]{4,3,2,1,0:T(8,128)(2,1)S(1)} %bitcast.6), custom_call_target="tpu_custom_call" | custom-call | flops 268435456 | bytes 1048576 | tf_op jit(solution)/shard_map/weights/pallas_call | solution.py:316
  10.4 0.8 %copy-done.4 = bf16[384,768]{1,0:T(8,128)(2,1)} copy-done((bf16[384,768]{1,0:T(8,128)(2,1)}, bf16[384,768]{1,0:T(8,128)(2,1)S(1)}, u32[]{:S(2)}) %copy-start.4) | copy-done | bytes 589848
  11.2 2.3 %collective-permute-done.1.got_b = bf16[4,32,128]{2,1,0:T(8,128)(2,1)S(1)} collective-permute-done((bf16[4,32,128]{2,1,0:T(8,128)(2,1)S(1)}, bf16[4,32,128]{2,1,0:T(8,128)(2,1)S(1)}, u32[]{:S(2)}, u32[]{:S(2)}) %collective-permute-start.1) | collective-permute-done | bytes 32800 | tf_op jit(solution)/shard_map/ppermute | solution.py:289
  13.5 0.1 collective-permute-start.2
  13.6 3.4 %collective-permute-start.3 = (bf16[32,256]{1,0:T(8,128)(2,1)S(1)}, bf16[32,256]{1,0:T(8,128)(2,1)S(1)}, u32[]{:S(2)}, u32[]{:S(2)}) collective-permute-start(bf16[32,256]{1,0:T(8,128)(2,1)S(1)} %get-tuple-element.25), channel_id=1, source_target_pairs={{4,8},{8,4},{12,16},{16,12},{20,24},{24,20},{5,9},{9,5},{13,17},{1... | collective-permute-start | bytes 49160 | tf_op jit(solution)/shard_map/ppermute | solution.py:289
  17.0 0.0 collective-permute-done.5.halo
  17.0 3.9 %late.1 = bf16[8,32,128]{2,1,0:T(8,128)(2,1)S(1)} custom-call(bf16[16,4,32,256]{3,2,1,0:T(8,128)(2,1)S(1)} %get-tuple-element.26.own, bf16[16,32,256]{2,1,0:T(8,128)(2,1)S(1)} %collective-permute-done.5.halo, bf16[192,384]{1,0:T(8,128)(2,1)S(1)} %get-tuple-element.28.a1, f32[32,1]{1,0:T(8,128)S(1)} %copy.8.bias), custom_call_target="tpu_custom_call" | custom-call | flops 1073741824 | bytes 1048576 | tf_op jit(solution)/shard_map/late/pallas_call | solution.py:340
  20.9 3.9 %early.1 = bf16[8,32,128]{2,1,0:T(8,128)(2,1)S(1)} custom-call(bf16[16,4,32,256]{3,2,1,0:T(8,128)(2,1)S(1)} %get-tuple-element.26.own, bf16[16,32,256]{2,1,0:T(8,128)(2,1)S(1)} %collective-permute-done.4.halo, bf16[192,384]{1,0:T(8,128)(2,1)S(1)} %get-tuple-element.28.a1, f32[32,1]{1,0:T(8,128)S(1)} %copy.8.bias), custom_call_target="tpu_custom_call" | custom-call | flops 1073741824 | bytes 1048576 | tf_op jit(solution)/shard_map/early/pallas_call | solution.py:339
  24.8 0.7 %edge.1.own = bf16[2,9,32,128]{3,2,1,0:T(8,128)(2,1)S(1)} custom-call(bf16[4,32,256]{2,1,0:T(8,128)(2,1)S(1)} %get-tuple-element.23.strips, bf16[32,256]{1,0:T(8,128)(2,1)S(1)} %collective-permute-done.2.corner_a, bf16[32,256]{1,0:T(8,128)(2,1)S(1)} %collective-permute-done.3.corner_b, bf16[8,32,128]{2,1,0:T(8,128)(2,1)S(1)} %early.1, ...), custom_call_target="tpu_custom_call" | custom-call | flops 268435456 | bytes 1048576 | tf_op jit(solution)/shard_map/edge/pallas_call | solution.py:341
  25.5 0.0 copy-start.6
  25.5 0.1 collective-permute-start.6
  25.6 3.0 %collective-permute-start.7 = (bf16[2,9,32,128]{3,2,1,0:T(8,128)(2,1)S(1)}, bf16[2,9,32,128]{3,2,1,0:T(8,128)(2,1)S(1)}, u32[]{:S(2)}, u32[]{:S(2)}) collective-permute-start(bf16[2,9,32,128]{3,2,1,0:T(8,128)(2,1)S(1)} %edge.1.own), channel_id=1, source_target_pairs={{4,8},{8,4},{12,16},{16,12},{20,24},{24,20},{5,9},{9,5},{13,17},{1... | collective-permute-start | bytes 442376 | tf_op jit(solution)/shard_map/ppermute | solution.py:289
  28.6 0.1 copy.11.b2
  28.7 0.7 %copy-done.7 = f32[64]{0:T(128)S(1)} copy-done((f32[64]{0:T(128)S(1)}, f32[64]{0:T(128)}, u32[]{:S(2)}) %copy-start.7) | copy-done | bytes 280
  29.4 0.1 copy.12.b3
  29.5 4.3 %collective-permute-done.7.got_b = bf16[2,9,32,128]{3,2,1,0:T(8,128)(2,1)S(1)} collective-permute-done((bf16[2,9,32,128]{3,2,1,0:T(8,128)(2,1)S(1)}, bf16[2,9,32,128]{3,2,1,0:T(8,128)(2,1)S(1)}, u32[]{:S(2)}, u32[]{:S(2)}) %collective-permute-start.7) | collective-permute-done | bytes 147488 | tf_op jit(solution)/shard_map/ppermute | solution.py:289
  33.8 8.1 %coarse.1 = bf16[64,2,8,128]{3,2,1,0:T(8,128)(2,1)} custom-call(bf16[2,9,32,128]{3,2,1,0:T(8,128)(2,1)S(1)} %edge.1.own, bf16[2,9,32,128]{3,2,1,0:T(8,128)(2,1)S(1)} %collective-permute-done.6.got_a, bf16[2,9,32,128]{3,2,1,0:T(8,128)(2,1)S(1)} %collective-permute-done.7.got_b, bf16[384,384]{1,0:T(8,128)(2,1)S(1)} %get-tuple-element.31.a2, ...), custom_call_target="tpu_custom_call" | custom-call | flops 2147483648 | bytes 1048576 | tf_op jit(solution)/shard_map/coarse/pallas_call | solution.py:350
  (20 shorter events, 0.1 us)
Async XLA Ops:
  0.0 1.2 %copy-start = (bf16[32,4,16,256]{3,2,1,0:T(8,128)(2,1)S(1)}, bf16[32,4,16,256]{3,2,1,0:T(8,128)(2,1)}, u32[]{:S(2)}) copy-start(bf16[32,4,16,256]{3,2,1,0:T(8,128)(2,1)} %image.1) | copy-start | bytes 3145732
  1.2 8.5 %copy-start.1 = (bf16[64,64,3,3,3]{1,0,4,3,2:T(8,128)(2,1)S(1)}, bf16[64,64,3,3,3]{1,0,4,3,2:T(8,128)(2,1)}, u32[]{:S(2)}) copy-start(bf16[64,64,3,3,3]{1,0,4,3,2:T(8,128)(2,1)} %param.12) | copy-start | bytes 663556
  1.2 8.5 %copy-start.2 = (bf16[32,32,3,3,3]{1,0,4,3,2:T(8,128)(2,1)S(1)}, bf16[32,32,3,3,3]{1,0,4,3,2:T(8,128)(2,1)}, u32[]{:S(2)}) copy-start(bf16[32,32,3,3,3]{1,0,4,3,2:T(8,128)(2,1)} %param.8) | copy-start | bytes 165892
  1.2 8.5 %copy-start.3 = (bf16[64,32,3,3,3]{0,1,4,3,2:T(8,128)(2,1)S(1)}, bf16[64,32,3,3,3]{0,1,4,3,2:T(8,128)(2,1)}, u32[]{:S(2)}) copy-start(bf16[64,32,3,3,3]{0,1,4,3,2:T(8,128)(2,1)} %param.10) | copy-start | bytes 331780
  2.4 14.7 %collective-permute-start.5 = (bf16[16,32,256]{2,1,0:T(8,128)(2,1)S(1)}, bf16[16,32,256]{2,1,0:T(8,128)(2,1)S(1)}, u32[]{:S(2)}, u32[]{:S(2)}) collective-permute-start(bf16[16,32,256]{2,1,0:T(8,128)(2,1)S(1)} %get-tuple-element.29), channel_id=1, source_target_pairs={{4,8},{8,4},{12,16},{16,12},{20,24},{24,20},{5,9},{9,5},{13,17},{1... | collective-permute-start | bytes 786440 | tf_op jit(solution)/shard_map/ppermute | solution.py:289
  5.2 15.7 %collective-permute-start.4 = (bf16[16,32,256]{2,1,0:T(8,128)(2,1)S(1)}, bf16[16,32,256]{2,1,0:T(8,128)(2,1)S(1)}, u32[]{:S(2)}, u32[]{:S(2)}) collective-permute-start(bf16[16,32,256]{2,1,0:T(8,128)(2,1)S(1)} %get-tuple-element.27), channel_id=1, source_target_pairs={{0,4},{4,0},{8,12},{12,8},{16,20},{20,16},{24,28},{28,24},{1,5},{5... | collective-permute-start | bytes 786440 | tf_op jit(solution)/shard_map/ppermute | solution.py:289
  6.0 5.2 %collective-permute-start = (bf16[4,32,128]{2,1,0:T(8,128)(2,1)S(1)}, bf16[4,32,128]{2,1,0:T(8,128)(2,1)S(1)}, u32[]{:S(2)}, u32[]{:S(2)}) collective-permute-start(bf16[4,32,128]{2,1,0:T(8,128)(2,1)S(1)} %get-tuple-element.21), channel_id=1, source_target_pairs={{0,1},{1,0},{2,3},{3,2},{4,5},{5,4},{6,7},{7,6},{8,9},{9,8},{10,11... | collective-permute-start | bytes 98312 | tf_op jit(solution)/shard_map/ppermute | solution.py:289
  7.5 2.1 %copy-start.8 = (f32[32]{0:T(128)S(1)}, f32[32]{0:T(128)}, u32[]{:S(2)}) copy-start(f32[32]{0:T(128)} %param.9) | copy-start | bytes 388
  7.5 5.9 %collective-permute-start.1 = (bf16[4,32,128]{2,1,0:T(8,128)(2,1)S(1)}, bf16[4,32,128]{2,1,0:T(8,128)(2,1)S(1)}, u32[]{:S(2)}, u32[]{:S(2)}) collective-permute-start(bf16[4,32,128]{2,1,0:T(8,128)(2,1)S(1)} %get-tuple-element.22), channel_id=1, source_target_pairs={{1,2},{2,1},{5,6},{6,5},{9,10},{10,9},{13,14},{14,13},{17,18},{18,... | collective-permute-start | bytes 98312 | tf_op jit(solution)/shard_map/ppermute | solution.py:289
  10.4 0.8 %copy-start.4 = (bf16[384,768]{1,0:T(8,128)(2,1)}, bf16[384,768]{1,0:T(8,128)(2,1)S(1)}, u32[]{:S(2)}) copy-start(bf16[384,768]{1,0:T(8,128)(2,1)S(1)} %get-tuple-element.32.a3) | copy-start | bytes 1769476
  13.5 11.3 %collective-permute-start.2 = (bf16[32,256]{1,0:T(8,128)(2,1)S(1)}, bf16[32,256]{1,0:T(8,128)(2,1)S(1)}, u32[]{:S(2)}, u32[]{:S(2)}) collective-permute-start(bf16[32,256]{1,0:T(8,128)(2,1)S(1)} %get-tuple-element.24), channel_id=1, source_target_pairs={{0,4},{4,0},{8,12},{12,8},{16,20},{20,16},{24,28},{28,24},{1,5},{5... | collective-permute-start | bytes 49160 | tf_op jit(solution)/shard_map/ppermute | solution.py:289
  13.6 11.2 %collective-permute-start.3 = (bf16[32,256]{1,0:T(8,128)(2,1)S(1)}, bf16[32,256]{1,0:T(8,128)(2,1)S(1)}, u32[]{:S(2)}, u32[]{:S(2)}) collective-permute-start(bf16[32,256]{1,0:T(8,128)(2,1)S(1)} %get-tuple-element.25), channel_id=1, source_target_pairs={{4,8},{8,4},{12,16},{16,12},{20,24},{24,20},{5,9},{9,5},{13,17},{1... | collective-permute-start | bytes 49160 | tf_op jit(solution)/shard_map/ppermute | solution.py:289
  24.8 9.1 %copy-start.5 = (bf16[384,768]{1,0:T(8,128)(2,1)S(1)}, bf16[384,768]{1,0:T(8,128)(2,1)}, u32[]{:S(2)}) copy-start(bf16[384,768]{1,0:T(8,128)(2,1)} %copy-done.4) | copy-start | bytes 1769476
  25.5 3.1 %copy-start.6 = (f32[64]{0:T(128)S(1)}, f32[64]{0:T(128)}, u32[]{:S(2)}) copy-start(f32[64]{0:T(128)} %param.11) | copy-start | bytes 772
  25.5 4.0 %collective-permute-start.6 = (bf16[2,9,32,128]{3,2,1,0:T(8,128)(2,1)S(1)}, bf16[2,9,32,128]{3,2,1,0:T(8,128)(2,1)S(1)}, u32[]{:S(2)}, u32[]{:S(2)}) collective-permute-start(bf16[2,9,32,128]{3,2,1,0:T(8,128)(2,1)S(1)} %edge.1.own), channel_id=1, source_target_pairs={{0,4},{4,0},{8,12},{12,8},{16,20},{20,16},{24,28},{28,24},{1,5},{5... | collective-permute-start | bytes 442376 | tf_op jit(solution)/shard_map/ppermute | solution.py:289
  25.6 8.3 %collective-permute-start.7 = (bf16[2,9,32,128]{3,2,1,0:T(8,128)(2,1)S(1)}, bf16[2,9,32,128]{3,2,1,0:T(8,128)(2,1)S(1)}, u32[]{:S(2)}, u32[]{:S(2)}) collective-permute-start(bf16[2,9,32,128]{3,2,1,0:T(8,128)(2,1)S(1)} %edge.1.own), channel_id=1, source_target_pairs={{4,8},{8,4},{12,16},{16,12},{20,24},{24,20},{5,9},{9,5},{13,17},{1... | collective-permute-start | bytes 442376 | tf_op jit(solution)/shard_map/ppermute | solution.py:289
  28.7 0.7 %copy-start.7 = (f32[64]{0:T(128)S(1)}, f32[64]{0:T(128)}, u32[]{:S(2)}) copy-start(f32[64]{0:T(128)} %param.13) | copy-start | bytes 772

commit v2 on v0

v2 whole, which is shorter than its diff:
```python
import jax
import jax.numpy as jnp
from jax import lax
from jax.experimental import pallas as pl
from jax.experimental.pallas import tpu as pltpu
from jax.sharding import PartitionSpec as P


BF = jnp.bfloat16
F32 = jnp.float32
VM = pl.BlockSpec(memory_space=pltpu.VMEM)
G = 8


def call(body, outs, scratch=(), flops=0):
    def run(*args):
        return pl.pallas_call(
            body,
            out_shape=[jax.ShapeDtypeStruct(s, d) for s, d in outs],
            in_specs=[VM] * len(args),
            out_specs=[VM] * len(outs),
            scratch_shapes=list(scratch),
            compiler_params=pltpu.CompilerParams(vmem_limit_bytes=16 << 20),
            cost_estimate=pl.CostEstimate(flops=flops, bytes_accessed=1 << 20, transcendentals=0),
        )(*args)

    return run


def dot(a, b):
    return jnp.dot(a, b, preferred_element_type=F32)


def lanes(shape):
    return lax.broadcasted_iota(jnp.int32, shape, len(shape) - 1)


def roll(v, by):
    return pltpu.roll(v, by % v.shape[-1], v.ndim - 1)


def weights_kernel(w1, w2, w3, b1, b2, b3, a1, a1s, a2, a3, c1, c2, c3, evens, ends):
    def band(pieces, first):
        zero = jnp.zeros_like(pieces[0])
        return jnp.concatenate([zero] + pieces if first else pieces + [zero], axis=1)

    n1, n2 = w1.shape[3], w3.shape[3]
    for e in range(3):
        for f in range(3):
            p1 = [w1[a, e, f].astype(F32) for a in range(3)]
            p2 = [w2[a, e, f].astype(F32).T for a in range(3)]
            p3 = [w3[a, e, f].astype(F32) for a in range(3)]
            for xo in range(2):
                v1 = band(p1, xo).astype(BF)
                k1 = v1.shape[1]
                a1[pl.ds((xo * 3 + f) * n1, n1), pl.ds(e * k1, k1)] = v1
                a1s[pl.ds(((xo * 3 + e) * 3 + f) * n1, n1), :] = v1
                a2[pl.ds((xo * 3 + f) * n2, n2), pl.ds(e * k1, k1)] = band(p2, xo).astype(BF)
                a3[pl.ds((xo * 3 + f) * n2, n2), pl.ds(e * 2 * k1, 2 * k1)] = band(p3, xo).astype(BF)
    for b, c in ((b1, c1), (b2, c2), (b3, c3)):
        n = b.shape[1]
        eye = lax.broadcasted_iota(jnp.int32, (n, n), 0) == lax.broadcasted_iota(jnp.int32, (n, n), 1)
        column = jnp.sum(jnp.where(eye, jnp.broadcast_to(b[...], (n, n)), 0.0), axis=1, keepdims=True)
        c[...] = jnp.broadcast_to(column, c.shape)
    src = lax.broadcasted_iota(jnp.int32, evens.shape, 0)
    dst = lax.broadcasted_iota(jnp.int32, evens.shape, 1)
    evens[...] = jnp.where(src == 2 * dst, 1.0, 0.0).astype(BF)
    half = evens.shape[1]
    top = half - 2 * G
    src = lax.broadcasted_iota(jnp.int32, ends.shape, 0) - top
    dst = lax.broadcasted_iota(jnp.int32, ends.shape, 1)
    move = (
        ((dst == 0) & (src == 5))
        | ((dst == half - 1) & (src == G + 1))
        | ((dst == half) & (src == G + 3))
        | ((dst == half + 1) & (src == G + 5))
        | ((dst == 254) & (src == 1))
        | ((dst == 255) & (src == 3))
    )
    ends[...] = jnp.where(move, 1.0, 0.0).astype(BF)


def relayout(cells, lo, hi, store):
    chans, depth, cross = cells.shape
    flat = cells.astype(F32).reshape(chans * depth, cross)
    lo[...] = flat[:, :128]
    hi[...] = flat[:, 128:]
    lane = lanes((chans, 128))
    left = jnp.zeros((chans, 128), F32)
    right = jnp.zeros((chans, 128), F32)
    for z in range(depth):
        a = lo[pl.ds(z, chans, stride=depth), :]
        b = hi[pl.ds(z, chans, stride=depth), :]
        store(z, a.astype(BF), b.astype(BF))
        here = (lane >= z * G) & (lane < z * G + G)
        left = jnp.where(here, roll(a, z * G), left)
        right = jnp.where(here, roll(b, z * G + G), right)
    part = lane % G
    msg_l = jnp.where(part >= 3, roll(left, 3), 0.0).astype(BF)
    own_l = jnp.where(part >= 5, roll(left, 5), 0.0).astype(BF)
    msg_r = jnp.where(part < 5, roll(right, -3), 0.0).astype(BF)
    own_r = jnp.where(part < 3, roll(right, -5), 0.0).astype(BF)
    return msg_l, msg_r, own_l, own_r


def pack_kernel(image, own, near_row, far_row, far_small, msgs, olds, lo, hi):
    _, inline, depth, _ = image.shape
    odd = lax.axis_index("gx") % 2
    for x in range(inline):

        def store(z, a, b):
            own[z, x, :, :128] = a
            own[z, x, :, 128:] = b

        msg_l, msg_r, own_l, own_r = relayout(image[:, x], lo, hi, store)
        msgs[x, :, :128] = msg_l
        msgs[x, :, 128:] = msg_r
        olds[x, :, :128] = own_l
        olds[x, :, 128:] = own_r
    near, far = (inline - 1) * (1 - odd), (inline - 1) * odd
    near_row[pl.ds(0, depth)] = own[:, near]
    near_row[depth] = msgs[near]
    near_row[depth + 1] = olds[near]
    far_row[...] = own[:, far]
    far_small[0] = msgs[far]
    far_small[1] = olds[far]


def at_map_end():
    at = lax.axis_index("gx")
    return (at == 0) | (at == lax.axis_size("gx") - 1)


def strip_kernel(far_row, mate, msgs, olds, send_l, send_r, strips):
    inline = msgs.shape[0]
    depth = mate.shape[0] - 2
    odd = lax.axis_index("gx") % 2
    outside = at_map_end()
    far, near = (inline + 1) * odd, (inline + 1) * (1 - odd)
    zero = jnp.zeros(strips.shape[1:], BF)
    far_msg = jnp.where(outside, zero, far_row[0])
    near_msg = mate[depth]
    strips[pl.ds(1, inline)] = olds[...]
    strips[near] = mate[depth + 1]
    strips[far] = jnp.where(outside, zero, far_row[1])
    for send, half in ((send_l, pl.ds(0, 128)), (send_r, pl.ds(128, 128))):
        send[pl.ds(1, inline)] = msgs[:, :, half]
        send[near] = near_msg[:, half.start : half.start + 128]
        send[far] = far_msg[:, half.start : half.start + 128]


def fine_pair(own, halo, halo_first, outside, a1, bias, evens, pooled, pad, acc):
    depth, inline, chans, cross = own.shape
    width = inline * chans
    zero = jnp.zeros((width, cross), BF)
    pad[pl.ds(0, width), :] = zero
    pad[pl.ds((depth + 1) * width, width), :] = zero
    first = 1 - halo_first
    for z in range(depth):
        base = (z + 1) * width
        beyond = halo[z] if outside is None else jnp.where(outside, zero[:chans], halo[z])
        pad[pl.ds(pl.multiple_of(base + (1 - halo_first) * (inline - 1) * chans, chans), chans), :] = beyond
        for r in range(inline - 1):
            pad[pl.ds(pl.multiple_of(base + (r + halo_first) * chans, chans), chans), :] = own[z, first + r]

    def layer(z):
        g = dot(a1[...], pad[pl.ds(z * width, 3 * width), :])
        rows = []
        for xo in range(2):
            t = g[xo * 3 * chans : (xo + 1) * 3 * chans]
            rows.append(roll(t[:chans], 1) + t[chans : 2 * chans] + roll(t[2 * chans :], -1))
        return jnp.maximum(rows[0], rows[1])

    for z in range(depth // 2):
        m = jnp.maximum(layer(2 * z), layer(2 * z + 1))
        m = jnp.maximum(jnp.maximum(m, roll(m, -1)) + bias[...], 0.0)
        acc[pl.ds(z * chans, chans), :] = m.astype(BF)
    pooled[...] = dot(acc[...], evens[...]).astype(BF).reshape(pooled.shape)


def early_kernel(own, mate, a1, bias, evens, pooled, pad, acc):
    fine_pair(own, mate, lax.axis_index("gx") % 2, None, a1, bias, evens, pooled, pad, acc)


def late_kernel(own, halo, strips, got_l, got_r, early, a1, a1s, bias, evens, message, pad, acc, rows, late):
    tall, chans, _ = strips.shape
    half_depth = early.shape[0]
    odd = lax.axis_index("gx") % 2
    message[1 - odd, pl.ds(0, half_depth)] = early[...]
    fine_pair(own, halo, 1 - odd, at_map_end(), a1, bias, evens, late, pad, acc)
    message[odd, pl.ds(0, half_depth)] = late[...]
    at, end = lax.axis_index("gy"), lax.axis_size("gy") - 1
    part = lanes((tall * chans, 128)) % G
    from_l = jnp.where(at == 0, 0.0, got_l[...].reshape(tall * chans, 128))
    from_r = jnp.where(at == end, 0.0, got_r[...].reshape(tall * chans, 128))
    s = strips[...].reshape(tall * chans, 256)
    rows[:, :128] = jnp.where(part < 5, from_l, s[:, :128]).astype(BF)
    rows[:, 128:] = jnp.where(part < 3, s[:, 128:], from_r).astype(BF)
    lane = lanes((chans, 128))
    for pair in range(2):
        g = dot(a1s[...], rows[pl.ds(pair * 2 * chans, 4 * chans), :])
        sides = []
        for side in range(2):
            best = None
            for xo in range(2):
                total = None
                for e in range(3):
                    part = None
                    for f in range(3):
                        k = (xo * 3 + e) * 3 + f
                        t = g[k * chans : (k + 1) * chans, side * 128 : side * 128 + 128]
                        t = roll(t, -(G * (e - 1) + f - 1))
                        part = t if part is None else part + t
                    if e == 0:
                        part = jnp.where(lane >= G, part, 0.0)
                    if e == 2:
                        part = jnp.where(lane < 128 - G, part, 0.0)
                    total = part if total is None else total + part
                best = total if best is None else jnp.maximum(best, total)
            best = jnp.maximum(best, roll(best, -G))
            best = jnp.maximum(best, roll(best, -1))
            best = jnp.maximum(best + bias[:, :128], 0.0)
            cell = lane % G
            outside = (cell < 5) & (at == 0) if side == 0 else (cell > 1) & (at == end)
            sides.append(jnp.where(outside, 0.0, best))
        edges = jnp.where((lane // G) % 2 == 0, sides[0], roll(sides[1], G))
        message[pair, half_depth] = edges.astype(BF)


def coarse_pair(own, other, own_first, beyond, a2, bias, ends, outside_x, put, pad, edge):
    coarse, tall, chans, half = own.shape
    depth = tall - 1
    c2 = bias.shape[0]
    width = 2 * coarse * chans
    at, end = lax.axis_index("gy"), lax.axis_size("gy") - 1
    spots = [(1 - own_first) * coarse, own_first * coarse]
    for source, spot in zip((own, other), spots):
        for r in range(coarse):
            value = source[r, depth]
            if source is other and beyond is not None:
                value = jnp.where(beyond, jnp.zeros_like(value), value)
            edge[pl.ds(pl.multiple_of((spot + r) * chans, chans), chans), :] = value
    zero = jnp.zeros((width, 256), BF)
    pad[pl.ds(0, width), :] = zero
    pad[pl.ds((depth + 1) * width, width), :] = zero
    lane = lanes((chans, half))
    inner = (lane > 0) & (lane < half - 1)
    for z in range(depth):
        base = (z + 1) * width
        fixed = dot(edge[...], ends[pl.ds(half - 2 * G - 2 * G * z, half), :]).astype(BF)
        pad[pl.ds(base, width), :] = fixed
        for source, spot in zip((own, other), spots):
            for r in range(coarse):
                where = pl.ds(pl.multiple_of(base + (spot + r) * chans, chans), chans)
                use = inner if source is own or beyond is None else inner & ~beyond
                pad[where, :half] = jnp.where(use, source[r, z], pad[where, :half])
    col = lanes((c2, 256))
    outside_y = ((col == 255) & (at == 0)) | ((col == half) & (at == end))
    for z in range(depth):
        g = dot(a2[...], pad[pl.ds(z * width, 3 * width), :])
        for xo in range(2):
            t = g[xo * 3 * c2 : (xo + 1) * 3 * c2]
            v = roll(t[:c2], 1) + t[c2 : 2 * c2] + roll(t[2 * c2 :], -1)
            v = jnp.maximum(v + bias[...], 0.0)
            hide = outside_y if outside_x is None else outside_y | outside_x[xo]
            put(z, xo, jnp.where(hide, 0.0, v).astype(BF))


def coarse_early_kernel(own, mate, a2, bias, ends, second, pad, edge):
    def put(z, xo, v):
        second[z, xo] = v

    coarse_pair(own, mate, 1 - lax.axis_index("gx") % 2, None, a2, bias, ends, None, put, pad, edge)


def coarse_late_kernel(own, far, second, a2, b2, a3, b3, ends, out, pad, edge, pad3, wide):
    depth, _, c2, _ = second.shape
    half = out.shape[-1]
    odd = lax.axis_index("gx") % 2
    at, end = lax.axis_index("gx"), lax.axis_size("gx") - 1
    width = 4 * c2
    zero = jnp.zeros((width, 256), BF)
    pad3[pl.ds(0, width), :] = zero
    pad3[pl.ds((depth + 1) * width, width), :] = zero
    for z in range(depth):
        for r in range(2):
            spot = (z + 1) * width + ((1 - odd) * 2 + r) * c2
            pad3[pl.ds(pl.multiple_of(spot, c2), c2), :] = second[z, r]

    def put(z, xo, v):
        spot = (z + 1) * width + (odd * 2 + xo) * c2
        pad3[pl.ds(pl.multiple_of(spot, c2), c2), :] = v

    outside = [(odd == 0) & (at == 0), (odd == 1) & (at == end)]
    coarse_pair(own, far, odd, at_map_end(), a2, b2, ends, outside, put, pad, edge)
    for z in range(depth):
        g = dot(a3[...], pad3[pl.ds(z * width, 3 * width), :])
        for xo in range(2):
            t = g[xo * 3 * c2 : (xo + 1) * 3 * c2]
            v = roll(t[:c2], 1) + t[c2 : 2 * c2] + roll(t[2 * c2 :], -1)
            v = jnp.maximum(v + b3[...], 0.0)
            wide[xo, pl.ds(z, c2, stride=depth), :] = v[:, :half]
    for xo in range(2):
        out[:, xo] = wide[xo].reshape(c2, depth, half).astype(BF)


def swap(value, parity):
    count = lax.axis_size("gx")
    pairs = []
    for i in range(parity, count, 2):
        j = (i + 1) % count
        pairs += [(i, j), (j, i)]
    return lax.ppermute(value, "gx", pairs)


def shift(value, by):
    count = lax.axis_size("gy")
    return lax.ppermute(value, "gy", [(i, (i + by) % count) for i in range(count)])


def per_device(image, w_first, b_first, w_second, b_second, w_third, b_third):
    c1, inline, depth, cross = image.shape
    c2 = w_third.shape[0]
    half, hz, coarse = cross // 2, depth // 2, inline // 2
    k1 = 4 * c1
    tall = inline + 2
    own, near_row, far_row, far_small, msgs, olds = call(
        pack_kernel,
        [
            ((depth, inline, c1, cross), BF),
            ((depth + 2, c1, cross), BF),
            ((depth, c1, cross), BF),
            ((2, c1, 256), BF),
            ((inline, c1, 256), BF),
            ((inline, c1, 256), BF),
        ],
        scratch=[pltpu.VMEM((c1 * depth, 128), F32)] * 2,
        flops=1 << 28,
    )(image)
    got_small = swap(far_small, 1)
    got_far = swap(far_row, 1)
    got_row = swap(near_row, 0)
    a1, a1s, a2, a3, b1, b2, b3, evens, ends = call(
        weights_kernel,
        [
            ((6 * c1, 3 * k1), BF),
            ((18 * c1, k1), BF),
            ((6 * c2, 3 * k1), BF),
            ((6 * c2, 12 * c2), BF),
            ((c1, 256), F32),
            ((c2, 256), F32),
            ((c2, 256), F32),
            ((cross, half), BF),
            ((2 * half, 256), BF),
        ],
        flops=1 << 28,
    )(
        jnp.transpose(w_first, (2, 3, 4, 0, 1)),
        jnp.transpose(w_second, (2, 3, 4, 1, 0)),
        jnp.transpose(w_third, (2, 3, 4, 0, 1)),
        b_first.reshape(1, c1),
        b_second.reshape(1, c2),
        b_third.reshape(1, c2),
    )
    fine = [pltpu.VMEM(((depth + 2) * k1, cross), BF), pltpu.VMEM((hz * c1, cross), BF)]
    (early,) = call(early_kernel, [((hz, c1, half), BF)], scratch=fine, flops=1 << 29)(own, got_row, a1, b1, evens)
    send_l, send_r, strips = call(
        strip_kernel, [((tall, c1, 128), BF)] * 2 + [((tall, c1, 256), BF)], flops=1 << 20
    )(got_small, got_row, msgs, olds)
    got_l = shift(send_r, 1)
    got_r = shift(send_l, -1)
    (message,) = call(
        late_kernel,
        [((coarse, hz + 1, c1, half), BF)],
        scratch=fine + [pltpu.VMEM((tall * c1, 256), BF), pltpu.VMEM((hz, c1, half), BF)],
        flops=1 << 29,
    )(own, got_far, strips, got_l, got_r, early, a1, a1s, b1, evens)
    got_pa = swap(message, 0)
    got_pb = swap(message, 1)
    mid = [pltpu.VMEM(((hz + 2) * k1, 256), BF), pltpu.VMEM((k1, half), BF)]
    (second,) = call(
        coarse_early_kernel, [((hz, 2, c2, 256), BF)], scratch=mid, flops=1 << 29
    )(message, got_pa, a2, b2, ends)
    (out,) = call(
        coarse_late_kernel,
        [((c2, coarse, hz, half), BF)],
        scratch=mid + [pltpu.VMEM(((hz + 2) * 4 * c2, 256), BF), pltpu.VMEM((coarse, c2 * hz, half), F32)],
        flops=1 << 29,
    )(message, got_pb, second, a2, b2, a3, b3, ends)
    return out


def solution(mesh):
    placed = (P(None, "gx", None, "gy"), P(), P(), P(), P(), P(), P())

    return jax.shard_map(per_device, mesh=mesh, in_specs=placed, out_specs=P(None, "gx", None, "gy"), check_vma=False)
```

time: 177 us -> 31.5 us (0.18)
  the two profiles are of different devices: /device:TPU:3 before, /device:TPU:0 now
where the time goes in v2:
time: 31.5 us; the launch traced here: 31.4 us
  Pallas kernels  10.1 us (32%)
  starting transfers between devices  10.1 us (32%)
  waiting for transfers between devices  9.17 us (29%)
  local copies, waits for them, and re-layouts  1.89 us (6%)
    pallas_call x7, Pallas kernels, run(): pl.pallas_call(body, out_shape=[jax.ShapeDtypeStruct(s, d) for s, d in ou...  10.1 us
    ppermute x5, waiting for transfers between devices, swap(): return lax.ppermute(value, 'gx', pairs)  8.03 us
    ppermute x5, starting transfers between devices, swap(): return lax.ppermute(value, 'gx', pairs)  6.11 us
    ppermute x2, starting transfers between devices, shift(): lax.ppermute(value, 'gy', [(i, (i + by) % count) for i in range(count)])  4.04 us
    unnamed x14, local copies, waits for them, and re-layouts  1.89 us
    ppermute x2, waiting for transfers between devices, shift(): lax.ppermute(value, 'gy', [(i, (i + by) % count) for i in range(count)])  1.14 us
  transfers between devices with their start and end apart: 7, of which 4 were waited for; matrix products, arithmetic and copies ran while one was open for 0% of the time, Pallas kernels for 11%

profile of v2, /device:TPU:0, one launch (start us, length us, event | category | flops | bytes accessed | tf_op | source)
XLA Modules:
  0.0 31.4 jit_solution(17064656896776454168)
XLA Ops:
  0.0 1.2 %copy-done = bf16[32,4,16,256]{3,2,1,0:T(8,128)(2,1)S(1)} copy-done((bf16[32,4,16,256]{3,2,1,0:T(8,128)(2,1)S(1)}, bf16[32,4,16,256]{3,2,1,0:T(8,128)(2,1)}, u32[]{:S(2)}) %copy-start) | copy-done | bytes 1048600
  1.2 1.1 %shard_map.73 = (bf16[16,4,32,256]{3,2,1,0:T(8,128)(2,1)S(1)}, bf16[18,32,256]{2,1,0:T(8,128)(2,1)S(1)}, bf16[16,32,256]{2,1,0:T(8,128)(2,1)S(1)}, bf16[2,32,256...) custom-call(bf16[32,4,16,256]{3,2,1,0:T(8,128)(2,1)S(1)} %copy-done), custom_call_target="tpu_custom_call" | custom-call | flops 268435456 | bytes 1048576 | tf_op jit(solution)/shard_map/pallas_call | solution.py:17
  2.4 0.6 %collective-permute-start.2 = (bf16[18,32,256]{2,1,0:T(8,128)(2,1)S(1)}, bf16[18,32,256]{2,1,0:T(8,128)(2,1)S(1)}, u32[]{:S(2)}, u32[]{:S(2)}) collective-permute-start(bf16[18,32,256]{2,1,0:T(8,128)(2,1)S(1)} %get-tuple-element.26), channel_id=1, source_target_pairs={{0,4},{4,0},{8,12},{12,8},{16,20},{20,16},{24,28},{28,24},{1,5},{5... | collective-permute-start | bytes 884744 | tf_op jit(solution)/shard_map/ppermute | solution.py:313
  2.9 3.6 %collective-permute-start = (bf16[16,32,256]{2,1,0:T(8,128)(2,1)S(1)}, bf16[16,32,256]{2,1,0:T(8,128)(2,1)S(1)}, u32[]{:S(2)}, u32[]{:S(2)}) collective-permute-start(bf16[16,32,256]{2,1,0:T(8,128)(2,1)S(1)} %get-tuple-element.24), channel_id=1, source_target_pairs={{4,8},{8,4},{12,16},{16,12},{20,24},{24,20},{28,0},{0,28},{5,9},{9... | collective-permute-start | bytes 786440 | tf_op jit(solution)/shard_map/ppermute | solution.py:313
  6.5 0.0 collective-permute-start.1
  6.6 0.6 %copy-done.4 = f32[32]{0:T(128)S(1)} copy-done((f32[32]{0:T(128)S(1)}, f32[32]{0:T(128)}, u32[]{:S(2)}) %copy-start.4) | copy-done | bytes 152
  7.2 0.0 copy-done.5
  7.2 0.0 copy-done.6
  7.2 0.7 %shard_map.75 = (bf16[192,384]{1,0:T(8,128)(2,1)S(1)}, bf16[576,128]{1,0:T(8,128)(2,1)S(1)}, bf16[384,384]{1,0:T(8,128)(2,1)S(1)}, bf16[384,768]{1,0:T(8,128)(2,...) custom-call(bf16[3,3,3,32,32]{4,3,2,1,0:T(8,128)(2,1)S(1)} %bitcast., ...), custom_call_target="tpu_custom_call" | custom-call | flops 268435456 | bytes 1048576 | tf_op jit(solution)/shard_map/pallas_call | solution.py:17
  7.9 5.3 %collective-permute-done.1.far_row = bf16[2,32,256]{2,1,0:T(8,128)(2,1)S(1)} collective-permute-done((bf16[2,32,256]{2,1,0:T(8,128)(2,1)S(1)}, bf16[2,32,256]{2,1,0:T(8,128)(2,1)S(1)}, u32[]{:S(2)}, u32[]{:S(2)}) %collective-permute-start.1) | collective-permute-done | bytes 32800 | tf_op jit(solution)/shard_map/ppermute | solution.py:313
  13.2 0.0 collective-permute-done.2.mate
  13.3 1.9 %collective-permute-start.3 = (bf16[6,32,128]{2,1,0:T(8,128)(2,1)S(1)}, bf16[6,32,128]{2,1,0:T(8,128)(2,1)S(1)}, u32[]{:S(2)}, u32[]{:S(2)}) collective-permute-start(bf16[6,32,128]{2,1,0:T(8,128)(2,1)S(1)} %get-tuple-element.30), channel_id=1, source_target_pairs={{0,1},{1,2},{2,3},{3,0},{4,5},{5,6},{6,7},{7,4},{8,9},{9,10},{10,1... | collective-permute-start | bytes 147464 | tf_op jit(solution)/shard_map/ppermute | solution.py:318
  15.2 2.1 %collective-permute-start.4 = (bf16[6,32,128]{2,1,0:T(8,128)(2,1)S(1)}, bf16[6,32,128]{2,1,0:T(8,128)(2,1)S(1)}, u32[]{:S(2)}, u32[]{:S(2)}) collective-permute-start(bf16[6,32,128]{2,1,0:T(8,128)(2,1)S(1)} %get-tuple-element.31), channel_id=1, source_target_pairs={{0,3},{1,0},{2,1},{3,2},{4,7},{5,4},{6,5},{7,6},{8,11},{9,8},{10,9... | collective-permute-start | bytes 147464 | tf_op jit(solution)/shard_map/ppermute | solution.py:318
  17.3 1.4 %shard_map.76.early = bf16[8,32,128]{2,1,0:T(8,128)(2,1)S(1)} custom-call(bf16[16,4,32,256]{3,2,1,0:T(8,128)(2,1)S(1)} %get-tuple-element.23.own, bf16[18,32,256]{2,1,0:T(8,128)(2,1)S(1)} %collective-permute-done.2.mate, bf16[192,384]{1,0:T(8,128)(2,1)S(1)} %get-tuple-element.32.a1, f32[32,256]{1,0:T(8,128)S(1)} %get-tuple-element.33.bias, ...), custom_call_target="tpu_custom_call" | custom-call | flops 536870912 | bytes 1048576 | tf_op jit(solution)/shard_map/pallas_call | solution.py:17
  18.7 0.0 collective-permute-done.halo
  18.7 0.7 %collective-permute-done.3.got_l = bf16[6,32,128]{2,1,0:T(8,128)(2,1)S(1)} collective-permute-done((bf16[6,32,128]{2,1,0:T(8,128)(2,1)S(1)}, bf16[6,32,128]{2,1,0:T(8,128)(2,1)S(1)}, u32[]{:S(2)}, u32[]{:S(2)}) %collective-permute-start.3) | collective-permute-done | bytes 49184 | tf_op jit(solution)/shard_map/ppermute | solution.py:318
  19.4 0.4 %collective-permute-done.4.got_r = bf16[6,32,128]{2,1,0:T(8,128)(2,1)S(1)} collective-permute-done((bf16[6,32,128]{2,1,0:T(8,128)(2,1)S(1)}, bf16[6,32,128]{2,1,0:T(8,128)(2,1)S(1)}, u32[]{:S(2)}, u32[]{:S(2)}) %collective-permute-start.4) | collective-permute-done | bytes 49184 | tf_op jit(solution)/shard_map/ppermute | solution.py:318
  19.8 1.9 %shard_map.77.own = bf16[2,9,32,128]{3,2,1,0:T(8,128)(2,1)S(1)} custom-call(bf16[16,4,32,256]{3,2,1,0:T(8,128)(2,1)S(1)} %get-tuple-element.23.own, bf16[16,32,256]{2,1,0:T(8,128)(2,1)S(1)} %collective-permute-done.halo, bf16[6,32,256]{2,1,0:T(8,128)(2,1)S(1)} %get-tuple-element.29.strips, bf16[6,32,128]{2,1,0:T(8,128)(2,1)S(1)} %collective-permute-done.3.got_l, ...), custom_call_target="tpu_custom_call" | custom-call | flops 536870912 | bytes 1048576 | tf_op jit(solution)/shard_map/pallas_call | solution.py:17
  21.7 0.0 collective-permute-start.6
  21.8 1.9 %collective-permute-start.5 = (bf16[2,9,32,128]{3,2,1,0:T(8,128)(2,1)S(1)}, bf16[2,9,32,128]{3,2,1,0:T(8,128)(2,1)S(1)}, u32[]{:S(2)}, u32[]{:S(2)}) collective-permute-start(bf16[2,9,32,128]{3,2,1,0:T(8,128)(2,1)S(1)} %shard_map.77.own), channel_id=1, source_target_pairs={{4,8},{8,4},{12,16},{16,12},{20,24},{24,20},{28,0},{0,28},{5,9},{9... | collective-permute-start | bytes 442376 | tf_op jit(solution)/shard_map/ppermute | solution.py:313
  23.7 0.0 collective-permute-done.6.mate
  23.7 1.4 %shard_map.78.second = bf16[8,2,64,256]{3,2,1,0:T(8,128)(2,1)S(1)} custom-call(bf16[2,9,32,128]{3,2,1,0:T(8,128)(2,1)S(1)} %shard_map.77.own, bf16[2,9,32,128]{3,2,1,0:T(8,128)(2,1)S(1)} %collective-permute-done.6.mate, bf16[384,384]{1,0:T(8,128)(2,1)S(1)} %get-tuple-element.36.a2, f32[64,256]{1,0:T(8,128)S(1)} %get-tuple-element.37.bias.b2, ...), custom_call_target="tpu_custom_call" | custom-call | flops 536870912 | bytes 1048576 | tf_op jit(solution)/shard_map/pallas_call | solution.py:17
  25.1 2.7 %collective-permute-done.5.far = bf16[2,9,32,128]{3,2,1,0:T(8,128)(2,1)S(1)} collective-permute-done((bf16[2,9,32,128]{3,2,1,0:T(8,128)(2,1)S(1)}, bf16[2,9,32,128]{3,2,1,0:T(8,128)(2,1)S(1)}, u32[]{:S(2)}, u32[]{:S(2)}) %collective-permute-start.5) | collective-permute-done | bytes 147488 | tf_op jit(solution)/shard_map/ppermute | solution.py:313
  27.9 3.5 %shard_map.79 = bf16[64,2,8,128]{3,2,1,0:T(8,128)(2,1)} custom-call(bf16[2,9,32,128]{3,2,1,0:T(8,128)(2,1)S(1)} %shard_map.77.own, bf16[2,9,32,128]{3,2,1,0:T(8,128)(2,1)S(1)} %collective-permute-done.5.far, bf16[8,2,64,256]{3,2,1,0:T(8,128)(2,1)S(1)} %shard_map.78.second, bf16[384,384]{1,0:T(8,128)(2,1)S(1)} %get-tuple-element.36.a2, ...), custom_call_target="tpu_custom_call" | custom-call | flops 536870912 | bytes 1048576 | tf_op jit(solution)/shard_map/pallas_call | solution.py:17
  (11 shorter events, 0.0 us)
Async XLA Ops:
  0.0 1.2 %copy-start = (bf16[32,4,16,256]{3,2,1,0:T(8,128)(2,1)S(1)}, bf16[32,4,16,256]{3,2,1,0:T(8,128)(2,1)}, u32[]{:S(2)}) copy-start(bf16[32,4,16,256]{3,2,1,0:T(8,128)(2,1)} %image.1) | copy-start | bytes 3145732
  1.2 5.3 %copy-start.1 = (bf16[64,64,3,3,3]{1,0,4,3,2:T(8,128)(2,1)S(1)}, bf16[64,64,3,3,3]{1,0,4,3,2:T(8,128)(2,1)}, u32[]{:S(2)}) copy-start(bf16[64,64,3,3,3]{1,0,4,3,2:T(8,128)(2,1)} %param.12) | copy-start | bytes 663556
  1.2 5.3 %copy-start.2 = (bf16[32,32,3,3,3]{1,0,4,3,2:T(8,128)(2,1)S(1)}, bf16[32,32,3,3,3]{1,0,4,3,2:T(8,128)(2,1)}, u32[]{:S(2)}) copy-start(bf16[32,32,3,3,3]{1,0,4,3,2:T(8,128)(2,1)} %param.8) | copy-start | bytes 165892
  1.2 5.3 %copy-start.3 = (bf16[64,32,3,3,3]{0,1,4,3,2:T(8,128)(2,1)S(1)}, bf16[64,32,3,3,3]{0,1,4,3,2:T(8,128)(2,1)}, u32[]{:S(2)}) copy-start(bf16[64,32,3,3,3]{0,1,4,3,2:T(8,128)(2,1)} %param.10) | copy-start | bytes 331780
  2.4 10.8 %collective-permute-start.2 = (bf16[18,32,256]{2,1,0:T(8,128)(2,1)S(1)}, bf16[18,32,256]{2,1,0:T(8,128)(2,1)S(1)}, u32[]{:S(2)}, u32[]{:S(2)}) collective-permute-start(bf16[18,32,256]{2,1,0:T(8,128)(2,1)S(1)} %get-tuple-element.26), channel_id=1, source_target_pairs={{0,4},{4,0},{8,12},{12,8},{16,20},{20,16},{24,28},{28,24},{1,5},{5... | collective-permute-start | bytes 884744 | tf_op jit(solution)/shard_map/ppermute | solution.py:313
  2.9 15.7 %collective-permute-start = (bf16[16,32,256]{2,1,0:T(8,128)(2,1)S(1)}, bf16[16,32,256]{2,1,0:T(8,128)(2,1)S(1)}, u32[]{:S(2)}, u32[]{:S(2)}) collective-permute-start(bf16[16,32,256]{2,1,0:T(8,128)(2,1)S(1)} %get-tuple-element.24), channel_id=1, source_target_pairs={{4,8},{8,4},{12,16},{16,12},{20,24},{24,20},{28,0},{0,28},{5,9},{9... | collective-permute-start | bytes 786440 | tf_op jit(solution)/shard_map/ppermute | solution.py:313
  6.5 6.7 %collective-permute-start.1 = (bf16[2,32,256]{2,1,0:T(8,128)(2,1)S(1)}, bf16[2,32,256]{2,1,0:T(8,128)(2,1)S(1)}, u32[]{:S(2)}, u32[]{:S(2)}) collective-permute-start(bf16[2,32,256]{2,1,0:T(8,128)(2,1)S(1)} %get-tuple-element.25), channel_id=1, source_target_pairs={{4,8},{8,4},{12,16},{16,12},{20,24},{24,20},{28,0},{0,28},{5,9},{9... | collective-permute-start | bytes 98312 | tf_op jit(solution)/shard_map/ppermute | solution.py:313
  6.5 0.7 %copy-start.4 = (f32[32]{0:T(128)S(1)}, f32[32]{0:T(128)}, u32[]{:S(2)}) copy-start(f32[32]{0:T(128)} %param.9) | copy-start | bytes 388
  6.5 0.7 %copy-start.5 = (f32[64]{0:T(128)S(1)}, f32[64]{0:T(128)}, u32[]{:S(2)}) copy-start(f32[64]{0:T(128)} %param.11) | copy-start | bytes 772
  6.5 0.7 %copy-start.6 = (f32[64]{0:T(128)S(1)}, f32[64]{0:T(128)}, u32[]{:S(2)}) copy-start(f32[64]{0:T(128)} %param.13) | copy-start | bytes 772
  13.3 6.1 %collective-permute-start.3 = (bf16[6,32,128]{2,1,0:T(8,128)(2,1)S(1)}, bf16[6,32,128]{2,1,0:T(8,128)(2,1)S(1)}, u32[]{:S(2)}, u32[]{:S(2)}) collective-permute-start(bf16[6,32,128]{2,1,0:T(8,128)(2,1)S(1)} %get-tuple-element.30), channel_id=1, source_target_pairs={{0,1},{1,2},{2,3},{3,0},{4,5},{5,6},{6,7},{7,4},{8,9},{9,10},{10,1... | collective-permute-start | bytes 147464 | tf_op jit(solution)/shard_map/ppermute | solution.py:318
  15.2 4.6 %collective-permute-start.4 = (bf16[6,32,128]{2,1,0:T(8,128)(2,1)S(1)}, bf16[6,32,128]{2,1,0:T(8,128)(2,1)S(1)}, u32[]{:S(2)}, u32[]{:S(2)}) collective-permute-start(bf16[6,32,128]{2,1,0:T(8,128)(2,1)S(1)} %get-tuple-element.31), channel_id=1, source_target_pairs={{0,3},{1,0},{2,1},{3,2},{4,7},{5,4},{6,5},{7,6},{8,11},{9,8},{10,9... | collective-permute-start | bytes 147464 | tf_op jit(solution)/shard_map/ppermute | solution.py:318
  21.7 2.0 %collective-permute-start.6 = (bf16[2,9,32,128]{3,2,1,0:T(8,128)(2,1)S(1)}, bf16[2,9,32,128]{3,2,1,0:T(8,128)(2,1)S(1)}, u32[]{:S(2)}, u32[]{:S(2)}) collective-permute-start(bf16[2,9,32,128]{3,2,1,0:T(8,128)(2,1)S(1)} %shard_map.77.own), channel_id=1, source_target_pairs={{0,4},{4,0},{8,12},{12,8},{16,20},{20,16},{24,28},{28,24},{1,5},{5... | collective-permute-start | bytes 442376 | tf_op jit(solution)/shard_map/ppermute | solution.py:313
  21.8 6.1 %collective-permute-start.5 = (bf16[2,9,32,128]{3,2,1,0:T(8,128)(2,1)S(1)}, bf16[2,9,32,128]{3,2,1,0:T(8,128)(2,1)S(1)}, u32[]{:S(2)}, u32[]{:S(2)}) collective-permute-start(bf16[2,9,32,128]{3,2,1,0:T(8,128)(2,1)S(1)} %shard_map.77.own), channel_id=1, source_target_pairs={{4,8},{8,4},{12,16},{16,12},{20,24},{24,20},{28,0},{0,28},{5,9},{9... | collective-permute-start | bytes 442376 | tf_op jit(solution)/shard_map/ppermute | solution.py:313

commit v3 on v2

--- a/solution.py
+++ b/solution.py
@@ -131,7 +131,7 @@
     return (at == 0) | (at == lax.axis_size("gx") - 1)
 
 
-def strip_kernel(far_row, mate, msgs, olds, send_l, send_r, strips):
+def strip_kernel(far_row, mate, msgs, olds, send_1, send_2, strips):
     inline = msgs.shape[0]
     depth = mate.shape[0] - 2
     odd = lax.axis_index("gx") % 2
@@ -143,10 +143,14 @@
     strips[pl.ds(1, inline)] = olds[...]
     strips[near] = mate[depth + 1]
     strips[far] = jnp.where(outside, zero, far_row[1])
-    for send, half in ((send_l, pl.ds(0, 128)), (send_r, pl.ds(128, 128))):
-        send[pl.ds(1, inline)] = msgs[:, :, half]
-        send[near] = near_msg[:, half.start : half.start + 128]
-        send[far] = far_msg[:, half.start : half.start + 128]
+    for send, right in ((send_1, odd == 0), (send_2, odd == 1)):
+
+        def pick(v):
+            return jnp.where(right, v[..., 128:], v[..., :128])
+
+        send[pl.ds(1, inline)] = pick(msgs[...])
+        send[near] = pick(near_msg)
+        send[far] = pick(far_msg)
 
 
 def fine_pair(own, halo, halo_first, outside, a1, bias, evens, pooled, pad, acc):
@@ -182,7 +186,7 @@
     fine_pair(own, mate, lax.axis_index("gx") % 2, None, a1, bias, evens, pooled, pad, acc)
 
 
-def late_kernel(own, halo, strips, got_l, got_r, early, a1, a1s, bias, evens, message, pad, acc, rows, late):
+def late_kernel(own, halo, strips, got_1, got_2, early, a1, a1s, bias, evens, message, pad, acc, rows, late):
     tall, chans, _ = strips.shape
     half_depth = early.shape[0]
     odd = lax.axis_index("gx") % 2
@@ -191,8 +195,9 @@
     message[odd, pl.ds(0, half_depth)] = late[...]
     at, end = lax.axis_index("gy"), lax.axis_size("gy") - 1
     part = lanes((tall * chans, 128)) % G
-    from_l = jnp.where(at == 0, 0.0, got_l[...].reshape(tall * chans, 128))
-    from_r = jnp.where(at == end, 0.0, got_r[...].reshape(tall * chans, 128))
+    one, two = got_1[...].reshape(tall * chans, 128), got_2[...].reshape(tall * chans, 128)
+    from_l = jnp.where(at == 0, 0.0, jnp.where(odd == 0, one, two))
+    from_r = jnp.where(at == end, 0.0, jnp.where(odd == 0, two, one))
     s = strips[...].reshape(tall * chans, 256)
     rows[:, :128] = jnp.where(part < 5, from_l, s[:, :128]).astype(BF)
     rows[:, 128:] = jnp.where(part < 3, s[:, 128:], from_r).astype(BF)
@@ -304,18 +309,35 @@
         out[:, xo] = wide[xo].reshape(c2, depth, half).astype(BF)
 
 
-def swap(value, parity):
-    count = lax.axis_size("gx")
+def permute(value, target):
+    wide, deep = lax.axis_size("gx"), lax.axis_size("gy")
     pairs = []
-    for i in range(parity, count, 2):
-        j = (i + 1) % count
-        pairs += [(i, j), (j, i)]
-    return lax.ppermute(value, "gx", pairs)
-
-
-def shift(value, by):
-    count = lax.axis_size("gy")
-    return lax.ppermute(value, "gy", [(i, (i + by) % count) for i in range(count)])
+    for x in range(wide):
+        for y in range(deep):
+            tx, ty = target(x, y, wide, deep)
+            pairs.append((x * deep + y, tx * deep + ty))
+    return lax.ppermute(value, ("gx", "gy"), pairs)
+
+
+def mate_of(x, y, wide, deep):
+    return x ^ 1, y
+
+
+def far_of(x, y, wide, deep):
+    to = x + 1 if x % 2 else x - 1
+    if 0 <= to < wide:
+        return to, y
+    if deep % 2 == 0:
+        return x, y ^ 1
+    return to % wide, y
+
+
+def loop_of(up):
+    def target(x, y, wide, deep):
+        to = y + 1 if (x % 2 == 0) == up else y - 1
+        return (x, to) if 0 <= to < deep else (x ^ 1, y)
+
+    return target
 
 
 def per_device(image, w_first, b_first, w_second, b_second, w_third, b_third):
@@ -337,9 +359,9 @@
         scratch=[pltpu.VMEM((c1 * depth, 128), F32)] * 2,
         flops=1 << 28,
     )(image)
-    got_small = swap(far_small, 1)
-    got_far = swap(far_row, 1)
-    got_row = swap(near_row, 0)
+    got_small = permute(far_small, far_of)
+    got_far = permute(far_row, far_of)
+    got_row = permute(near_row, mate_of)
     a1, a1s, a2, a3, b1, b2, b3, evens, ends = call(
         weights_kernel,
         [
@@ -364,19 +386,19 @@
     )
     fine = [pltpu.VMEM(((depth + 2) * k1, cross), BF), pltpu.VMEM((hz * c1, cross), BF)]
     (early,) = call(early_kernel, [((hz, c1, half), BF)], scratch=fine, flops=1 << 29)(own, got_row, a1, b1, evens)
-    send_l, send_r, strips = call(
+    send_1, send_2, strips = call(
         strip_kernel, [((tall, c1, 128), BF)] * 2 + [((tall, c1, 256), BF)], flops=1 << 20
     )(got_small, got_row, msgs, olds)
-    got_l = shift(send_r, 1)
-    got_r = shift(send_l, -1)
+    got_1 = permute(send_1, loop_of(True))
+    got_2 = permute(send_2, loop_of(False))
     (message,) = call(
         late_kernel,
         [((coarse, hz + 1, c1, half), BF)],
         scratch=fine + [pltpu.VMEM((tall * c1, 256), BF), pltpu.VMEM((hz, c1, half), BF)],
         flops=1 << 29,
-    )(own, got_far, strips, got_l, got_r, early, a1, a1s, b1, evens)
-    got_pa = swap(message, 0)
-    got_pb = swap(message, 1)
+    )(own, got_far, strips, got_1, got_2, early, a1, a1s, b1, evens)
+    got_pa = permute(message, mate_of)
+    got_pb = permute(message, far_of)
     mid = [pltpu.VMEM(((hz + 2) * k1, 256), BF), pltpu.VMEM((k1, half), BF)]
     (second,) = call(
         coarse_early_kernel, [((hz, 2, c2, 256), BF)], scratch=mid, flops=1 << 29

time: 31.5 us -> 29.7 us (0.943)
  the two profiles are of different devices: /device:TPU:0 before, /device:TPU:3 now
where the time goes in v3:
time: 29.7 us; the launch traced here: 29.6 us
  Pallas kernels  10.1 us (34%)
  waiting for transfers between devices  9.17 us (31%)
  starting transfers between devices  8.36 us (28%)
  local copies, waits for them, and re-layouts  1.89 us (6%)
    pallas_call x7, Pallas kernels, run(): pl.pallas_call(body, out_shape=[jax.ShapeDtypeStruct(s, d) for s, d in ou...  10.1 us
    ppermute x7, waiting for transfers between devices, permute(): return lax.ppermute(value, ('gx', 'gy'), pairs)  9.17 us
    ppermute x7, starting transfers between devices, permute(): return lax.ppermute(value, ('gx', 'gy'), pairs)  8.36 us
    unnamed x14, local copies, waits for them, and re-layouts  1.89 us
  transfers between devices with their start and end apart: 7, of which 3 were waited for; matrix products, arithmetic and copies ran while one was open for 0% of the time, Pallas kernels for 12%

profile of v3, /device:TPU:3, one launch (start us, length us, event | category | flops | bytes accessed | tf_op | source)
XLA Modules:
  0.0 29.6 jit_solution(8912197788917753897)
XLA Ops:
  0.0 1.2 %copy-done = bf16[32,4,16,256]{3,2,1,0:T(8,128)(2,1)S(1)} copy-done((bf16[32,4,16,256]{3,2,1,0:T(8,128)(2,1)S(1)}, bf16[32,4,16,256]{3,2,1,0:T(8,128)(2,1)}, u32[]{:S(2)}) %copy-start) | copy-done | bytes 1048600
  1.2 1.1 %shard_map.73 = (bf16[16,4,32,256]{3,2,1,0:T(8,128)(2,1)S(1)}, bf16[18,32,256]{2,1,0:T(8,128)(2,1)S(1)}, bf16[16,32,256]{2,1,0:T(8,128)(2,1)S(1)}, bf16[2,32,256...) custom-call(bf16[32,4,16,256]{3,2,1,0:T(8,128)(2,1)S(1)} %copy-done), custom_call_target="tpu_custom_call" | custom-call | flops 268435456 | bytes 1048576 | tf_op jit(solution)/shard_map/pallas_call | solution.py:17
  2.4 0.7 %collective-permute-start.2 = (bf16[18,32,256]{2,1,0:T(8,128)(2,1)S(1)}, bf16[18,32,256]{2,1,0:T(8,128)(2,1)S(1)}, u32[]{:S(2)}, u32[]{:S(2)}) collective-permute-start(bf16[18,32,256]{2,1,0:T(8,128)(2,1)S(1)} %get-tuple-element.26), channel_id=1, source_target_pairs={{0,4},{1,5},{2,6},{3,7},{4,0},{5,1},{6,2},{7,3},{8,12},{9,13},{10,... | collective-permute-start | bytes 884744 | tf_op jit(solution)/shard_map/ppermute | solution.py:319
  3.1 1.2 %collective-permute-start = (bf16[16,32,256]{2,1,0:T(8,128)(2,1)S(1)}, bf16[16,32,256]{2,1,0:T(8,128)(2,1)S(1)}, u32[]{:S(2)}, u32[]{:S(2)}) collective-permute-start(bf16[16,32,256]{2,1,0:T(8,128)(2,1)S(1)} %get-tuple-element.24), channel_id=1, source_target_pairs={{0,1},{1,0},{2,3},{3,2},{4,8},{5,9},{6,10},{7,11},{8,4},{9,5},{10,... | collective-permute-start | bytes 786440 | tf_op jit(solution)/shard_map/ppermute | solution.py:319
  4.3 1.5 %collective-permute-start.1 = (bf16[2,32,256]{2,1,0:T(8,128)(2,1)S(1)}, bf16[2,32,256]{2,1,0:T(8,128)(2,1)S(1)}, u32[]{:S(2)}, u32[]{:S(2)}) collective-permute-start(bf16[2,32,256]{2,1,0:T(8,128)(2,1)S(1)} %get-tuple-element.25), channel_id=1, source_target_pairs={{0,1},{1,0},{2,3},{3,2},{4,8},{5,9},{6,10},{7,11},{8,4},{9,5},{10,... | collective-permute-start | bytes 98312 | tf_op jit(solution)/shard_map/ppermute | solution.py:319
  5.8 0.6 %copy-done.4 = f32[32]{0:T(128)S(1)} copy-done((f32[32]{0:T(128)S(1)}, f32[32]{0:T(128)}, u32[]{:S(2)}) %copy-start.4) | copy-done | bytes 152
  6.4 0.0 copy-done.5
  6.4 0.0 copy-done.6
  6.5 0.7 %shard_map.75 = (bf16[192,384]{1,0:T(8,128)(2,1)S(1)}, bf16[576,128]{1,0:T(8,128)(2,1)S(1)}, bf16[384,384]{1,0:T(8,128)(2,1)S(1)}, bf16[384,768]{1,0:T(8,128)(2,...) custom-call(bf16[3,3,3,32,32]{4,3,2,1,0:T(8,128)(2,1)S(1)} %bitcast., ...), custom_call_target="tpu_custom_call" | custom-call | flops 268435456 | bytes 1048576 | tf_op jit(solution)/shard_map/pallas_call | solution.py:17
  7.2 5.6 %collective-permute-done.1.far_row = bf16[2,32,256]{2,1,0:T(8,128)(2,1)S(1)} collective-permute-done((bf16[2,32,256]{2,1,0:T(8,128)(2,1)S(1)}, bf16[2,32,256]{2,1,0:T(8,128)(2,1)S(1)}, u32[]{:S(2)}, u32[]{:S(2)}) %collective-permute-start.1) | collective-permute-done | bytes 32800 | tf_op jit(solution)/shard_map/ppermute | solution.py:319
  12.8 0.0 collective-permute-done.2.mate
  12.8 0.0 collective-permute-start.3
  12.8 1.5 %collective-permute-start.4 = (bf16[6,32,128]{2,1,0:T(8,128)(2,1)S(1)}, bf16[6,32,128]{2,1,0:T(8,128)(2,1)S(1)}, u32[]{:S(2)}, u32[]{:S(2)}) collective-permute-start(bf16[6,32,128]{2,1,0:T(8,128)(2,1)S(1)} %get-tuple-element.31), channel_id=1, source_target_pairs={{0,4},{1,0},{2,1},{3,2},{4,5},{5,6},{6,7},{7,3},{8,12},{9,8},{10,9... | collective-permute-start | bytes 147464 | tf_op jit(solution)/shard_map/ppermute | solution.py:319
  14.3 1.4 %shard_map.76.early = bf16[8,32,128]{2,1,0:T(8,128)(2,1)S(1)} custom-call(bf16[16,4,32,256]{3,2,1,0:T(8,128)(2,1)S(1)} %get-tuple-element.23.own, bf16[18,32,256]{2,1,0:T(8,128)(2,1)S(1)} %collective-permute-done.2.mate, bf16[192,384]{1,0:T(8,128)(2,1)S(1)} %get-tuple-element.32.a1, f32[32,256]{1,0:T(8,128)S(1)} %get-tuple-element.33.bias, ...), custom_call_target="tpu_custom_call" | custom-call | flops 536870912 | bytes 1048576 | tf_op jit(solution)/shard_map/pallas_call | solution.py:17
  15.7 0.0 collective-permute-done.halo
  15.7 0.8 %collective-permute-done.3.got_1 = bf16[6,32,128]{2,1,0:T(8,128)(2,1)S(1)} collective-permute-done((bf16[6,32,128]{2,1,0:T(8,128)(2,1)S(1)}, bf16[6,32,128]{2,1,0:T(8,128)(2,1)S(1)}, u32[]{:S(2)}, u32[]{:S(2)}) %collective-permute-start.3) | collective-permute-done | bytes 49184 | tf_op jit(solution)/shard_map/ppermute | solution.py:319
  16.5 0.0 collective-permute-done.4.got_2
  16.5 1.9 %shard_map.77.own = bf16[2,9,32,128]{3,2,1,0:T(8,128)(2,1)S(1)} custom-call(bf16[16,4,32,256]{3,2,1,0:T(8,128)(2,1)S(1)} %get-tuple-element.23.own, bf16[16,32,256]{2,1,0:T(8,128)(2,1)S(1)} %collective-permute-done.halo, bf16[6,32,256]{2,1,0:T(8,128)(2,1)S(1)} %get-tuple-element.29.strips, bf16[6,32,128]{2,1,0:T(8,128)(2,1)S(1)} %collective-permute-done.3.got_1, ...), custom_call_target="tpu_custom_call" | custom-call | flops 536870912 | bytes 1048576 | tf_op jit(solution)/shard_map/pallas_call | solution.py:17
  18.4 0.5 %collective-permute-start.6 = (bf16[2,9,32,128]{3,2,1,0:T(8,128)(2,1)S(1)}, bf16[2,9,32,128]{3,2,1,0:T(8,128)(2,1)S(1)}, u32[]{:S(2)}, u32[]{:S(2)}) collective-permute-start(bf16[2,9,32,128]{3,2,1,0:T(8,128)(2,1)S(1)} %shard_map.77.own), channel_id=1, source_target_pairs={{0,4},{1,5},{2,6},{3,7},{4,0},{5,1},{6,2},{7,3},{8,12},{9,13},{10,... | collective-permute-start | bytes 442376 | tf_op jit(solution)/shard_map/ppermute | solution.py:319
  18.9 3.0 %collective-permute-start.5 = (bf16[2,9,32,128]{3,2,1,0:T(8,128)(2,1)S(1)}, bf16[2,9,32,128]{3,2,1,0:T(8,128)(2,1)S(1)}, u32[]{:S(2)}, u32[]{:S(2)}) collective-permute-start(bf16[2,9,32,128]{3,2,1,0:T(8,128)(2,1)S(1)} %shard_map.77.own), channel_id=1, source_target_pairs={{0,1},{1,0},{2,3},{3,2},{4,8},{5,9},{6,10},{7,11},{8,4},{9,5},{10,... | collective-permute-start | bytes 442376 | tf_op jit(solution)/shard_map/ppermute | solution.py:319
  21.9 0.0 collective-permute-done.6.mate
  21.9 1.5 %shard_map.78.second = bf16[8,2,64,256]{3,2,1,0:T(8,128)(2,1)S(1)} custom-call(bf16[2,9,32,128]{3,2,1,0:T(8,128)(2,1)S(1)} %shard_map.77.own, bf16[2,9,32,128]{3,2,1,0:T(8,128)(2,1)S(1)} %collective-permute-done.6.mate, bf16[384,384]{1,0:T(8,128)(2,1)S(1)} %get-tuple-element.36.a2, f32[64,256]{1,0:T(8,128)S(1)} %get-tuple-element.37.bias.b2, ...), custom_call_target="tpu_custom_call" | custom-call | flops 536870912 | bytes 1048576 | tf_op jit(solution)/shard_map/pallas_call | solution.py:17
  23.3 2.7 %collective-permute-done.5.far = bf16[2,9,32,128]{3,2,1,0:T(8,128)(2,1)S(1)} collective-permute-done((bf16[2,9,32,128]{3,2,1,0:T(8,128)(2,1)S(1)}, bf16[2,9,32,128]{3,2,1,0:T(8,128)(2,1)S(1)}, u32[]{:S(2)}, u32[]{:S(2)}) %collective-permute-start.5) | collective-permute-done | bytes 147488 | tf_op jit(solution)/shard_map/ppermute | solution.py:319
  26.1 3.5 %shard_map.79 = bf16[64,2,8,128]{3,2,1,0:T(8,128)(2,1)} custom-call(bf16[2,9,32,128]{3,2,1,0:T(8,128)(2,1)S(1)} %shard_map.77.own, bf16[2,9,32,128]{3,2,1,0:T(8,128)(2,1)S(1)} %collective-permute-done.5.far, bf16[8,2,64,256]{3,2,1,0:T(8,128)(2,1)S(1)} %shard_map.78.second, bf16[384,384]{1,0:T(8,128)(2,1)S(1)} %get-tuple-element.36.a2, ...), custom_call_target="tpu_custom_call" | custom-call | flops 536870912 | bytes 1048576 | tf_op jit(solution)/shard_map/pallas_call | solution.py:17
  (11 shorter events, 0.0 us)
Async XLA Ops:
  0.0 1.2 %copy-start = (bf16[32,4,16,256]{3,2,1,0:T(8,128)(2,1)S(1)}, bf16[32,4,16,256]{3,2,1,0:T(8,128)(2,1)}, u32[]{:S(2)}) copy-start(bf16[32,4,16,256]{3,2,1,0:T(8,128)(2,1)} %image.1) | copy-start | bytes 3145732
  1.2 4.6 %copy-start.1 = (bf16[64,64,3,3,3]{1,0,4,3,2:T(8,128)(2,1)S(1)}, bf16[64,64,3,3,3]{1,0,4,3,2:T(8,128)(2,1)}, u32[]{:S(2)}) copy-start(bf16[64,64,3,3,3]{1,0,4,3,2:T(8,128)(2,1)} %param.12) | copy-start | bytes 663556
  1.2 4.6 %copy-start.2 = (bf16[32,32,3,3,3]{1,0,4,3,2:T(8,128)(2,1)S(1)}, bf16[32,32,3,3,3]{1,0,4,3,2:T(8,128)(2,1)}, u32[]{:S(2)}) copy-start(bf16[32,32,3,3,3]{1,0,4,3,2:T(8,128)(2,1)} %param.8) | copy-start | bytes 165892
  1.2 4.6 %copy-start.3 = (bf16[64,32,3,3,3]{0,1,4,3,2:T(8,128)(2,1)S(1)}, bf16[64,32,3,3,3]{0,1,4,3,2:T(8,128)(2,1)}, u32[]{:S(2)}) copy-start(bf16[64,32,3,3,3]{0,1,4,3,2:T(8,128)(2,1)} %param.10) | copy-start | bytes 331780
  2.4 10.4 %collective-permute-start.2 = (bf16[18,32,256]{2,1,0:T(8,128)(2,1)S(1)}, bf16[18,32,256]{2,1,0:T(8,128)(2,1)S(1)}, u32[]{:S(2)}, u32[]{:S(2)}) collective-permute-start(bf16[18,32,256]{2,1,0:T(8,128)(2,1)S(1)} %get-tuple-element.26), channel_id=1, source_target_pairs={{0,4},{1,5},{2,6},{3,7},{4,0},{5,1},{6,2},{7,3},{8,12},{9,13},{10,... | collective-permute-start | bytes 884744 | tf_op jit(solution)/shard_map/ppermute | solution.py:319
  3.1 12.5 %collective-permute-start = (bf16[16,32,256]{2,1,0:T(8,128)(2,1)S(1)}, bf16[16,32,256]{2,1,0:T(8,128)(2,1)S(1)}, u32[]{:S(2)}, u32[]{:S(2)}) collective-permute-start(bf16[16,32,256]{2,1,0:T(8,128)(2,1)S(1)} %get-tuple-element.24), channel_id=1, source_target_pairs={{0,1},{1,0},{2,3},{3,2},{4,8},{5,9},{6,10},{7,11},{8,4},{9,5},{10,... | collective-permute-start | bytes 786440 | tf_op jit(solution)/shard_map/ppermute | solution.py:319
  4.3 8.5 %collective-permute-start.1 = (bf16[2,32,256]{2,1,0:T(8,128)(2,1)S(1)}, bf16[2,32,256]{2,1,0:T(8,128)(2,1)S(1)}, u32[]{:S(2)}, u32[]{:S(2)}) collective-permute-start(bf16[2,32,256]{2,1,0:T(8,128)(2,1)S(1)} %get-tuple-element.25), channel_id=1, source_target_pairs={{0,1},{1,0},{2,3},{3,2},{4,8},{5,9},{6,10},{7,11},{8,4},{9,5},{10,... | collective-permute-start | bytes 98312 | tf_op jit(solution)/shard_map/ppermute | solution.py:319
  5.8 0.7 %copy-start.4 = (f32[32]{0:T(128)S(1)}, f32[32]{0:T(128)}, u32[]{:S(2)}) copy-start(f32[32]{0:T(128)} %param.9) | copy-start | bytes 388
  5.8 0.7 %copy-start.5 = (f32[64]{0:T(128)S(1)}, f32[64]{0:T(128)}, u32[]{:S(2)}) copy-start(f32[64]{0:T(128)} %param.11) | copy-start | bytes 772
  5.8 0.7 %copy-start.6 = (f32[64]{0:T(128)S(1)}, f32[64]{0:T(128)}, u32[]{:S(2)}) copy-start(f32[64]{0:T(128)} %param.13) | copy-start | bytes 772
  12.8 3.7 %collective-permute-start.3 = (bf16[6,32,128]{2,1,0:T(8,128)(2,1)S(1)}, bf16[6,32,128]{2,1,0:T(8,128)(2,1)S(1)}, u32[]{:S(2)}, u32[]{:S(2)}) collective-permute-start(bf16[6,32,128]{2,1,0:T(8,128)(2,1)S(1)} %get-tuple-element.30), channel_id=1, source_target_pairs={{0,1},{1,2},{2,3},{3,7},{4,0},{5,4},{6,5},{7,6},{8,9},{9,10},{10,1... | collective-permute-start | bytes 147464 | tf_op jit(solution)/shard_map/ppermute | solution.py:319
  12.8 3.7 %collective-permute-start.4 = (bf16[6,32,128]{2,1,0:T(8,128)(2,1)S(1)}, bf16[6,32,128]{2,1,0:T(8,128)(2,1)S(1)}, u32[]{:S(2)}, u32[]{:S(2)}) collective-permute-start(bf16[6,32,128]{2,1,0:T(8,128)(2,1)S(1)} %get-tuple-element.31), channel_id=1, source_target_pairs={{0,4},{1,0},{2,1},{3,2},{4,5},{5,6},{6,7},{7,3},{8,12},{9,8},{10,9... | collective-permute-start | bytes 147464 | tf_op jit(solution)/shard_map/ppermute | solution.py:319
  18.4 3.5 %collective-permute-start.6 = (bf16[2,9,32,128]{3,2,1,0:T(8,128)(2,1)S(1)}, bf16[2,9,32,128]{3,2,1,0:T(8,128)(2,1)S(1)}, u32[]{:S(2)}, u32[]{:S(2)}) collective-permute-start(bf16[2,9,32,128]{3,2,1,0:T(8,128)(2,1)S(1)} %shard_map.77.own), channel_id=1, source_target_pairs={{0,4},{1,5},{2,6},{3,7},{4,0},{5,1},{6,2},{7,3},{8,12},{9,13},{10,... | collective-permute-start | bytes 442376 | tf_op jit(solution)/shard_map/ppermute | solution.py:319
  18.9 7.2 %collective-permute-start.5 = (bf16[2,9,32,128]{3,2,1,0:T(8,128)(2,1)S(1)}, bf16[2,9,32,128]{3,2,1,0:T(8,128)(2,1)S(1)}, u32[]{:S(2)}, u32[]{:S(2)}) collective-permute-start(bf16[2,9,32,128]{3,2,1,0:T(8,128)(2,1)S(1)} %shard_map.77.own), channel_id=1, source_target_pairs={{0,1},{1,0},{2,3},{3,2},{4,8},{5,9},{6,10},{7,11},{8,4},{9,5},{10,... | collective-permute-start | bytes 442376 | tf_op jit(solution)/shard_map/ppermute | solution.py:319

commit v4 on v3

--- a/solution.py
+++ b/solution.py
@@ -39,24 +39,34 @@
     return pltpu.roll(v, by % v.shape[-1], v.ndim - 1)
 
 
-def weights_kernel(w1, w2, w3, b1, b2, b3, a1, a1s, a2, a3, c1, c2, c3, evens, ends):
-    def band(pieces, first):
-        zero = jnp.zeros_like(pieces[0])
-        return jnp.concatenate([zero] + pieces if first else pieces + [zero], axis=1)
-
+def weights_kernel(w1, w2, w3, b1, b2, b3, a1, a1s, a1h, a2, a3, c1, c2, c3, evens, ends):
     n1, n2 = w1.shape[3], w3.shape[3]
+    zero1, zero3 = jnp.zeros((n1, n1), F32), jnp.zeros((n2, n2), F32)
+    zero2 = jnp.zeros((n2, n1), F32)
+    p1, p2, p3 = {}, {}, {}
     for e in range(3):
         for f in range(3):
-            p1 = [w1[a, e, f].astype(F32) for a in range(3)]
-            p2 = [w2[a, e, f].astype(F32).T for a in range(3)]
-            p3 = [w3[a, e, f].astype(F32) for a in range(3)]
-            for xo in range(2):
-                v1 = band(p1, xo).astype(BF)
-                k1 = v1.shape[1]
-                a1[pl.ds((xo * 3 + f) * n1, n1), pl.ds(e * k1, k1)] = v1
-                a1s[pl.ds(((xo * 3 + e) * 3 + f) * n1, n1), :] = v1
-                a2[pl.ds((xo * 3 + f) * n2, n2), pl.ds(e * k1, k1)] = band(p2, xo).astype(BF)
-                a3[pl.ds((xo * 3 + f) * n2, n2), pl.ds(e * 2 * k1, 2 * k1)] = band(p3, xo).astype(BF)
+            for a in range(-1, 4):
+                inside = 0 <= a < 3
+                p1[a, e, f] = w1[a, e, f].astype(F32) if inside else zero1
+                p2[a, e, f] = w2[a, e, f].astype(F32).T if inside else zero2
+                p3[a, e, f] = w3[a, e, f].astype(F32) if inside else zero3
+    join = lambda pieces: jnp.concatenate(pieces, axis=1).astype(BF)
+    for xo in range(2):
+        for f in range(3):
+            for e in range(3):
+                v = join([p1[xi - xo, e, f] for xi in range(4)])
+                a1[pl.ds((xo * 3 + f) * n1, n1), pl.ds(e * 4 * n1, 4 * n1)] = v
+                a1s[pl.ds(((xo * 3 + e) * 3 + f) * n1, n1), :] = v
+            for h in range(2):
+                row = [p2[2 * h + r - xo, e, f] for e in range(3) for r in range(2)]
+                a2[h, pl.ds((xo * 3 + f) * n2, n2), :] = join(row)
+                for e in range(3):
+                    spot = pl.ds((e * 3 + f) * 2 * n2, 2 * n2)
+                    a3[h, pl.ds(xo * n2, n2), spot] = join([p3[2 * h + r - xo, e, f] for r in range(2)])
+    for h in range(2):
+        for f in range(3):
+            a1h[h, pl.ds(f * n1, n1), :] = join([p1[2 * h, e, f] for e in range(3)])
     for b, c in ((b1, c1), (b2, c2), (b3, c3)):
         n = b.shape[1]
         eye = lax.broadcasted_iota(jnp.int32, (n, n), 0) == lax.broadcasted_iota(jnp.int32, (n, n), 1)
@@ -153,7 +163,17 @@
         send[far] = pick(far_msg)
 
 
-def fine_pair(own, halo, halo_first, outside, a1, bias, evens, pooled, pad, acc):
+def taps(g, rows):
+    return roll(g[:rows], 1) + g[rows : 2 * rows] + roll(g[2 * rows :], -1)
+
+
+def finish(z, m, bias, acc):
+    m = jnp.maximum(jnp.maximum(m, roll(m, -1)) + bias[...], 0.0)
+    rows = m.shape[0]
+    acc[pl.ds(z * rows, rows), :] = m.astype(BF)
+
+
+def fill(own, halo, halo_first, pad):
     depth, inline, chans, cross = own.shape
     width = inline * chans
     zero = jnp.zeros((width, cross), BF)
@@ -162,37 +182,71 @@
     first = 1 - halo_first
     for z in range(depth):
         base = (z + 1) * width
-        beyond = halo[z] if outside is None else jnp.where(outside, zero[:chans], halo[z])
+        beyond = zero[:chans] if halo is None else halo[z]
         pad[pl.ds(pl.multiple_of(base + (1 - halo_first) * (inline - 1) * chans, chans), chans), :] = beyond
         for r in range(inline - 1):
             pad[pl.ds(pl.multiple_of(base + (r + halo_first) * chans, chans), chans), :] = own[z, first + r]
 
+
+def layer_rows(z, a1, pad, width):
+    g = dot(a1[...], pad[pl.ds(z * width, 3 * width), :])
+    rows = g.shape[0] // 6
+    return [taps(g[xo * 3 * rows : (xo + 1) * 3 * rows], rows) for xo in range(2)]
+
+
+def early_kernel(own, mate, a1, bias, evens, pooled, sums, pad, rest, acc):
+    depth, inline, chans, _ = own.shape
+    width = inline * chans
+    odd = lax.axis_index("gx") % 2
+    fill(own, mate, odd, pad)
+    fill(own, None, 1 - odd, rest)
+
     def layer(z):
-        g = dot(a1[...], pad[pl.ds(z * width, 3 * width), :])
-        rows = []
-        for xo in range(2):
-            t = g[xo * 3 * chans : (xo + 1) * 3 * chans]
-            rows.append(roll(t[:chans], 1) + t[chans : 2 * chans] + roll(t[2 * chans :], -1))
+        rows = layer_rows(z, a1, pad, width)
         return jnp.maximum(rows[0], rows[1])
 
     for z in range(depth // 2):
-        m = jnp.maximum(layer(2 * z), layer(2 * z + 1))
-        m = jnp.maximum(jnp.maximum(m, roll(m, -1)) + bias[...], 0.0)
-        acc[pl.ds(z * chans, chans), :] = m.astype(BF)
+        finish(z, jnp.maximum(layer(2 * z), layer(2 * z + 1)), bias, acc)
     pooled[...] = dot(acc[...], evens[...]).astype(BF).reshape(pooled.shape)
-
-
-def early_kernel(own, mate, a1, bias, evens, pooled, pad, acc):
-    fine_pair(own, mate, lax.axis_index("gx") % 2, None, a1, bias, evens, pooled, pad, acc)
-
-
-def late_kernel(own, halo, strips, got_1, got_2, early, a1, a1s, bias, evens, message, pad, acc, rows, late):
+    for z in range(depth):
+        rows = layer_rows(z, a1, rest, width)
+        sums[z, 0] = rows[0]
+        sums[z, 1] = rows[1]
+
+
+def late_kernel(
+    sums, halo, early, strips, got_1, got_2, a1h, a1s, bias, evens, message, far_message, pad, acc, edges, rows
+):
+    depth, _, chans, cross = sums.shape
+    half_depth = depth // 2
+    odd = lax.axis_index("gx") % 2
+    outside = at_map_end()
+    edge_columns(strips, got_1, got_2, a1s, bias, edges, rows)
+    zero = jnp.zeros((chans, cross), BF)
+    pad[pl.ds(0, chans), :] = zero
+    pad[pl.ds((depth + 1) * chans, chans), :] = zero
+    for z in range(depth):
+        pad[pl.ds((z + 1) * chans, chans), :] = jnp.where(outside, zero, halo[z])
+
+    def layer(z):
+        g = dot(a1h[odd], pad[pl.ds(z * chans, 3 * chans), :])
+        return jnp.maximum(sums[z, odd] + taps(g, chans), sums[z, 1 - odd])
+
+    for z in range(half_depth):
+        finish(z, jnp.maximum(layer(2 * z), layer(2 * z + 1)), bias, acc)
+    late = dot(acc[...], evens[...]).astype(BF).reshape(early.shape)
+    message[odd, pl.ds(0, half_depth)] = late
+    message[1 - odd, pl.ds(0, half_depth)] = early[...]
+    message[0, half_depth] = edges[0]
+    message[1, half_depth] = edges[1]
+    far_message[pl.ds(0, half_depth)] = late
+    far_message[half_depth] = edges[0]
+    far_message[half_depth + 1] = edges[1]
+
+
+def edge_columns(strips, got_1, got_2, a1s, bias, edges, rows):
     tall, chans, _ = strips.shape
-    half_depth = early.shape[0]
-    odd = lax.axis_index("gx") % 2
-    message[1 - odd, pl.ds(0, half_depth)] = early[...]
-    fine_pair(own, halo, 1 - odd, at_map_end(), a1, bias, evens, late, pad, acc)
-    message[odd, pl.ds(0, half_depth)] = late[...]
+    odd = lax.axis_index("gx") % 2
     at, end = lax.axis_index("gy"), lax.axis_size("gy") - 1
     part = lanes((tall * chans, 128)) % G
     one, two = got_1[...].reshape(tall * chans, 128), got_2[...].reshape(tall * chans, 128)
@@ -228,84 +282,120 @@
             cell = lane % G
             outside = (cell < 5) & (at == 0) if side == 0 else (cell > 1) & (at == end)
             sides.append(jnp.where(outside, 0.0, best))
-        edges = jnp.where((lane // G) % 2 == 0, sides[0], roll(sides[1], G))
-        message[pair, half_depth] = edges.astype(BF)
-
-
-def coarse_pair(own, other, own_first, beyond, a2, bias, ends, outside_x, put, pad, edge):
-    coarse, tall, chans, half = own.shape
-    depth = tall - 1
-    c2 = bias.shape[0]
-    width = 2 * coarse * chans
-    at, end = lax.axis_index("gy"), lax.axis_size("gy") - 1
-    spots = [(1 - own_first) * coarse, own_first * coarse]
-    for source, spot in zip((own, other), spots):
-        for r in range(coarse):
-            value = source[r, depth]
-            if source is other and beyond is not None:
-                value = jnp.where(beyond, jnp.zeros_like(value), value)
-            edge[pl.ds(pl.multiple_of((spot + r) * chans, chans), chans), :] = value
+        edges[pair] = jnp.where((lane // G) % 2 == 0, sides[0], roll(sides[1], G)).astype(BF)
+
+
+def assemble(cells, columns, depth, ends, outside, pad, edge):
+    coarse = 2
+    width, half = edge.shape
+    chans = width // coarse
     zero = jnp.zeros((width, 256), BF)
     pad[pl.ds(0, width), :] = zero
     pad[pl.ds((depth + 1) * width, width), :] = zero
+
+    def hide(v):
+        return v if outside is None else jnp.where(outside, zero[:chans, :half], v)
+
+    for r in range(coarse):
+        edge[pl.ds(r * chans, chans), :] = hide(columns(r))
     lane = lanes((chans, half))
     inner = (lane > 0) & (lane < half - 1)
     for z in range(depth):
+        fixed = dot(edge[...], ends[pl.ds(half - 2 * G - 2 * G * z, half), :]).astype(BF)
         base = (z + 1) * width
-        fixed = dot(edge[...], ends[pl.ds(half - 2 * G - 2 * G * z, half), :]).astype(BF)
-        pad[pl.ds(base, width), :] = fixed
-        for source, spot in zip((own, other), spots):
-            for r in range(coarse):
-                where = pl.ds(pl.multiple_of(base + (spot + r) * chans, chans), chans)
-                use = inner if source is own or beyond is None else inner & ~beyond
-                pad[where, :half] = jnp.where(use, source[r, z], pad[where, :half])
-    col = lanes((c2, 256))
-    outside_y = ((col == 255) & (at == 0)) | ((col == half) & (at == end))
-    for z in range(depth):
-        g = dot(a2[...], pad[pl.ds(z * width, 3 * width), :])
+        pad[pl.ds(base, width), half:] = fixed[:, half:]
+        for r in range(coarse):
+            spot = pl.ds(base + r * chans, chans)
+            pad[spot, :half] = jnp.where(inner, hide(cells(r, z)), fixed[r * chans : (r + 1) * chans, :half])
+
+
+def keep(q, z, r, v):
+    rows = v.shape[0]
+    half = v.shape[1] // 2
+    for f in range(3):
+        s = v if f == 1 else roll(v, 1 - f)
+        s = s[:, :half].astype(BF)
+        q[pl.ds(((z * 3 + f) * 2 + r) * rows, rows), half:] = s
+        q[pl.ds((((z + 1) * 3 + f) * 2 + r) * rows, rows), :half] = s
+
+
+def clear(q, depth):
+    rows = q.shape[0] // (depth + 1)
+    half = q.shape[1] // 2
+    q[pl.ds(0, rows), :half] = jnp.zeros((rows, half), BF)
+    q[pl.ds(depth * rows, rows), half:] = jnp.zeros((rows, half), BF)
+
+
+def beyond_cross(c2, half):
+    at, end = lax.axis_index("gy"), lax.axis_size("gy") - 1
+    col = lanes((c2, 2 * half))
+    return ((col == 2 * half - 1) & (at == 0)) | ((col == half) & (at == end))
+
+
+def coarse_own_kernel(own, a2, ends, near, part2, pad, edge):
+    coarse, tall, chans, _ = own.shape
+    depth = tall - 1
+    odd = lax.axis_index("gx") % 2
+    width = coarse * chans
+    c2 = near.shape[2]
+    assemble(lambda r, z: own[r, z], lambda r: own[r, depth], depth, ends, None, pad, edge)
+    for z in range(depth):
+        window = pl.ds(z * width, 3 * width)
+        for half_of, into in ((odd, near), (1 - odd, part2)):
+            g = dot(a2[half_of], pad[window, :])
+            for xo in range(2):
+                into[z, xo] = taps(g[xo * 3 * c2 : (xo + 1) * 3 * c2], c2)
+
+
+def coarse_near_kernel(mate, near, a2, b2, a3, ends, part3, pad, edge, q):
+    coarse, tall, chans, half = mate.shape
+    depth = tall - 1
+    c2 = b2.shape[0]
+    odd = lax.axis_index("gx") % 2
+    width = coarse * chans
+    assemble(lambda r, z: mate[r, z], lambda r: mate[r, depth], depth, ends, None, pad, edge)
+    clear(q, depth)
+    hide = beyond_cross(c2, half)
+    for z in range(depth):
+        g = dot(a2[1 - odd], pad[pl.ds(z * width, 3 * width), :])
         for xo in range(2):
-            t = g[xo * 3 * c2 : (xo + 1) * 3 * c2]
-            v = roll(t[:c2], 1) + t[c2 : 2 * c2] + roll(t[2 * c2 :], -1)
-            v = jnp.maximum(v + bias[...], 0.0)
-            hide = outside_y if outside_x is None else outside_y | outside_x[xo]
-            put(z, xo, jnp.where(hide, 0.0, v).astype(BF))
-
-
-def coarse_early_kernel(own, mate, a2, bias, ends, second, pad, edge):
-    def put(z, xo, v):
-        second[z, xo] = v
-
-    coarse_pair(own, mate, 1 - lax.axis_index("gx") % 2, None, a2, bias, ends, None, put, pad, edge)
-
-
-def coarse_late_kernel(own, far, second, a2, b2, a3, b3, ends, out, pad, edge, pad3, wide):
-    depth, _, c2, _ = second.shape
-    half = out.shape[-1]
+            v = taps(g[xo * 3 * c2 : (xo + 1) * 3 * c2], c2) + near[z, xo]
+            v = jnp.maximum(v + b2[...], 0.0)
+            keep(q, z, xo, jnp.where(hide, 0.0, v))
+    rows = 6 * c2
+    for z in range(0, depth, 2):
+        part3[z // 2] = dot(a3[1 - odd], q[pl.ds(z * rows, 3 * rows), :])
+
+
+def coarse_far_kernel(first, far, part2, part3, a2, b2, a3, b3, ends, out, pad, edge, q, wide):
+    depth, chans, half = first.shape
+    coarse = out.shape[1]
+    c2 = b2.shape[0]
     odd = lax.axis_index("gx") % 2
     at, end = lax.axis_index("gx"), lax.axis_size("gx") - 1
-    width = 4 * c2
-    zero = jnp.zeros((width, 256), BF)
-    pad3[pl.ds(0, width), :] = zero
-    pad3[pl.ds((depth + 1) * width, width), :] = zero
-    for z in range(depth):
-        for r in range(2):
-            spot = (z + 1) * width + ((1 - odd) * 2 + r) * c2
-            pad3[pl.ds(pl.multiple_of(spot, c2), c2), :] = second[z, r]
-
-    def put(z, xo, v):
-        spot = (z + 1) * width + (odd * 2 + xo) * c2
-        pad3[pl.ds(pl.multiple_of(spot, c2), c2), :] = v
-
+    width = coarse * chans
+
+    def cells(r, z):
+        return jnp.where(odd == r, first[z], far[z])
+
+    assemble(cells, lambda r: far[depth + r], depth, ends, at_map_end(), pad, edge)
+    clear(q, depth)
     outside = [(odd == 0) & (at == 0), (odd == 1) & (at == end)]
-    coarse_pair(own, far, odd, at_map_end(), a2, b2, ends, outside, put, pad, edge)
-    for z in range(depth):
-        g = dot(a3[...], pad3[pl.ds(z * width, 3 * width), :])
+    hide = beyond_cross(c2, half)
+    for z in range(depth):
+        g = dot(a2[odd], pad[pl.ds(z * width, 3 * width), :])
         for xo in range(2):
-            t = g[xo * 3 * c2 : (xo + 1) * 3 * c2]
-            v = roll(t[:c2], 1) + t[c2 : 2 * c2] + roll(t[2 * c2 :], -1)
-            v = jnp.maximum(v + b3[...], 0.0)
+            v = taps(g[xo * 3 * c2 : (xo + 1) * 3 * c2], c2) + part2[z, xo]
+            v = jnp.maximum(v + b2[...], 0.0)
+            keep(q, z, xo, jnp.where(hide | outside[xo], 0.0, v))
+    rows = 6 * c2
+    for z in range(0, depth, 2):
+        g = dot(a3[odd], q[pl.ds(z * rows, 3 * rows), :]) + part3[z // 2]
+        for xo in range(2):
+            v = jnp.maximum(g[xo * c2 : (xo + 1) * c2] + b3[...], 0.0)
             wide[xo, pl.ds(z, c2, stride=depth), :] = v[:, :half]
-    for xo in range(2):
+            wide[xo, pl.ds(z + 1, c2, stride=depth), :] = v[:, half:]
+    for xo in range(coarse):
         out[:, xo] = wide[xo].reshape(c2, depth, half).astype(BF)
 
 
@@ -362,13 +452,14 @@
     got_small = permute(far_small, far_of)
     got_far = permute(far_row, far_of)
     got_row = permute(near_row, mate_of)
-    a1, a1s, a2, a3, b1, b2, b3, evens, ends = call(
+    a1, a1s, a1h, a2, a3, b1, b2, b3, evens, ends = call(
         weights_kernel,
         [
             ((6 * c1, 3 * k1), BF),
             ((18 * c1, k1), BF),
-            ((6 * c2, 3 * k1), BF),
-            ((6 * c2, 12 * c2), BF),
+            ((2, 3 * c1, 3 * c1), BF),
+            ((2, 6 * c2, 6 * c1), BF),
+            ((2, 2 * c2, 18 * c2), BF),
             ((c1, 256), F32),
             ((c2, 256), F32),
             ((c2, 256), F32),
@@ -385,30 +476,43 @@
         b_third.reshape(1, c2),
     )
     fine = [pltpu.VMEM(((depth + 2) * k1, cross), BF), pltpu.VMEM((hz * c1, cross), BF)]
-    (early,) = call(early_kernel, [((hz, c1, half), BF)], scratch=fine, flops=1 << 29)(own, got_row, a1, b1, evens)
+    early, sums = call(
+        early_kernel, [((hz, c1, half), BF), ((depth, 2, c1, cross), F32)], scratch=fine[:1] + fine, flops=1 << 30
+    )(own, got_row, a1, b1, evens)
     send_1, send_2, strips = call(
         strip_kernel, [((tall, c1, 128), BF)] * 2 + [((tall, c1, 256), BF)], flops=1 << 20
     )(got_small, got_row, msgs, olds)
     got_1 = permute(send_1, loop_of(True))
     got_2 = permute(send_2, loop_of(False))
-    (message,) = call(
+    got_first = permute(early, far_of)
+    message, far_message = call(
         late_kernel,
-        [((coarse, hz + 1, c1, half), BF)],
-        scratch=fine + [pltpu.VMEM((tall * c1, 256), BF), pltpu.VMEM((hz, c1, half), BF)],
+        [((coarse, hz + 1, c1, half), BF), ((hz + 2, c1, half), BF)],
+        scratch=[
+            pltpu.VMEM(((depth + 2) * c1, cross), BF),
+            pltpu.VMEM((hz * c1, cross), BF),
+            pltpu.VMEM((coarse, c1, half), BF),
+            pltpu.VMEM((tall * c1, 256), BF),
+        ],
+        flops=1 << 28,
+    )(sums, got_far, early, strips, got_1, got_2, a1h, a1s, b1, evens)
+    got_pa = permute(message, mate_of)
+    got_pb = permute(far_message, far_of)
+    pad = pltpu.VMEM(((hz + 2) * 2 * c1, 256), BF)
+    edge = pltpu.VMEM((2 * c1, half), BF)
+    q = pltpu.VMEM(((hz + 1) * 6 * c2, 256), BF)
+    near, part2 = call(
+        coarse_own_kernel, [((hz, 2, c2, 256), F32)] * 2, scratch=[pad, edge], flops=1 << 29
+    )(message, a2, ends)
+    (part3,) = call(
+        coarse_near_kernel, [((hz // 2, 2 * c2, 256), F32)], scratch=[pad, edge, q], flops=1 << 29
+    )(got_pa, near, a2, b2, a3, ends)
+    (out,) = call(
+        coarse_far_kernel,
+        [((c2, coarse, hz, half), BF)],
+        scratch=[pad, edge, q, pltpu.VMEM((coarse, c2 * hz, half), F32)],
         flops=1 << 29,
-    )(own, got_far, strips, got_1, got_2, early, a1, a1s, b1, evens)
-    got_pa = permute(message, mate_of)
-    got_pb = permute(message, far_of)
-    mid = [pltpu.VMEM(((hz + 2) * k1, 256), BF), pltpu.VMEM((k1, half), BF)]
-    (second,) = call(
-        coarse_early_kernel, [((hz, 2, c2, 256), BF)], scratch=mid, flops=1 << 29
-    )(message, got_pa, a2, b2, ends)
-    (out,) = call(
-        coarse_late_kernel,
-        [((c2, coarse, hz, half), BF)],
-        scratch=mid + [pltpu.VMEM(((hz + 2) * 4 * c2, 256), BF), pltpu.VMEM((coarse, c2 * hz, half), F32)],
-        flops=1 << 29,
-    )(message, got_pb, second, a2, b2, a3, b3, ends)
+    )(got_first, got_pb, part2, part3, a2, b2, a3, b3, ends)
     return out
 
 

time: 29.7 us -> 28.4 us (0.956)
  waiting for transfers between devices: 9.17 us -> 7.21 us
  Pallas kernels: 10.1 us -> 10.6 us
    ppermute x7 -> x8, waiting for transfers between devices: 9.17 us -> 7.21 us  [permute(): return lax.ppermute(value, ('gx', 'gy'), pairs)]
    pallas_call x7 -> x8, Pallas kernels: 10.1 us -> 10.6 us  [run(): pl.pallas_call(body, out_shape=[jax.ShapeDtypeStruct(s, d) for s, d in ou...]
    ppermute x7 -> x8, starting transfers between devices: 8.36 us -> 8.37 us  [permute(): return lax.ppermute(value, ('gx', 'gy'), pairs)]
  transfers between devices with their start and end apart: 7 -> 8, of which waited for: 3 -> 2; matrix products, arithmetic and copies ran while one was open for 0% -> 0% of each run, Pallas kernels for 12% -> 21%
where the time goes in v4:
time: 28.4 us; the launch traced here: 28.2 us
  Pallas kernels  10.6 us (37%)
  starting transfers between devices  8.37 us (29%)
  waiting for transfers between devices  7.21 us (25%)
  local copies, waits for them, and re-layouts  1.89 us (7%)
    pallas_call x8, Pallas kernels, run(): pl.pallas_call(body, out_shape=[jax.ShapeDtypeStruct(s, d) for s, d in ou...  10.6 us
    ppermute x8, starting transfers between devices, permute(): return lax.ppermute(value, ('gx', 'gy'), pairs)  8.37 us
    ppermute x8, waiting for transfers between devices, permute(): return lax.ppermute(value, ('gx', 'gy'), pairs)  7.21 us
    unnamed x14, local copies, waits for them, and re-layouts  1.89 us
  transfers between devices with their start and end apart: 8, of which 2 were waited for; matrix products, arithmetic and copies ran while one was open for 0% of the time, Pallas kernels for 21%

profile of v4, /device:TPU:3, one launch (start us, length us, event | category | flops | bytes accessed | tf_op | source)
XLA Modules:
  0.0 28.2 jit_solution(4955653932305249888)
XLA Ops:
  0.0 1.2 %copy-done = bf16[32,4,16,256]{3,2,1,0:T(8,128)(2,1)S(1)} copy-done((bf16[32,4,16,256]{3,2,1,0:T(8,128)(2,1)S(1)}, bf16[32,4,16,256]{3,2,1,0:T(8,128)(2,1)}, u32[]{:S(2)}) %copy-start) | copy-done | bytes 1048600
  1.2 1.1 %shard_map.73 = (bf16[16,4,32,256]{3,2,1,0:T(8,128)(2,1)S(1)}, bf16[18,32,256]{2,1,0:T(8,128)(2,1)S(1)}, bf16[16,32,256]{2,1,0:T(8,128)(2,1)S(1)}, bf16[2,32,256...) custom-call(bf16[32,4,16,256]{3,2,1,0:T(8,128)(2,1)S(1)} %copy-done), custom_call_target="tpu_custom_call" | custom-call | flops 268435456 | bytes 1048576 | tf_op jit(solution)/shard_map/pallas_call | solution.py:17
  2.4 0.7 %collective-permute-start = (bf16[18,32,256]{2,1,0:T(8,128)(2,1)S(1)}, bf16[18,32,256]{2,1,0:T(8,128)(2,1)S(1)}, u32[]{:S(2)}, u32[]{:S(2)}) collective-permute-start(bf16[18,32,256]{2,1,0:T(8,128)(2,1)S(1)} %get-tuple-element.31), channel_id=1, source_target_pairs={{0,4},{1,5},{2,6},{3,7},{4,0},{5,1},{6,2},{7,3},{8,12},{9,13},{10,... | collective-permute-start | bytes 884744 | tf_op jit(solution)/shard_map/ppermute | solution.py:409
  3.1 1.2 %collective-permute-start.2 = (bf16[16,32,256]{2,1,0:T(8,128)(2,1)S(1)}, bf16[16,32,256]{2,1,0:T(8,128)(2,1)S(1)}, u32[]{:S(2)}, u32[]{:S(2)}) collective-permute-start(bf16[16,32,256]{2,1,0:T(8,128)(2,1)S(1)} %get-tuple-element.37), channel_id=1, source_target_pairs={{0,1},{1,0},{2,3},{3,2},{4,8},{5,9},{6,10},{7,11},{8,4},{9,5},{10,... | collective-permute-start | bytes 786440 | tf_op jit(solution)/shard_map/ppermute | solution.py:409
  4.3 1.5 %collective-permute-start.3 = (bf16[2,32,256]{2,1,0:T(8,128)(2,1)S(1)}, bf16[2,32,256]{2,1,0:T(8,128)(2,1)S(1)}, u32[]{:S(2)}, u32[]{:S(2)}) collective-permute-start(bf16[2,32,256]{2,1,0:T(8,128)(2,1)S(1)} %get-tuple-element.38), channel_id=1, source_target_pairs={{0,1},{1,0},{2,3},{3,2},{4,8},{5,9},{6,10},{7,11},{8,4},{9,5},{10,... | collective-permute-start | bytes 98312 | tf_op jit(solution)/shard_map/ppermute | solution.py:409
  5.8 0.6 %copy-done.4 = f32[32]{0:T(128)S(1)} copy-done((f32[32]{0:T(128)S(1)}, f32[32]{0:T(128)}, u32[]{:S(2)}) %copy-start.4) | copy-done | bytes 152
  6.4 0.0 copy-done.5
  6.4 0.0 copy-done.6
  6.5 0.7 %shard_map.74 = (bf16[192,384]{1,0:T(8,128)(2,1)S(1)}, bf16[576,128]{1,0:T(8,128)(2,1)S(1)}, bf16[2,96,96]{2,1,0:T(8,128)(2,1)S(1)}, bf16[2,384,192]{2,1,0:T(8,1...) custom-call(bf16[3,3,3,32,32]{4,3,2,1,0:T(8,128)(2,1)S(1)} %bitcast., ...), custom_call_target="tpu_custom_call" | custom-call | flops 268435456 | bytes 1048576 | tf_op jit(solution)/shard_map/pallas_call | solution.py:17
  7.1 5.6 %collective-permute-done.3.far_row = bf16[2,32,256]{2,1,0:T(8,128)(2,1)S(1)} collective-permute-done((bf16[2,32,256]{2,1,0:T(8,128)(2,1)S(1)}, bf16[2,32,256]{2,1,0:T(8,128)(2,1)S(1)}, u32[]{:S(2)}, u32[]{:S(2)}) %collective-permute-start.3) | collective-permute-done | bytes 32800 | tf_op jit(solution)/shard_map/ppermute | solution.py:409
  12.8 0.0 collective-permute-done.mate
  12.8 0.0 collective-permute-start.4
  12.8 1.5 %collective-permute-start.5 = (bf16[6,32,128]{2,1,0:T(8,128)(2,1)S(1)}, bf16[6,32,128]{2,1,0:T(8,128)(2,1)S(1)}, u32[]{:S(2)}, u32[]{:S(2)}) collective-permute-start(bf16[6,32,128]{2,1,0:T(8,128)(2,1)S(1)} %get-tuple-element.43), channel_id=1, source_target_pairs={{0,4},{1,0},{2,1},{3,2},{4,5},{5,6},{6,7},{7,3},{8,12},{9,8},{10,9... | collective-permute-start | bytes 147464 | tf_op jit(solution)/shard_map/ppermute | solution.py:409
  14.3 2.2 %shard_map.75 = (bf16[8,32,128]{2,1,0:T(8,128)(2,1)S(1)}, f32[16,2,32,256]{3,2,1,0:T(8,128)S(1)}) custom-call(bf16[16,4,32,256]{3,2,1,0:T(8,128)(2,1)S(1)} %get-tuple-element.30.own, bf16[18,32,256]{2,1,0:T(8,128)(2,1)S(1)} %collective-permute-done.mate, bf16[192,384]{1,0:T(8,128)(2,1)S(1)} %get-tuple-element.32.a1, f32[32,256]{1,0:T(8,128)S(1)} %get-tuple-element.33.bias, ...), custom_call_target="tpu_custom_call" | custom-call | flops 1073741824 | bytes 1048576 | tf_op jit(solution)/shard_map/pallas_call | solution.py:17
  16.5 0.0 collective-permute-done.2.halo
  16.6 0.0 collective-permute-done.4.got_1
  16.6 1.1 %shard_map.77 = (bf16[2,9,32,128]{3,2,1,0:T(8,128)(2,1)S(1)}, bf16[10,32,128]{2,1,0:T(8,128)(2,1)S(1)}) custom-call(f32[16,2,32,256]{3,2,1,0:T(8,128)S(1)} %get-tuple-element.36.sums, bf16[16,32,256]{2,1,0:T(8,128)(2,1)S(1)} %collective-permute-done.2.halo, bf16[8,32,128]{2,1,0:T(8,128)(2,1)S(1)} %get-tuple-element.35.early, ...), custom_call_target="tpu_custom_call" | custom-call | flops 268435456 | bytes 1048576 | tf_op jit(solution)/shard_map/pallas_call | solution.py:17
  17.7 0.5 %collective-permute-start.7 = (bf16[2,9,32,128]{3,2,1,0:T(8,128)(2,1)S(1)}, bf16[2,9,32,128]{3,2,1,0:T(8,128)(2,1)S(1)}, u32[]{:S(2)}, u32[]{:S(2)}) collective-permute-start(bf16[2,9,32,128]{3,2,1,0:T(8,128)(2,1)S(1)} %get-tuple-element.47.own), channel_id=1, source_target_pairs={{0,4},{1,5},{2,6},{3,7},{4,0},{5,1},{6,2},{7,3},{8,12},{9,13},{10,... | collective-permute-start | bytes 442376 | tf_op jit(solution)/shard_map/ppermute | solution.py:409
  18.1 3.0 %collective-permute-start.1 = (bf16[8,32,128]{2,1,0:T(8,128)(2,1)S(1)}, bf16[8,32,128]{2,1,0:T(8,128)(2,1)S(1)}, u32[]{:S(2)}, u32[]{:S(2)}) collective-permute-start(bf16[8,32,128]{2,1,0:T(8,128)(2,1)S(1)} %get-tuple-element.35.early), channel_id=1, source_target_pairs={{0,1},{1,0},{2,3},{3,2},{4,8},{5,9},{6,10},{7,11},{8,4},{9,5},{10,... | collective-permute-start | bytes 196616 | tf_op jit(solution)/shard_map/ppermute | solution.py:409
  21.1 0.1 collective-permute-start.6
  21.2 1.5 %shard_map.78 = (f32[8,2,64,256]{3,2,1,0:T(8,128)S(1)}, f32[8,2,64,256]{3,2,1,0:T(8,128)S(1)}) custom-call(bf16[2,9,32,128]{3,2,1,0:T(8,128)(2,1)S(1)} %get-tuple-element.47.own, bf16[2,384,192]{2,1,0:T(8,128)(2,1)S(1)} %get-tuple-element.48.a2, bf16[256,256]{1,0:T(8,128)(2,1)S(1)} %get-tuple-element.49.ends), custom_call_target="tpu_custom_call" | custom-call | flops 536870912 | bytes 1048576 | tf_op jit(solution)/shard_map/pallas_call | solution.py:17
  22.7 1.6 %shard_map.79.part3 = f32[4,128,256]{2,1,0:T(8,128)S(1)} custom-call(bf16[2,9,32,128]{3,2,1,0:T(8,128)(2,1)S(1)} %collective-permute-done.7.mate, f32[8,2,64,256]{3,2,1,0:T(8,128)S(1)} %get-tuple-element.51.near, bf16[2,384,192]{2,1,0:T(8,128)(2,1)S(1)} %get-tuple-element.48.a2, f32[64,256]{1,0:T(8,128)S(1)} %get-tuple-element.52.b2, ...), custom_call_target="tpu_custom_call" | custom-call | flops 536870912 | bytes 1048576 | tf_op jit(solution)/shard_map/pallas_call | solution.py:17
  24.3 1.6 %collective-permute-done.6.far = bf16[10,32,128]{2,1,0:T(8,128)(2,1)S(1)} collective-permute-done((bf16[10,32,128]{2,1,0:T(8,128)(2,1)S(1)}, bf16[10,32,128]{2,1,0:T(8,128)(2,1)S(1)}, u32[]{:S(2)}, u32[]{:S(2)}) %collective-permute-start.6) | collective-permute-done | bytes 81952 | tf_op jit(solution)/shard_map/ppermute | solution.py:409
  25.9 2.4 %shard_map.80 = bf16[64,2,8,128]{3,2,1,0:T(8,128)(2,1)} custom-call(bf16[8,32,128]{2,1,0:T(8,128)(2,1)S(1)} %collective-permute-done.1.first, bf16[10,32,128]{2,1,0:T(8,128)(2,1)S(1)} %collective-permute-done.6.far, f32[8,2,64,256]{3,2,1,0:T(8,128)S(1)} %get-tuple-element.50.part2, f32[4,128,256]{2,1,0:T(8,128)S(1)} %shard_map.79.part3, ...), custom_call_target="tpu_custom_call" | custom-call | flops 536870912 | bytes 1048576 | tf_op jit(solution)/shard_map/pallas_call | solution.py:17
  (14 shorter events, 0.1 us)
Async XLA Ops:
  0.0 1.2 %copy-start = (bf16[32,4,16,256]{3,2,1,0:T(8,128)(2,1)S(1)}, bf16[32,4,16,256]{3,2,1,0:T(8,128)(2,1)}, u32[]{:S(2)}) copy-start(bf16[32,4,16,256]{3,2,1,0:T(8,128)(2,1)} %image.1) | copy-start | bytes 3145732
  1.2 4.6 %copy-start.1 = (bf16[64,64,3,3,3]{1,0,4,3,2:T(8,128)(2,1)S(1)}, bf16[64,64,3,3,3]{1,0,4,3,2:T(8,128)(2,1)}, u32[]{:S(2)}) copy-start(bf16[64,64,3,3,3]{1,0,4,3,2:T(8,128)(2,1)} %param.12) | copy-start | bytes 663556
  1.2 4.6 %copy-start.2 = (bf16[32,32,3,3,3]{1,0,4,3,2:T(8,128)(2,1)S(1)}, bf16[32,32,3,3,3]{1,0,4,3,2:T(8,128)(2,1)}, u32[]{:S(2)}) copy-start(bf16[32,32,3,3,3]{1,0,4,3,2:T(8,128)(2,1)} %param.8) | copy-start | bytes 165892
  1.2 4.6 %copy-start.3 = (bf16[64,32,3,3,3]{0,1,4,3,2:T(8,128)(2,1)S(1)}, bf16[64,32,3,3,3]{0,1,4,3,2:T(8,128)(2,1)}, u32[]{:S(2)}) copy-start(bf16[64,32,3,3,3]{0,1,4,3,2:T(8,128)(2,1)} %param.10) | copy-start | bytes 331780
  2.4 10.4 %collective-permute-start = (bf16[18,32,256]{2,1,0:T(8,128)(2,1)S(1)}, bf16[18,32,256]{2,1,0:T(8,128)(2,1)S(1)}, u32[]{:S(2)}, u32[]{:S(2)}) collective-permute-start(bf16[18,32,256]{2,1,0:T(8,128)(2,1)S(1)} %get-tuple-element.31), channel_id=1, source_target_pairs={{0,4},{1,5},{2,6},{3,7},{4,0},{5,1},{6,2},{7,3},{8,12},{9,13},{10,... | collective-permute-start | bytes 884744 | tf_op jit(solution)/shard_map/ppermute | solution.py:409
  3.1 13.4 %collective-permute-start.2 = (bf16[16,32,256]{2,1,0:T(8,128)(2,1)S(1)}, bf16[16,32,256]{2,1,0:T(8,128)(2,1)S(1)}, u32[]{:S(2)}, u32[]{:S(2)}) collective-permute-start(bf16[16,32,256]{2,1,0:T(8,128)(2,1)S(1)} %get-tuple-element.37), channel_id=1, source_target_pairs={{0,1},{1,0},{2,3},{3,2},{4,8},{5,9},{6,10},{7,11},{8,4},{9,5},{10,... | collective-permute-start | bytes 786440 | tf_op jit(solution)/shard_map/ppermute | solution.py:409
  4.3 8.5 %collective-permute-start.3 = (bf16[2,32,256]{2,1,0:T(8,128)(2,1)S(1)}, bf16[2,32,256]{2,1,0:T(8,128)(2,1)S(1)}, u32[]{:S(2)}, u32[]{:S(2)}) collective-permute-start(bf16[2,32,256]{2,1,0:T(8,128)(2,1)S(1)} %get-tuple-element.38), channel_id=1, source_target_pairs={{0,1},{1,0},{2,3},{3,2},{4,8},{5,9},{6,10},{7,11},{8,4},{9,5},{10,... | collective-permute-start | bytes 98312 | tf_op jit(solution)/shard_map/ppermute | solution.py:409
  5.8 0.7 %copy-start.4 = (f32[32]{0:T(128)S(1)}, f32[32]{0:T(128)}, u32[]{:S(2)}) copy-start(f32[32]{0:T(128)} %param.9) | copy-start | bytes 388
  5.8 0.7 %copy-start.5 = (f32[64]{0:T(128)S(1)}, f32[64]{0:T(128)}, u32[]{:S(2)}) copy-start(f32[64]{0:T(128)} %param.11) | copy-start | bytes 772
  5.8 0.7 %copy-start.6 = (f32[64]{0:T(128)S(1)}, f32[64]{0:T(128)}, u32[]{:S(2)}) copy-start(f32[64]{0:T(128)} %param.13) | copy-start | bytes 772
  12.8 3.7 %collective-permute-start.4 = (bf16[6,32,128]{2,1,0:T(8,128)(2,1)S(1)}, bf16[6,32,128]{2,1,0:T(8,128)(2,1)S(1)}, u32[]{:S(2)}, u32[]{:S(2)}) collective-permute-start(bf16[6,32,128]{2,1,0:T(8,128)(2,1)S(1)} %get-tuple-element.42), channel_id=1, source_target_pairs={{0,1},{1,2},{2,3},{3,7},{4,0},{5,4},{6,5},{7,6},{8,9},{9,10},{10,1... | collective-permute-start | bytes 147464 | tf_op jit(solution)/shard_map/ppermute | solution.py:409
  12.8 3.7 %collective-permute-start.5 = (bf16[6,32,128]{2,1,0:T(8,128)(2,1)S(1)}, bf16[6,32,128]{2,1,0:T(8,128)(2,1)S(1)}, u32[]{:S(2)}, u32[]{:S(2)}) collective-permute-start(bf16[6,32,128]{2,1,0:T(8,128)(2,1)S(1)} %get-tuple-element.43), channel_id=1, source_target_pairs={{0,4},{1,0},{2,1},{3,2},{4,5},{5,6},{6,7},{7,3},{8,12},{9,8},{10,9... | collective-permute-start | bytes 147464 | tf_op jit(solution)/shard_map/ppermute | solution.py:409
  17.7 5.0 %collective-permute-start.7 = (bf16[2,9,32,128]{3,2,1,0:T(8,128)(2,1)S(1)}, bf16[2,9,32,128]{3,2,1,0:T(8,128)(2,1)S(1)}, u32[]{:S(2)}, u32[]{:S(2)}) collective-permute-start(bf16[2,9,32,128]{3,2,1,0:T(8,128)(2,1)S(1)} %get-tuple-element.47.own), channel_id=1, source_target_pairs={{0,4},{1,5},{2,6},{3,7},{4,0},{5,1},{6,2},{7,3},{8,12},{9,13},{10,... | collective-permute-start | bytes 442376 | tf_op jit(solution)/shard_map/ppermute | solution.py:409
  18.1 6.2 %collective-permute-start.1 = (bf16[8,32,128]{2,1,0:T(8,128)(2,1)S(1)}, bf16[8,32,128]{2,1,0:T(8,128)(2,1)S(1)}, u32[]{:S(2)}, u32[]{:S(2)}) collective-permute-start(bf16[8,32,128]{2,1,0:T(8,128)(2,1)S(1)} %get-tuple-element.35.early), channel_id=1, source_target_pairs={{0,1},{1,0},{2,3},{3,2},{4,8},{5,9},{6,10},{7,11},{8,4},{9,5},{10,... | collective-permute-start | bytes 196616 | tf_op jit(solution)/shard_map/ppermute | solution.py:409
  21.1 4.8 %collective-permute-start.6 = (bf16[10,32,128]{2,1,0:T(8,128)(2,1)S(1)}, bf16[10,32,128]{2,1,0:T(8,128)(2,1)S(1)}, u32[]{:S(2)}, u32[]{:S(2)}) collective-permute-start(bf16[10,32,128]{2,1,0:T(8,128)(2,1)S(1)} %get-tuple-element.46), channel_id=1, source_target_pairs={{0,1},{1,0},{2,3},{3,2},{4,8},{5,9},{6,10},{7,11},{8,4},{9,5},{10,... | collective-permute-start | bytes 245768 | tf_op jit(solution)/shard_map/ppermute | solution.py:409

commit v5 on v4

--- a/solution.py
+++ b/solution.py
@@ -12,15 +12,15 @@
 G = 8
 
 
-def call(body, outs, scratch=(), flops=0):
+def call(body, outs, scratch=(), flops=0, space=pltpu.VMEM, limit=16):
     def run(*args):
         return pl.pallas_call(
             body,
             out_shape=[jax.ShapeDtypeStruct(s, d) for s, d in outs],
-            in_specs=[VM] * len(args),
+            in_specs=[pl.BlockSpec(memory_space=space)] * len(args),
             out_specs=[VM] * len(outs),
             scratch_shapes=list(scratch),
-            compiler_params=pltpu.CompilerParams(vmem_limit_bytes=16 << 20),
+            compiler_params=pltpu.CompilerParams(vmem_limit_bytes=limit << 20),
             cost_estimate=pl.CostEstimate(flops=flops, bytes_accessed=1 << 20, transcendentals=0),
         )(*args)
 
@@ -59,12 +59,13 @@
                 a1[pl.ds((xo * 3 + f) * n1, n1), pl.ds(e * 4 * n1, 4 * n1)] = v
                 a1s[pl.ds(((xo * 3 + e) * 3 + f) * n1, n1), :] = v
             for h in range(2):
-                row = [p2[2 * h + r - xo, e, f] for e in range(3) for r in range(2)]
-                a2[h, pl.ds((xo * 3 + f) * n2, n2), :] = join(row)
                 for e in range(3):
                     spot = pl.ds((e * 3 + f) * 2 * n2, 2 * n2)
                     a3[h, pl.ds(xo * n2, n2), spot] = join([p3[2 * h + r - xo, e, f] for r in range(2)])
     for h in range(2):
+        for xo in range(2):
+            row = [p2[2 * h + r - xo, e, f] for e in range(3) for f in range(3) for r in range(2)]
+            a2[h, pl.ds(xo * n2, n2), :] = join(row)
         for f in range(3):
             a1h[h, pl.ds(f * n1, n1), :] = join([p1[2 * h, e, f] for e in range(3)])
     for b, c in ((b1, c1), (b2, c2), (b3, c3)):
@@ -113,27 +114,51 @@
     return msg_l, msg_r, own_l, own_r
 
 
-def pack_kernel(image, own, near_row, far_row, far_small, msgs, olds, lo, hi):
-    _, inline, depth, _ = image.shape
-    odd = lax.axis_index("gx") % 2
-    for x in range(inline):
+def row_kernel(image, local, far_row, far_small, lo, hi, sems):
+    inline = image.shape[1]
+    far = (inline - 1) * (lax.axis_index("gx") % 2)
+    copies = []
+    for k in range(inline):
+        x = (far + k) % inline
+        copies.append(pltpu.make_async_copy(image.at[:, x], local.at[x], sems.at[k]))
+        copies[k].start()
+    copies[0].wait()
+
+    def store(z, a, b):
+        far_row[z, :, :128] = a
+        far_row[z, :, 128:] = b
+
+    msg_l, msg_r, own_l, own_r = relayout(local[far], lo, hi, store)
+    far_small[0, :, :128] = msg_l
+    far_small[0, :, 128:] = msg_r
+    far_small[1, :, :128] = own_l
+    far_small[1, :, 128:] = own_r
+    for copy in copies[1:]:
+        copy.wait()
+
+
+def pack_kernel(local, far_row, far_small, own, near_row, msgs, olds, lo, hi):
+    inline, _, depth, _ = local.shape
+    odd = lax.axis_index("gx") % 2
+    near, far = (inline - 1) * (1 - odd), (inline - 1) * odd
+    own[:, far] = far_row[...]
+    msgs[far] = far_small[0]
+    olds[far] = far_small[1]
+    for k in range(1, inline):
+        x = (far + k) % inline
 
         def store(z, a, b):
             own[z, x, :, :128] = a
             own[z, x, :, 128:] = b
 
-        msg_l, msg_r, own_l, own_r = relayout(image[:, x], lo, hi, store)
+        msg_l, msg_r, own_l, own_r = relayout(local[x], lo.at[k - 1], hi.at[k - 1], store)
         msgs[x, :, :128] = msg_l
         msgs[x, :, 128:] = msg_r
         olds[x, :, :128] = own_l
         olds[x, :, 128:] = own_r
-    near, far = (inline - 1) * (1 - odd), (inline - 1) * odd
     near_row[pl.ds(0, depth)] = own[:, near]
     near_row[depth] = msgs[near]
     near_row[depth + 1] = olds[near]
-    far_row[...] = own[:, far]
-    far_small[0] = msgs[far]
-    far_small[1] = olds[far]
 
 
 def at_map_end():
@@ -285,28 +310,37 @@
         edges[pair] = jnp.where((lane // G) % 2 == 0, sides[0], roll(sides[1], G)).astype(BF)
 
 
-def assemble(cells, columns, depth, ends, outside, pad, edge):
+def assemble(cells, columns, depth, ends, outside, q2, eb):
     coarse = 2
-    width, half = edge.shape
-    chans = width // coarse
-    zero = jnp.zeros((width, 256), BF)
-    pad[pl.ds(0, width), :] = zero
-    pad[pl.ds((depth + 1) * width, width), :] = zero
+    half = eb.shape[1]
+    chans = q2.shape[0] // (depth + 1) // 6
+    width = coarse * chans
+    zero = jnp.zeros((chans, half), BF)
 
     def hide(v):
-        return v if outside is None else jnp.where(outside, zero[:chans, :half], v)
-
-    for r in range(coarse):
-        edge[pl.ds(r * chans, chans), :] = hide(columns(r))
+        return v if outside is None else jnp.where(outside, zero, v)
+
+    edge = jnp.concatenate([hide(columns(r)) for r in range(coarse)], axis=0)
+    flat = edge.astype(F32)
+    lane = lanes((width, half))
+    for e in range(3):
+        for f in range(3):
+            by = 2 * G * (e - 1) + 2 * (f - 1)
+            v = roll(flat, -by) if by else flat
+            if e == 0:
+                v = jnp.where(lane >= 2 * G, v, 0.0)
+            if e == 2:
+                v = jnp.where(lane < half - 2 * G, v, 0.0)
+            eb[pl.ds((e * 3 + f) * width, width), :] = v.astype(BF)
+    clear(q2, depth)
     lane = lanes((chans, half))
     inner = (lane > 0) & (lane < half - 1)
     for z in range(depth):
-        fixed = dot(edge[...], ends[pl.ds(half - 2 * G - 2 * G * z, half), :]).astype(BF)
-        base = (z + 1) * width
-        pad[pl.ds(base, width), half:] = fixed[:, half:]
+        fixed = dot(edge, ends[pl.ds(half - 2 * G - 2 * G * z, half), :])
         for r in range(coarse):
-            spot = pl.ds(base + r * chans, chans)
-            pad[spot, :half] = jnp.where(inner, hide(cells(r, z)), fixed[r * chans : (r + 1) * chans, :half])
+            own = fixed[r * chans : (r + 1) * chans]
+            main = jnp.where(inner, hide(cells(r, z)).astype(F32), own[:, :half])
+            keep(q2, z, r, jnp.concatenate([main, own[:, half:]], axis=1))
 
 
 def keep(q, z, r, v):
@@ -326,68 +360,72 @@
     q[pl.ds(depth * rows, rows), half:] = jnp.zeros((rows, half), BF)
 
 
-def beyond_cross(c2, half):
+def coarse_own_kernel(own, a2, ends, near, near_ends, part2, part2_ends, q2, eb):
+    _, tall, chans, _ = own.shape
+    depth = tall - 1
+    odd = lax.axis_index("gx") % 2
+    assemble(lambda r, z: own[r, z], lambda r: own[r, depth], depth, ends, None, q2, eb)
+    rows = 6 * chans
+    for part, into, into_ends in ((odd, near, near_ends), (1 - odd, part2, part2_ends)):
+        for z in range(0, depth, 2):
+            into[z // 2] = dot(a2[part], q2[pl.ds(z * rows, 3 * rows), :])
+        into_ends[...] = dot(a2[part], eb[...])
+
+
+def first_map(part, a2, b2, add, add_ends, outside, q2, eb, q, depth):
+    half = eb.shape[1]
+    c2 = b2.shape[0]
     at, end = lax.axis_index("gy"), lax.axis_size("gy") - 1
-    col = lanes((c2, 2 * half))
-    return ((col == 2 * half - 1) & (at == 0)) | ((col == half) & (at == end))
-
-
-def coarse_own_kernel(own, a2, ends, near, part2, pad, edge):
-    coarse, tall, chans, _ = own.shape
-    depth = tall - 1
-    odd = lax.axis_index("gx") % 2
-    width = coarse * chans
-    c2 = near.shape[2]
-    assemble(lambda r, z: own[r, z], lambda r: own[r, depth], depth, ends, None, pad, edge)
-    for z in range(depth):
-        window = pl.ds(z * width, 3 * width)
-        for half_of, into in ((odd, near), (1 - odd, part2)):
-            g = dot(a2[half_of], pad[window, :])
-            for xo in range(2):
-                into[z, xo] = taps(g[xo * 3 * c2 : (xo + 1) * 3 * c2], c2)
-
-
-def coarse_near_kernel(mate, near, a2, b2, a3, ends, part3, pad, edge, q):
-    coarse, tall, chans, half = mate.shape
+    rows = q2.shape[0] // (depth + 1)
+    lane = lanes((c2, half))
+    left = (lane % (2 * G)) < G
+    beyond = (left & (at == 0)) | (~left & (at == end))
+    clear(q, depth)
+    g = dot(a2[part], eb[...]) + add_ends[...]
+    ends = []
+    for xo in range(2):
+        v = jnp.maximum(g[xo * c2 : (xo + 1) * c2] + b2[:, :half], 0.0)
+        ends.append(jnp.where(beyond, 0.0, v))
+    for z in range(0, depth, 2):
+        g = dot(a2[part], q2[pl.ds(z * rows, 3 * rows), :]) + add[z // 2]
+        for xo in range(2):
+            v = jnp.maximum(g[xo * c2 : (xo + 1) * c2] + b2[...], 0.0)
+            for k in range(2):
+                spot = 2 * G * (z + k) + 3
+                right = roll(ends[xo], -(spot + G))
+                before = roll(ends[xo], half - 1 - spot)
+                side = jnp.where(lane == 0, right, before)
+                w = jnp.concatenate([v[:, k * half : (k + 1) * half], side], axis=1)
+                if outside is not None:
+                    w = jnp.where(outside[xo], 0.0, w)
+                keep(q, z + k, xo, w)
+
+
+def coarse_near_kernel(mate, near, near_ends, a2, b2, a3, ends, part3, q2, eb, q):
+    _, tall, _, _ = mate.shape
     depth = tall - 1
     c2 = b2.shape[0]
     odd = lax.axis_index("gx") % 2
-    width = coarse * chans
-    assemble(lambda r, z: mate[r, z], lambda r: mate[r, depth], depth, ends, None, pad, edge)
-    clear(q, depth)
-    hide = beyond_cross(c2, half)
-    for z in range(depth):
-        g = dot(a2[1 - odd], pad[pl.ds(z * width, 3 * width), :])
-        for xo in range(2):
-            v = taps(g[xo * 3 * c2 : (xo + 1) * 3 * c2], c2) + near[z, xo]
-            v = jnp.maximum(v + b2[...], 0.0)
-            keep(q, z, xo, jnp.where(hide, 0.0, v))
+    assemble(lambda r, z: mate[r, z], lambda r: mate[r, depth], depth, ends, None, q2, eb)
+    first_map(1 - odd, a2, b2, near, near_ends, None, q2, eb, q, depth)
     rows = 6 * c2
     for z in range(0, depth, 2):
         part3[z // 2] = dot(a3[1 - odd], q[pl.ds(z * rows, 3 * rows), :])
 
 
-def coarse_far_kernel(first, far, part2, part3, a2, b2, a3, b3, ends, out, pad, edge, q, wide):
-    depth, chans, half = first.shape
+def coarse_far_kernel(first, far, part2, part2_ends, part3, a2, b2, a3, b3, ends, out, q2, eb, q, wide):
+    depth, _, half = first.shape
     coarse = out.shape[1]
     c2 = b2.shape[0]
     odd = lax.axis_index("gx") % 2
     at, end = lax.axis_index("gx"), lax.axis_size("gx") - 1
-    width = coarse * chans
 
     def cells(r, z):
         return jnp.where(odd == r, first[z], far[z])
 
-    assemble(cells, lambda r: far[depth + r], depth, ends, at_map_end(), pad, edge)
-    clear(q, depth)
+    assemble(cells, lambda r: far[depth + r], depth, ends, at_map_end(), q2, eb)
     outside = [(odd == 0) & (at == 0), (odd == 1) & (at == end)]
-    hide = beyond_cross(c2, half)
-    for z in range(depth):
-        g = dot(a2[odd], pad[pl.ds(z * width, 3 * width), :])
-        for xo in range(2):
-            v = taps(g[xo * 3 * c2 : (xo + 1) * 3 * c2], c2) + part2[z, xo]
-            v = jnp.maximum(v + b2[...], 0.0)
-            keep(q, z, xo, jnp.where(hide | outside[xo], 0.0, v))
+    first_map(odd, a2, b2, part2, part2_ends, outside, q2, eb, q, depth)
     rows = 6 * c2
     for z in range(0, depth, 2):
         g = dot(a3[odd], q[pl.ds(z * rows, 3 * rows), :]) + part3[z // 2]
@@ -436,21 +474,27 @@
     half, hz, coarse = cross // 2, depth // 2, inline // 2
     k1 = 4 * c1
     tall = inline + 2
-    own, near_row, far_row, far_small, msgs, olds = call(
+    local, far_row, far_small = call(
+        row_kernel,
+        [((inline, c1, depth, cross), BF), ((depth, c1, cross), BF), ((2, c1, 256), BF)],
+        scratch=[pltpu.VMEM((c1 * depth, 128), F32)] * 2 + [pltpu.SemaphoreType.DMA((inline,))],
+        flops=1 << 20,
+        space=pltpu.MemorySpace.HBM,
+        limit=52,
+    )(image)
+    got_small = permute(far_small, far_of)
+    got_far = permute(far_row, far_of)
+    own, near_row, msgs, olds = call(
         pack_kernel,
         [
             ((depth, inline, c1, cross), BF),
             ((depth + 2, c1, cross), BF),
-            ((depth, c1, cross), BF),
-            ((2, c1, 256), BF),
             ((inline, c1, 256), BF),
             ((inline, c1, 256), BF),
         ],
-        scratch=[pltpu.VMEM((c1 * depth, 128), F32)] * 2,
+        scratch=[pltpu.VMEM((inline - 1, c1 * depth, 128), F32)] * 2,
         flops=1 << 28,
-    )(image)
-    got_small = permute(far_small, far_of)
-    got_far = permute(far_row, far_of)
+    )(local, far_row, far_small)
     got_row = permute(near_row, mate_of)
     a1, a1s, a1h, a2, a3, b1, b2, b3, evens, ends = call(
         weights_kernel,
@@ -458,7 +502,7 @@
             ((6 * c1, 3 * k1), BF),
             ((18 * c1, k1), BF),
             ((2, 3 * c1, 3 * c1), BF),
-            ((2, 6 * c2, 6 * c1), BF),
+            ((2, 2 * c2, 18 * c1), BF),
             ((2, 2 * c2, 18 * c2), BF),
             ((c1, 256), F32),
             ((c2, 256), F32),
@@ -498,21 +542,22 @@
     )(sums, got_far, early, strips, got_1, got_2, a1h, a1s, b1, evens)
     got_pa = permute(message, mate_of)
     got_pb = permute(far_message, far_of)
-    pad = pltpu.VMEM(((hz + 2) * 2 * c1, 256), BF)
-    edge = pltpu.VMEM((2 * c1, half), BF)
+    q2 = pltpu.VMEM(((hz + 1) * 6 * c1, 256), BF)
+    eb = pltpu.VMEM((18 * c1, half), BF)
     q = pltpu.VMEM(((hz + 1) * 6 * c2, 256), BF)
-    near, part2 = call(
-        coarse_own_kernel, [((hz, 2, c2, 256), F32)] * 2, scratch=[pad, edge], flops=1 << 29
+    sums2 = [((hz // 2, 2 * c2, 256), F32), ((2 * c2, half), F32)]
+    near, near_ends, part2, part2_ends = call(
+        coarse_own_kernel, sums2 * 2, scratch=[q2, eb], flops=1 << 29
     )(message, a2, ends)
     (part3,) = call(
-        coarse_near_kernel, [((hz // 2, 2 * c2, 256), F32)], scratch=[pad, edge, q], flops=1 << 29
-    )(got_pa, near, a2, b2, a3, ends)
+        coarse_near_kernel, [((hz // 2, 2 * c2, 256), F32)], scratch=[q2, eb, q], flops=1 << 29
+    )(got_pa, near, near_ends, a2, b2, a3, ends)
     (out,) = call(
         coarse_far_kernel,
         [((c2, coarse, hz, half), BF)],
-        scratch=[pad, edge, q, pltpu.VMEM((coarse, c2 * hz, half), F32)],
+        scratch=[q2, eb, q, pltpu.VMEM((coarse, c2 * hz, half), F32)],
         flops=1 << 29,
-    )(got_first, got_pb, part2, part3, a2, b2, a3, b3, ends)
+    )(got_first, got_pb, part2, part2_ends, part3, a2, b2, a3, b3, ends)
     return out
 
 

time: 28.4 us -> 28.1 us (0.989)
  local copies, waits for them, and re-layouts: 1.89 us -> 0.68 us
  waiting for transfers between devices: 7.21 us -> 8.04 us
    unnamed x14 -> x12, local copies, waits for them, and re-layouts: 1.89 us -> 0.68 us
    ppermute x8, waiting for transfers between devices: 7.21 us -> 8.04 us  [permute(): return lax.ppermute(value, ('gx', 'gy'), pairs)]
    pallas_call x8 -> x9, Pallas kernels: 10.6 us -> 10.7 us  [run(): pl.pallas_call(body, out_shape=[jax.ShapeDtypeStruct(s, d) for s, d in ou...]
  transfers between devices with their start and end apart: 8 -> 8, of which waited for: 2 -> 3; matrix products, arithmetic and copies ran while one was open for 0% -> 0% of each run, Pallas kernels for 21% -> 19%
where the time goes in v5:
time: 28.1 us; the launch traced here: 27.9 us
  Pallas kernels  10.7 us (38%)
  starting transfers between devices  8.33 us (30%)
  waiting for transfers between devices  8.04 us (29%)
  local copies, waits for them, and re-layouts  0.68 us (2%)
    pallas_call x9, Pallas kernels, run(): pl.pallas_call(body, out_shape=[jax.ShapeDtypeStruct(s, d) for s, d in ou...  10.7 us
    ppermute x8, starting transfers between devices, permute(): return lax.ppermute(value, ('gx', 'gy'), pairs)  8.33 us
    ppermute x8, waiting for transfers between devices, permute(): return lax.ppermute(value, ('gx', 'gy'), pairs)  8.04 us
    unnamed x12, local copies, waits for them, and re-layouts  0.68 us
  transfers between devices with their start and end apart: 8, of which 3 were waited for; matrix products, arithmetic and copies ran while one was open for 0% of the time, Pallas kernels for 19%

profile of v5, /device:TPU:3, one launch (start us, length us, event | category | flops | bytes accessed | tf_op | source)
XLA Modules:
  0.0 27.9 jit_solution(1085419786968353532)
XLA Ops:
  0.0 1.3 %shard_map.73 = (bf16[4,32,16,256]{3,2,1,0:T(8,128)(2,1)S(1)}, bf16[16,32,256]{2,1,0:T(8,128)(2,1)S(1)}, bf16[2,32,256]{2,1,0:T(8,128)(2,1)S(1)}) custom-call(bf16[32,4,16,256]{3,2,1,0:T(8,128)(2,1)} %image.1), custom_call_target="tpu_custom_call" | custom-call | flops 1048576 | bytes 1048576 | tf_op jit(solution)/shard_map/pallas_call | solution.py:17
  1.3 0.0 copy-start
  1.4 1.0 %shard_map.74 = (bf16[16,4,32,256]{3,2,1,0:T(8,128)(2,1)S(1)}, bf16[18,32,256]{2,1,0:T(8,128)(2,1)S(1)}, bf16[4,32,256]{2,1,0:T(8,128)(2,1)S(1)}, bf16[4,32,256]{2,1,0:T(8,128)(2,1)S(1)}) custom-call(bf16[4,32,16,256]{3,2,1,0:T(8,128)(2,1)S(1)} %get-tuple-element.33.local, bf16[16,32,256]{2,1,0:T(8,128)(2,1)S(1)} %get-tuple-element.34.far_row, ...), custom_call_target="tpu_custom_call" | custom-call | flops 268435456 | bytes 1048576 | tf_op jit(solution)/shard_map/pallas_call | solution.py:17
  2.3 0.7 %collective-permute-start = (bf16[18,32,256]{2,1,0:T(8,128)(2,1)S(1)}, bf16[18,32,256]{2,1,0:T(8,128)(2,1)S(1)}, u32[]{:S(2)}, u32[]{:S(2)}) collective-permute-start(bf16[18,32,256]{2,1,0:T(8,128)(2,1)S(1)} %get-tuple-element.37), channel_id=1, source_target_pairs={{0,4},{1,5},{2,6},{3,7},{4,0},{5,1},{6,2},{7,3},{8,12},{9,13},{10,... | collective-permute-start | bytes 884744 | tf_op jit(solution)/shard_map/ppermute | solution.py:447
  3.1 1.2 %collective-permute-start.2 = (bf16[16,32,256]{2,1,0:T(8,128)(2,1)S(1)}, bf16[16,32,256]{2,1,0:T(8,128)(2,1)S(1)}, u32[]{:S(2)}, u32[]{:S(2)}) collective-permute-start(bf16[16,32,256]{2,1,0:T(8,128)(2,1)S(1)} %get-tuple-element.34.far_row), channel_id=1, source_target_pairs={{0,1},{1,0},{2,3},{3,2},{4,8},{5,9},{6,10},{7,11},{8,4},{9,5},{10,... | collective-permute-start | bytes 786440 | tf_op jit(solution)/shard_map/ppermute | solution.py:447
  4.3 1.5 %collective-permute-start.3 = (bf16[2,32,256]{2,1,0:T(8,128)(2,1)S(1)}, bf16[2,32,256]{2,1,0:T(8,128)(2,1)S(1)}, u32[]{:S(2)}, u32[]{:S(2)}) collective-permute-start(bf16[2,32,256]{2,1,0:T(8,128)(2,1)S(1)} %get-tuple-element.35.far_small), channel_id=1, source_target_pairs={{0,1},{1,0},{2,3},{3,2},{4,8},{5,9},{6,10},{7,11},{8,4},{9,5},{10,... | collective-permute-start | bytes 98312 | tf_op jit(solution)/shard_map/ppermute | solution.py:447
  5.8 0.6 %copy-done.3 = f32[32]{0:T(128)S(1)} copy-done((f32[32]{0:T(128)S(1)}, f32[32]{0:T(128)}, u32[]{:S(2)}) %copy-start.3) | copy-done | bytes 152
  6.4 0.0 copy-done.4
  6.4 0.0 copy-done.5
  6.4 0.7 %shard_map.75 = (bf16[192,384]{1,0:T(8,128)(2,1)S(1)}, bf16[576,128]{1,0:T(8,128)(2,1)S(1)}, bf16[2,96,96]{2,1,0:T(8,128)(2,1)S(1)}, bf16[2,128,576]{2,1,0:T(8,1...) custom-call(bf16[3,3,3,32,32]{4,3,2,1,0:T(8,128)(2,1)S(1)} %bitcast., ...), custom_call_target="tpu_custom_call" | custom-call | flops 268435456 | bytes 1048576 | tf_op jit(solution)/shard_map/pallas_call | solution.py:17
  7.1 5.6 %collective-permute-done.3.far_row = bf16[2,32,256]{2,1,0:T(8,128)(2,1)S(1)} collective-permute-done((bf16[2,32,256]{2,1,0:T(8,128)(2,1)S(1)}, bf16[2,32,256]{2,1,0:T(8,128)(2,1)S(1)}, u32[]{:S(2)}, u32[]{:S(2)}) %collective-permute-start.3) | collective-permute-done | bytes 32800 | tf_op jit(solution)/shard_map/ppermute | solution.py:447
  12.8 0.0 collective-permute-start.4
  12.8 1.5 %collective-permute-start.5 = (bf16[6,32,128]{2,1,0:T(8,128)(2,1)S(1)}, bf16[6,32,128]{2,1,0:T(8,128)(2,1)S(1)}, u32[]{:S(2)}, u32[]{:S(2)}) collective-permute-start(bf16[6,32,128]{2,1,0:T(8,128)(2,1)S(1)} %get-tuple-element.47), channel_id=1, source_target_pairs={{0,4},{1,0},{2,1},{3,2},{4,5},{5,6},{6,7},{7,3},{8,12},{9,8},{10,9... | collective-permute-start | bytes 147464 | tf_op jit(solution)/shard_map/ppermute | solution.py:447
  14.3 2.3 %shard_map.76 = (bf16[8,32,128]{2,1,0:T(8,128)(2,1)S(1)}, f32[16,2,32,256]{3,2,1,0:T(8,128)S(1)}) custom-call(bf16[16,4,32,256]{3,2,1,0:T(8,128)(2,1)S(1)} %get-tuple-element.36.own, bf16[18,32,256]{2,1,0:T(8,128)(2,1)S(1)} %collective-permute-done.mate, bf16[192,384]{1,0:T(8,128)(2,1)S(1)} %get-tuple-element.38.a1, f32[32,256]{1,0:T(8,128)S(1)} %get-tuple-element.39.bias, ...), custom_call_target="tpu_custom_call" | custom-call | flops 1073741824 | bytes 1048576 | tf_op jit(solution)/shard_map/pallas_call | solution.py:17
  16.5 0.0 collective-permute-done.2.halo
  16.6 1.1 %shard_map.78 = (bf16[2,9,32,128]{3,2,1,0:T(8,128)(2,1)S(1)}, bf16[10,32,128]{2,1,0:T(8,128)(2,1)S(1)}) custom-call(f32[16,2,32,256]{3,2,1,0:T(8,128)S(1)} %get-tuple-element.42.sums, bf16[16,32,256]{2,1,0:T(8,128)(2,1)S(1)} %collective-permute-done.2.halo, bf16[8,32,128]{2,1,0:T(8,128)(2,1)S(1)} %get-tuple-element.41.early, ...), custom_call_target="tpu_custom_call" | custom-call | flops 268435456 | bytes 1048576 | tf_op jit(solution)/shard_map/pallas_call | solution.py:17
  17.7 0.4 %collective-permute-start.7 = (bf16[2,9,32,128]{3,2,1,0:T(8,128)(2,1)S(1)}, bf16[2,9,32,128]{3,2,1,0:T(8,128)(2,1)S(1)}, u32[]{:S(2)}, u32[]{:S(2)}) collective-permute-start(bf16[2,9,32,128]{3,2,1,0:T(8,128)(2,1)S(1)} %get-tuple-element.51.own), channel_id=1, source_target_pairs={{0,4},{1,5},{2,6},{3,7},{4,0},{5,1},{6,2},{7,3},{8,12},{9,13},{10,... | collective-permute-start | bytes 442376 | tf_op jit(solution)/shard_map/ppermute | solution.py:447
  18.1 3.0 %collective-permute-start.1 = (bf16[8,32,128]{2,1,0:T(8,128)(2,1)S(1)}, bf16[8,32,128]{2,1,0:T(8,128)(2,1)S(1)}, u32[]{:S(2)}, u32[]{:S(2)}) collective-permute-start(bf16[8,32,128]{2,1,0:T(8,128)(2,1)S(1)} %get-tuple-element.41.early), channel_id=1, source_target_pairs={{0,1},{1,0},{2,3},{3,2},{4,8},{5,9},{6,10},{7,11},{8,4},{9,5},{10,... | collective-permute-start | bytes 196616 | tf_op jit(solution)/shard_map/ppermute | solution.py:447
  21.1 0.1 collective-permute-start.6
  21.1 1.0 %shard_map.79 = (f32[4,128,256]{2,1,0:T(8,128)S(1)}, f32[128,128]{1,0:T(8,128)S(1)}, f32[4,128,256]{2,1,0:T(8,128)S(1)}, f32[128,128]{1,0:T(8,128)S(1)}) custom-call(bf16[2,9,32,128]{3,2,1,0:T(8,128)(2,1)S(1)} %get-tuple-element.51.own, bf16[2,128,576]{2,1,0:T(8,128)(2,1)S(1)} %get-tuple-element.52.a2, bf16[256,256]{1,0:T(8,128)(2,1)S(1)} %get-tuple-element.53.ends), custom_call_target="tpu_custom_call" | custom-call | flops 536870912 | bytes 1048576 | tf_op jit(solution)/shard_map/pallas_call | solution.py:17
  22.1 1.3 %shard_map.80.part3 = f32[4,128,256]{2,1,0:T(8,128)S(1)} custom-call(bf16[2,9,32,128]{3,2,1,0:T(8,128)(2,1)S(1)} %collective-permute-done.7.mate, f32[4,128,256]{2,1,0:T(8,128)S(1)} %get-tuple-element.56.near, f32[128,128]{1,0:T(8,128)S(1)} %get-tuple-element.57.near_ends, bf16[2,128,576]{2,1,0:T(8,128)(2,1)S(1)} %get-tuple-element.52.a2, ...), custom_call_target="tpu_custom_call" | custom-call | flops 536870912 | bytes 1048576 | tf_op jit(solution)/shard_map/pallas_call | solution.py:17
  23.4 0.1 collective-permute-done.1.first
  23.5 2.3 %collective-permute-done.6.far = bf16[10,32,128]{2,1,0:T(8,128)(2,1)S(1)} collective-permute-done((bf16[10,32,128]{2,1,0:T(8,128)(2,1)S(1)}, bf16[10,32,128]{2,1,0:T(8,128)(2,1)S(1)}, u32[]{:S(2)}, u32[]{:S(2)}) %collective-permute-start.6) | collective-permute-done | bytes 81952 | tf_op jit(solution)/shard_map/ppermute | solution.py:447
  25.8 2.1 %shard_map.81 = bf16[64,2,8,128]{3,2,1,0:T(8,128)(2,1)} custom-call(bf16[8,32,128]{2,1,0:T(8,128)(2,1)S(1)} %collective-permute-done.1.first, bf16[10,32,128]{2,1,0:T(8,128)(2,1)S(1)} %collective-permute-done.6.far, f32[4,128,256]{2,1,0:T(8,128)S(1)} %get-tuple-element.54.part2, f32[128,128]{1,0:T(8,128)S(1)} %get-tuple-element.55.part2_ends, ...), custom_call_target="tpu_custom_call" | custom-call | flops 536870912 | bytes 1048576 | tf_op jit(solution)/shard_map/pallas_call | solution.py:17
  (13 shorter events, 0.1 us)
Async XLA Ops:
  1.3 4.4 %copy-start = (bf16[64,64,3,3,3]{1,0,4,3,2:T(8,128)(2,1)S(1)}, bf16[64,64,3,3,3]{1,0,4,3,2:T(8,128)(2,1)}, u32[]{:S(2)}) copy-start(bf16[64,64,3,3,3]{1,0,4,3,2:T(8,128)(2,1)} %param.12) | copy-start | bytes 663556
  1.3 4.4 %copy-start.1 = (bf16[32,32,3,3,3]{1,0,4,3,2:T(8,128)(2,1)S(1)}, bf16[32,32,3,3,3]{1,0,4,3,2:T(8,128)(2,1)}, u32[]{:S(2)}) copy-start(bf16[32,32,3,3,3]{1,0,4,3,2:T(8,128)(2,1)} %param.8) | copy-start | bytes 165892
  1.4 4.4 %copy-start.2 = (bf16[64,32,3,3,3]{0,1,4,3,2:T(8,128)(2,1)S(1)}, bf16[64,32,3,3,3]{0,1,4,3,2:T(8,128)(2,1)}, u32[]{:S(2)}) copy-start(bf16[64,32,3,3,3]{0,1,4,3,2:T(8,128)(2,1)} %param.10) | copy-start | bytes 331780
  2.3 10.4 %collective-permute-start = (bf16[18,32,256]{2,1,0:T(8,128)(2,1)S(1)}, bf16[18,32,256]{2,1,0:T(8,128)(2,1)S(1)}, u32[]{:S(2)}, u32[]{:S(2)}) collective-permute-start(bf16[18,32,256]{2,1,0:T(8,128)(2,1)S(1)} %get-tuple-element.37), channel_id=1, source_target_pairs={{0,4},{1,5},{2,6},{3,7},{4,0},{5,1},{6,2},{7,3},{8,12},{9,13},{10,... | collective-permute-start | bytes 884744 | tf_op jit(solution)/shard_map/ppermute | solution.py:447
  3.1 13.5 %collective-permute-start.2 = (bf16[16,32,256]{2,1,0:T(8,128)(2,1)S(1)}, bf16[16,32,256]{2,1,0:T(8,128)(2,1)S(1)}, u32[]{:S(2)}, u32[]{:S(2)}) collective-permute-start(bf16[16,32,256]{2,1,0:T(8,128)(2,1)S(1)} %get-tuple-element.34.far_row), channel_id=1, source_target_pairs={{0,1},{1,0},{2,3},{3,2},{4,8},{5,9},{6,10},{7,11},{8,4},{9,5},{10,... | collective-permute-start | bytes 786440 | tf_op jit(solution)/shard_map/ppermute | solution.py:447
  4.3 8.5 %collective-permute-start.3 = (bf16[2,32,256]{2,1,0:T(8,128)(2,1)S(1)}, bf16[2,32,256]{2,1,0:T(8,128)(2,1)S(1)}, u32[]{:S(2)}, u32[]{:S(2)}) collective-permute-start(bf16[2,32,256]{2,1,0:T(8,128)(2,1)S(1)} %get-tuple-element.35.far_small), channel_id=1, source_target_pairs={{0,1},{1,0},{2,3},{3,2},{4,8},{5,9},{6,10},{7,11},{8,4},{9,5},{10,... | collective-permute-start | bytes 98312 | tf_op jit(solution)/shard_map/ppermute | solution.py:447
  5.7 0.7 %copy-start.3 = (f32[32]{0:T(128)S(1)}, f32[32]{0:T(128)}, u32[]{:S(2)}) copy-start(f32[32]{0:T(128)} %param.9) | copy-start | bytes 388
  5.7 0.7 %copy-start.4 = (f32[64]{0:T(128)S(1)}, f32[64]{0:T(128)}, u32[]{:S(2)}) copy-start(f32[64]{0:T(128)} %param.11) | copy-start | bytes 772
  5.7 0.7 %copy-start.5 = (f32[64]{0:T(128)S(1)}, f32[64]{0:T(128)}, u32[]{:S(2)}) copy-start(f32[64]{0:T(128)} %param.13) | copy-start | bytes 772
  12.8 3.8 %collective-permute-start.4 = (bf16[6,32,128]{2,1,0:T(8,128)(2,1)S(1)}, bf16[6,32,128]{2,1,0:T(8,128)(2,1)S(1)}, u32[]{:S(2)}, u32[]{:S(2)}) collective-permute-start(bf16[6,32,128]{2,1,0:T(8,128)(2,1)S(1)} %get-tuple-element.46), channel_id=1, source_target_pairs={{0,1},{1,2},{2,3},{3,7},{4,0},{5,4},{6,5},{7,6},{8,9},{9,10},{10,1... | collective-permute-start | bytes 147464 | tf_op jit(solution)/shard_map/ppermute | solution.py:447
  12.8 3.8 %collective-permute-start.5 = (bf16[6,32,128]{2,1,0:T(8,128)(2,1)S(1)}, bf16[6,32,128]{2,1,0:T(8,128)(2,1)S(1)}, u32[]{:S(2)}, u32[]{:S(2)}) collective-permute-start(bf16[6,32,128]{2,1,0:T(8,128)(2,1)S(1)} %get-tuple-element.47), channel_id=1, source_target_pairs={{0,4},{1,0},{2,1},{3,2},{4,5},{5,6},{6,7},{7,3},{8,12},{9,8},{10,9... | collective-permute-start | bytes 147464 | tf_op jit(solution)/shard_map/ppermute | solution.py:447
  17.7 4.4 %collective-permute-start.7 = (bf16[2,9,32,128]{3,2,1,0:T(8,128)(2,1)S(1)}, bf16[2,9,32,128]{3,2,1,0:T(8,128)(2,1)S(1)}, u32[]{:S(2)}, u32[]{:S(2)}) collective-permute-start(bf16[2,9,32,128]{3,2,1,0:T(8,128)(2,1)S(1)} %get-tuple-element.51.own), channel_id=1, source_target_pairs={{0,4},{1,5},{2,6},{3,7},{4,0},{5,1},{6,2},{7,3},{8,12},{9,13},{10,... | collective-permute-start | bytes 442376 | tf_op jit(solution)/shard_map/ppermute | solution.py:447
  18.1 5.4 %collective-permute-start.1 = (bf16[8,32,128]{2,1,0:T(8,128)(2,1)S(1)}, bf16[8,32,128]{2,1,0:T(8,128)(2,1)S(1)}, u32[]{:S(2)}, u32[]{:S(2)}) collective-permute-start(bf16[8,32,128]{2,1,0:T(8,128)(2,1)S(1)} %get-tuple-element.41.early), channel_id=1, source_target_pairs={{0,1},{1,0},{2,3},{3,2},{4,8},{5,9},{6,10},{7,11},{8,4},{9,5},{10,... | collective-permute-start | bytes 196616 | tf_op jit(solution)/shard_map/ppermute | solution.py:447
  21.1 4.8 %collective-permute-start.6 = (bf16[10,32,128]{2,1,0:T(8,128)(2,1)S(1)}, bf16[10,32,128]{2,1,0:T(8,128)(2,1)S(1)}, u32[]{:S(2)}, u32[]{:S(2)}) collective-permute-start(bf16[10,32,128]{2,1,0:T(8,128)(2,1)S(1)} %get-tuple-element.50), channel_id=1, source_target_pairs={{0,1},{1,0},{2,3},{3,2},{4,8},{5,9},{6,10},{7,11},{8,4},{9,5},{10,... | collective-permute-start | bytes 245768 | tf_op jit(solution)/shard_map/ppermute | solution.py:447

commit v6 on v5

--- a/solution.py
+++ b/solution.py
@@ -137,28 +137,42 @@
         copy.wait()
 
 
-def pack_kernel(local, far_row, far_small, own, near_row, msgs, olds, lo, hi):
+def near_kernel(local, near_row, lo, hi):
+    inline, _, depth, _ = local.shape
+    near = (inline - 1) * (1 - lax.axis_index("gx") % 2)
+
+    def store(z, a, b):
+        near_row[z, :, :128] = a
+        near_row[z, :, 128:] = b
+
+    msg_l, msg_r, own_l, own_r = relayout(local[near], lo, hi, store)
+    near_row[depth, :, :128] = msg_l
+    near_row[depth, :, 128:] = msg_r
+    near_row[depth + 1, :, :128] = own_l
+    near_row[depth + 1, :, 128:] = own_r
+
+
+def pack_kernel(local, near_row, far_row, far_small, own, msgs, olds, lo, hi):
     inline, _, depth, _ = local.shape
     odd = lax.axis_index("gx") % 2
     near, far = (inline - 1) * (1 - odd), (inline - 1) * odd
     own[:, far] = far_row[...]
     msgs[far] = far_small[0]
     olds[far] = far_small[1]
-    for k in range(1, inline):
-        x = (far + k) % inline
+    own[:, near] = near_row[pl.ds(0, depth)]
+    msgs[near] = near_row[depth]
+    olds[near] = near_row[depth + 1]
+    for x in range(1, inline - 1):
 
         def store(z, a, b):
             own[z, x, :, :128] = a
             own[z, x, :, 128:] = b
 
-        msg_l, msg_r, own_l, own_r = relayout(local[x], lo.at[k - 1], hi.at[k - 1], store)
+        msg_l, msg_r, own_l, own_r = relayout(local[x], lo.at[x - 1], hi.at[x - 1], store)
         msgs[x, :, :128] = msg_l
         msgs[x, :, 128:] = msg_r
         olds[x, :, :128] = own_l
         olds[x, :, 128:] = own_r
-    near_row[pl.ds(0, depth)] = own[:, near]
-    near_row[depth] = msgs[near]
-    near_row[depth + 1] = olds[near]
 
 
 def at_map_end():
@@ -484,17 +498,15 @@
     )(image)
     got_small = permute(far_small, far_of)
     got_far = permute(far_row, far_of)
-    own, near_row, msgs, olds = call(
+    (near_row,) = call(
+        near_kernel, [((depth + 2, c1, cross), BF)], scratch=[pltpu.VMEM((c1 * depth, 128), F32)] * 2, flops=1 << 27
+    )(local)
+    own, msgs, olds = call(
         pack_kernel,
-        [
-            ((depth, inline, c1, cross), BF),
-            ((depth + 2, c1, cross), BF),
-            ((inline, c1, 256), BF),
-            ((inline, c1, 256), BF),
-        ],
-        scratch=[pltpu.VMEM((inline - 1, c1 * depth, 128), F32)] * 2,
+        [((depth, inline, c1, cross), BF), ((inline, c1, 256), BF), ((inline, c1, 256), BF)],
+        scratch=[pltpu.VMEM((inline - 2, c1 * depth, 128), F32)] * 2,
         flops=1 << 28,
-    )(local, far_row, far_small)
+    )(local, near_row, far_row, far_small)
     got_row = permute(near_row, mate_of)
     a1, a1s, a1h, a2, a3, b1, b2, b3, evens, ends = call(
         weights_kernel,

time: 28.1 us -> 27.4 us (0.975)
  waiting for transfers between devices: 8.04 us -> 7.42 us
    ppermute x8, waiting for transfers between devices: 8.04 us -> 7.42 us  [permute(): return lax.ppermute(value, ('gx', 'gy'), pairs)]
    pallas_call x9 -> x10, Pallas kernels: 10.7 us -> 10.7 us  [run(): pl.pallas_call(body, out_shape=[jax.ShapeDtypeStruct(s, d) for s, d in ou...]
  transfers between devices with their start and end apart: 8 -> 8, of which waited for: 3 -> 3; matrix products, arithmetic and copies ran while one was open for 0% -> 0% of each run, Pallas kernels for 19% -> 21%
where the time goes in v6:
time: 27.4 us; the launch traced here: 27.3 us
  Pallas kernels  10.7 us (39%)
  starting transfers between devices  8.33 us (30%)
  waiting for transfers between devices  7.42 us (27%)
  local copies, waits for them, and re-layouts  0.65 us (2%)
    pallas_call x10, Pallas kernels, run(): pl.pallas_call(body, out_shape=[jax.ShapeDtypeStruct(s, d) for s, d in ou...  10.7 us
    ppermute x8, starting transfers between devices, permute(): return lax.ppermute(value, ('gx', 'gy'), pairs)  8.33 us
    ppermute x8, waiting for transfers between devices, permute(): return lax.ppermute(value, ('gx', 'gy'), pairs)  7.42 us
    unnamed x12, local copies, waits for them, and re-layouts  0.65 us
  transfers between devices with their start and end apart: 8, of which 3 were waited for; matrix products, arithmetic and copies ran while one was open for 0% of the time, Pallas kernels for 21%

profile of v6, /device:TPU:3, one launch (start us, length us, event | category | flops | bytes accessed | tf_op | source)
XLA Modules:
  0.0 27.3 jit_solution(8124958636175702638)
XLA Ops:
  0.0 1.3 %shard_map.73 = (bf16[4,32,16,256]{3,2,1,0:T(8,128)(2,1)S(1)}, bf16[16,32,256]{2,1,0:T(8,128)(2,1)S(1)}, bf16[2,32,256]{2,1,0:T(8,128)(2,1)S(1)}) custom-call(bf16[32,4,16,256]{3,2,1,0:T(8,128)(2,1)} %image.1), custom_call_target="tpu_custom_call" | custom-call | flops 1048576 | bytes 1048576 | tf_op jit(solution)/shard_map/pallas_call | solution.py:17
  1.3 0.4 %shard_map.74.near_row = bf16[18,32,256]{2,1,0:T(8,128)(2,1)S(1)} custom-call(bf16[4,32,16,256]{3,2,1,0:T(8,128)(2,1)S(1)} %get-tuple-element.32.local), custom_call_target="tpu_custom_call" | custom-call | flops 134217728 | bytes 1048576 | tf_op jit(solution)/shard_map/pallas_call | solution.py:17
  1.7 0.7 %collective-permute-start = (bf16[18,32,256]{2,1,0:T(8,128)(2,1)S(1)}, bf16[18,32,256]{2,1,0:T(8,128)(2,1)S(1)}, u32[]{:S(2)}, u32[]{:S(2)}) collective-permute-start(bf16[18,32,256]{2,1,0:T(8,128)(2,1)S(1)} %shard_map.74.near_row), channel_id=1, source_target_pairs={{0,4},{1,5},{2,6},{3,7},{4,0},{5,1},{6,2},{7,3},{8,12},{9,13},{10,... | collective-permute-start | bytes 884744 | tf_op jit(solution)/shard_map/ppermute | solution.py:461
  2.4 1.2 %collective-permute-start.2 = (bf16[16,32,256]{2,1,0:T(8,128)(2,1)S(1)}, bf16[16,32,256]{2,1,0:T(8,128)(2,1)S(1)}, u32[]{:S(2)}, u32[]{:S(2)}) collective-permute-start(bf16[16,32,256]{2,1,0:T(8,128)(2,1)S(1)} %get-tuple-element.33.far_row), channel_id=1, source_target_pairs={{0,1},{1,0},{2,3},{3,2},{4,8},{5,9},{6,10},{7,11},{8,4},{9,5},{10,... | collective-permute-start | bytes 786440 | tf_op jit(solution)/shard_map/ppermute | solution.py:461
  3.6 1.5 %collective-permute-start.3 = (bf16[2,32,256]{2,1,0:T(8,128)(2,1)S(1)}, bf16[2,32,256]{2,1,0:T(8,128)(2,1)S(1)}, u32[]{:S(2)}, u32[]{:S(2)}) collective-permute-start(bf16[2,32,256]{2,1,0:T(8,128)(2,1)S(1)} %get-tuple-element.34.far_small), channel_id=1, source_target_pairs={{0,1},{1,0},{2,3},{3,2},{4,8},{5,9},{6,10},{7,11},{8,4},{9,5},{10,... | collective-permute-start | bytes 98312 | tf_op jit(solution)/shard_map/ppermute | solution.py:461
  5.1 0.6 %shard_map.75 = (bf16[16,4,32,256]{3,2,1,0:T(8,128)(2,1)S(1)}, bf16[4,32,256]{2,1,0:T(8,128)(2,1)S(1)}, bf16[4,32,256]{2,1,0:T(8,128)(2,1)S(1)}) custom-call(bf16[4,32,16,256]{3,2,1,0:T(8,128)(2,1)S(1)} %get-tuple-element.32.local, bf16[18,32,256]{2,1,0:T(8,128)(2,1)S(1)} %shard_map.74.near_row, bf16[16,32,256]{2,1,0:T(8,128)(2,1)S(1)} %get-tuple-element.33.far_row, ...), custom_call_target="tpu_custom_call" | custom-call | flops 268435456 | bytes 1048576 | tf_op jit(solution)/shard_map/pallas_call | solution.py:17
  5.8 0.6 %copy-done.3 = f32[32]{0:T(128)S(1)} copy-done((f32[32]{0:T(128)S(1)}, f32[32]{0:T(128)}, u32[]{:S(2)}) %copy-start.3) | copy-done | bytes 152
  6.4 0.0 copy-done.4
  6.4 0.0 copy-done.5
  6.4 0.7 %shard_map.76 = (bf16[192,384]{1,0:T(8,128)(2,1)S(1)}, bf16[576,128]{1,0:T(8,128)(2,1)S(1)}, bf16[2,96,96]{2,1,0:T(8,128)(2,1)S(1)}, bf16[2,128,576]{2,1,0:T(8,1...) custom-call(bf16[3,3,3,32,32]{4,3,2,1,0:T(8,128)(2,1)S(1)} %bitcast., ...), custom_call_target="tpu_custom_call" | custom-call | flops 268435456 | bytes 1048576 | tf_op jit(solution)/shard_map/pallas_call | solution.py:17
  7.1 5.0 %collective-permute-done.3.far_row = bf16[2,32,256]{2,1,0:T(8,128)(2,1)S(1)} collective-permute-done((bf16[2,32,256]{2,1,0:T(8,128)(2,1)S(1)}, bf16[2,32,256]{2,1,0:T(8,128)(2,1)S(1)}, u32[]{:S(2)}, u32[]{:S(2)}) %collective-permute-start.3) | collective-permute-done | bytes 32800 | tf_op jit(solution)/shard_map/ppermute | solution.py:461
  12.1 0.0 collective-permute-start.4
  12.2 1.5 %collective-permute-start.5 = (bf16[6,32,128]{2,1,0:T(8,128)(2,1)S(1)}, bf16[6,32,128]{2,1,0:T(8,128)(2,1)S(1)}, u32[]{:S(2)}, u32[]{:S(2)}) collective-permute-start(bf16[6,32,128]{2,1,0:T(8,128)(2,1)S(1)} %get-tuple-element.45), channel_id=1, source_target_pairs={{0,4},{1,0},{2,1},{3,2},{4,5},{5,6},{6,7},{7,3},{8,12},{9,8},{10,9... | collective-permute-start | bytes 147464 | tf_op jit(solution)/shard_map/ppermute | solution.py:461
  13.6 2.3 %shard_map.77 = (bf16[8,32,128]{2,1,0:T(8,128)(2,1)S(1)}, f32[16,2,32,256]{3,2,1,0:T(8,128)S(1)}) custom-call(bf16[16,4,32,256]{3,2,1,0:T(8,128)(2,1)S(1)} %get-tuple-element.35.own, bf16[18,32,256]{2,1,0:T(8,128)(2,1)S(1)} %collective-permute-done.mate, bf16[192,384]{1,0:T(8,128)(2,1)S(1)} %get-tuple-element.36.a1, f32[32,256]{1,0:T(8,128)S(1)} %get-tuple-element.37.bias, ...), custom_call_target="tpu_custom_call" | custom-call | flops 1073741824 | bytes 1048576 | tf_op jit(solution)/shard_map/pallas_call | solution.py:17
  15.9 0.0 collective-permute-done.2.halo
  15.9 1.1 %shard_map.79 = (bf16[2,9,32,128]{3,2,1,0:T(8,128)(2,1)S(1)}, bf16[10,32,128]{2,1,0:T(8,128)(2,1)S(1)}) custom-call(f32[16,2,32,256]{3,2,1,0:T(8,128)S(1)} %get-tuple-element.40.sums, bf16[16,32,256]{2,1,0:T(8,128)(2,1)S(1)} %collective-permute-done.2.halo, bf16[8,32,128]{2,1,0:T(8,128)(2,1)S(1)} %get-tuple-element.39.early, ...), custom_call_target="tpu_custom_call" | custom-call | flops 268435456 | bytes 1048576 | tf_op jit(solution)/shard_map/pallas_call | solution.py:17
  17.0 0.4 %collective-permute-start.7 = (bf16[2,9,32,128]{3,2,1,0:T(8,128)(2,1)S(1)}, bf16[2,9,32,128]{3,2,1,0:T(8,128)(2,1)S(1)}, u32[]{:S(2)}, u32[]{:S(2)}) collective-permute-start(bf16[2,9,32,128]{3,2,1,0:T(8,128)(2,1)S(1)} %get-tuple-element.49.own), channel_id=1, source_target_pairs={{0,4},{1,5},{2,6},{3,7},{4,0},{5,1},{6,2},{7,3},{8,12},{9,13},{10,... | collective-permute-start | bytes 442376 | tf_op jit(solution)/shard_map/ppermute | solution.py:461
  17.4 3.0 %collective-permute-start.1 = (bf16[8,32,128]{2,1,0:T(8,128)(2,1)S(1)}, bf16[8,32,128]{2,1,0:T(8,128)(2,1)S(1)}, u32[]{:S(2)}, u32[]{:S(2)}) collective-permute-start(bf16[8,32,128]{2,1,0:T(8,128)(2,1)S(1)} %get-tuple-element.39.early), channel_id=1, source_target_pairs={{0,1},{1,0},{2,3},{3,2},{4,8},{5,9},{6,10},{7,11},{8,4},{9,5},{10,... | collective-permute-start | bytes 196616 | tf_op jit(solution)/shard_map/ppermute | solution.py:461
  20.4 0.1 collective-permute-start.6
  20.5 1.0 %shard_map.80 = (f32[4,128,256]{2,1,0:T(8,128)S(1)}, f32[128,128]{1,0:T(8,128)S(1)}, f32[4,128,256]{2,1,0:T(8,128)S(1)}, f32[128,128]{1,0:T(8,128)S(1)}) custom-call(bf16[2,9,32,128]{3,2,1,0:T(8,128)(2,1)S(1)} %get-tuple-element.49.own, bf16[2,128,576]{2,1,0:T(8,128)(2,1)S(1)} %get-tuple-element.50.a2, bf16[256,256]{1,0:T(8,128)(2,1)S(1)} %get-tuple-element.51.ends), custom_call_target="tpu_custom_call" | custom-call | flops 536870912 | bytes 1048576 | tf_op jit(solution)/shard_map/pallas_call | solution.py:17
  21.5 1.3 %shard_map.81.part3 = f32[4,128,256]{2,1,0:T(8,128)S(1)} custom-call(bf16[2,9,32,128]{3,2,1,0:T(8,128)(2,1)S(1)} %collective-permute-done.7.mate, f32[4,128,256]{2,1,0:T(8,128)S(1)} %get-tuple-element.54.near, f32[128,128]{1,0:T(8,128)S(1)} %get-tuple-element.55.near_ends, bf16[2,128,576]{2,1,0:T(8,128)(2,1)S(1)} %get-tuple-element.50.a2, ...), custom_call_target="tpu_custom_call" | custom-call | flops 536870912 | bytes 1048576 | tf_op jit(solution)/shard_map/pallas_call | solution.py:17
  22.8 0.1 collective-permute-done.1.first
  22.9 2.3 %collective-permute-done.6.far = bf16[10,32,128]{2,1,0:T(8,128)(2,1)S(1)} collective-permute-done((bf16[10,32,128]{2,1,0:T(8,128)(2,1)S(1)}, bf16[10,32,128]{2,1,0:T(8,128)(2,1)S(1)}, u32[]{:S(2)}, u32[]{:S(2)}) %collective-permute-start.6) | collective-permute-done | bytes 81952 | tf_op jit(solution)/shard_map/ppermute | solution.py:461
  25.2 2.1 %shard_map.82 = bf16[64,2,8,128]{3,2,1,0:T(8,128)(2,1)} custom-call(bf16[8,32,128]{2,1,0:T(8,128)(2,1)S(1)} %collective-permute-done.1.first, bf16[10,32,128]{2,1,0:T(8,128)(2,1)S(1)} %collective-permute-done.6.far, f32[4,128,256]{2,1,0:T(8,128)S(1)} %get-tuple-element.52.part2, f32[128,128]{1,0:T(8,128)S(1)} %get-tuple-element.53.part2_ends, ...), custom_call_target="tpu_custom_call" | custom-call | flops 536870912 | bytes 1048576 | tf_op jit(solution)/shard_map/pallas_call | solution.py:17
  (14 shorter events, 0.1 us)
Async XLA Ops:
  1.7 10.4 %collective-permute-start = (bf16[18,32,256]{2,1,0:T(8,128)(2,1)S(1)}, bf16[18,32,256]{2,1,0:T(8,128)(2,1)S(1)}, u32[]{:S(2)}, u32[]{:S(2)}) collective-permute-start(bf16[18,32,256]{2,1,0:T(8,128)(2,1)S(1)} %shard_map.74.near_row), channel_id=1, source_target_pairs={{0,4},{1,5},{2,6},{3,7},{4,0},{5,1},{6,2},{7,3},{8,12},{9,13},{10,... | collective-permute-start | bytes 884744 | tf_op jit(solution)/shard_map/ppermute | solution.py:461
  2.4 13.5 %collective-permute-start.2 = (bf16[16,32,256]{2,1,0:T(8,128)(2,1)S(1)}, bf16[16,32,256]{2,1,0:T(8,128)(2,1)S(1)}, u32[]{:S(2)}, u32[]{:S(2)}) collective-permute-start(bf16[16,32,256]{2,1,0:T(8,128)(2,1)S(1)} %get-tuple-element.33.far_row), channel_id=1, source_target_pairs={{0,1},{1,0},{2,3},{3,2},{4,8},{5,9},{6,10},{7,11},{8,4},{9,5},{10,... | collective-permute-start | bytes 786440 | tf_op jit(solution)/shard_map/ppermute | solution.py:461
  3.6 2.1 %copy-start = (bf16[64,64,3,3,3]{1,0,4,3,2:T(8,128)(2,1)S(1)}, bf16[64,64,3,3,3]{1,0,4,3,2:T(8,128)(2,1)}, u32[]{:S(2)}) copy-start(bf16[64,64,3,3,3]{1,0,4,3,2:T(8,128)(2,1)} %param.12) | copy-start | bytes 663556
  3.6 2.1 %copy-start.1 = (bf16[32,32,3,3,3]{1,0,4,3,2:T(8,128)(2,1)S(1)}, bf16[32,32,3,3,3]{1,0,4,3,2:T(8,128)(2,1)}, u32[]{:S(2)}) copy-start(bf16[32,32,3,3,3]{1,0,4,3,2:T(8,128)(2,1)} %param.8) | copy-start | bytes 165892
  3.6 2.1 %copy-start.2 = (bf16[64,32,3,3,3]{0,1,4,3,2:T(8,128)(2,1)S(1)}, bf16[64,32,3,3,3]{0,1,4,3,2:T(8,128)(2,1)}, u32[]{:S(2)}) copy-start(bf16[64,32,3,3,3]{0,1,4,3,2:T(8,128)(2,1)} %param.10) | copy-start | bytes 331780
  3.6 8.5 %collective-permute-start.3 = (bf16[2,32,256]{2,1,0:T(8,128)(2,1)S(1)}, bf16[2,32,256]{2,1,0:T(8,128)(2,1)S(1)}, u32[]{:S(2)}, u32[]{:S(2)}) collective-permute-start(bf16[2,32,256]{2,1,0:T(8,128)(2,1)S(1)} %get-tuple-element.34.far_small), channel_id=1, source_target_pairs={{0,1},{1,0},{2,3},{3,2},{4,8},{5,9},{6,10},{7,11},{8,4},{9,5},{10,... | collective-permute-start | bytes 98312 | tf_op jit(solution)/shard_map/ppermute | solution.py:461
  5.7 0.7 %copy-start.3 = (f32[32]{0:T(128)S(1)}, f32[32]{0:T(128)}, u32[]{:S(2)}) copy-start(f32[32]{0:T(128)} %param.9) | copy-start | bytes 388
  5.7 0.7 %copy-start.4 = (f32[64]{0:T(128)S(1)}, f32[64]{0:T(128)}, u32[]{:S(2)}) copy-start(f32[64]{0:T(128)} %param.11) | copy-start | bytes 772
  5.7 0.7 %copy-start.5 = (f32[64]{0:T(128)S(1)}, f32[64]{0:T(128)}, u32[]{:S(2)}) copy-start(f32[64]{0:T(128)} %param.13) | copy-start | bytes 772
  12.1 3.8 %collective-permute-start.4 = (bf16[6,32,128]{2,1,0:T(8,128)(2,1)S(1)}, bf16[6,32,128]{2,1,0:T(8,128)(2,1)S(1)}, u32[]{:S(2)}, u32[]{:S(2)}) collective-permute-start(bf16[6,32,128]{2,1,0:T(8,128)(2,1)S(1)} %get-tuple-element.44), channel_id=1, source_target_pairs={{0,1},{1,2},{2,3},{3,7},{4,0},{5,4},{6,5},{7,6},{8,9},{9,10},{10,1... | collective-permute-start | bytes 147464 | tf_op jit(solution)/shard_map/ppermute | solution.py:461
  12.2 3.8 %collective-permute-start.5 = (bf16[6,32,128]{2,1,0:T(8,128)(2,1)S(1)}, bf16[6,32,128]{2,1,0:T(8,128)(2,1)S(1)}, u32[]{:S(2)}, u32[]{:S(2)}) collective-permute-start(bf16[6,32,128]{2,1,0:T(8,128)(2,1)S(1)} %get-tuple-element.45), channel_id=1, source_target_pairs={{0,4},{1,0},{2,1},{3,2},{4,5},{5,6},{6,7},{7,3},{8,12},{9,8},{10,9... | collective-permute-start | bytes 147464 | tf_op jit(solution)/shard_map/ppermute | solution.py:461
  17.0 4.4 %collective-permute-start.7 = (bf16[2,9,32,128]{3,2,1,0:T(8,128)(2,1)S(1)}, bf16[2,9,32,128]{3,2,1,0:T(8,128)(2,1)S(1)}, u32[]{:S(2)}, u32[]{:S(2)}) collective-permute-start(bf16[2,9,32,128]{3,2,1,0:T(8,128)(2,1)S(1)} %get-tuple-element.49.own), channel_id=1, source_target_pairs={{0,4},{1,5},{2,6},{3,7},{4,0},{5,1},{6,2},{7,3},{8,12},{9,13},{10,... | collective-permute-start | bytes 442376 | tf_op jit(solution)/shard_map/ppermute | solution.py:461
  17.4 5.4 %collective-permute-start.1 = (bf16[8,32,128]{2,1,0:T(8,128)(2,1)S(1)}, bf16[8,32,128]{2,1,0:T(8,128)(2,1)S(1)}, u32[]{:S(2)}, u32[]{:S(2)}) collective-permute-start(bf16[8,32,128]{2,1,0:T(8,128)(2,1)S(1)} %get-tuple-element.39.early), channel_id=1, source_target_pairs={{0,1},{1,0},{2,3},{3,2},{4,8},{5,9},{6,10},{7,11},{8,4},{9,5},{10,... | collective-permute-start | bytes 196616 | tf_op jit(solution)/shard_map/ppermute | solution.py:461
  20.4 4.8 %collective-permute-start.6 = (bf16[10,32,128]{2,1,0:T(8,128)(2,1)S(1)}, bf16[10,32,128]{2,1,0:T(8,128)(2,1)S(1)}, u32[]{:S(2)}, u32[]{:S(2)}) collective-permute-start(bf16[10,32,128]{2,1,0:T(8,128)(2,1)S(1)} %get-tuple-element.48), channel_id=1, source_target_pairs={{0,1},{1,0},{2,3},{3,2},{4,8},{5,9},{6,10},{7,11},{8,4},{9,5},{10,... | collective-permute-start | bytes 245768 | tf_op jit(solution)/shard_map/ppermute | solution.py:461
